TPU v7x, 8 devices: a whole 2x2x1 slice. The times are simulated.
8 devices in a mesh: dp: 1 (over z), dim: 2 (over y), heads: 4 (over x, core).
Axes of the slice: x: 2, y: 2, z: 1, core: 2. Of those that a mesh axis runs over, the one named last changes fastest.
Arguments:
- tokens: bfloat16 [128, 5120], P('dp')
- ln_attn: float32 [5120], replicated
- w_query: bfloat16 [5120, 64, 128], P(None, 'heads', 'dim')
- w_key: bfloat16 [5120, 8, 128], P(None, 'heads', 'dim')
- w_value: bfloat16 [5120, 8, 128], P(None, 'heads', 'dim')
- q_gain: float32 [128], P('dim')
- k_gain: float32 [128], P('dim')
- w_out: bfloat16 [64, 128, 5120], P('heads', 'dim')
- ln_mlp: float32 [5120], replicated
- w_gate: bfloat16 [5120, 25600], P(None, ('heads', 'dim'))
- w_up: bfloat16 [5120, 25600], P(None, ('heads', 'dim'))
- w_down: bfloat16 [25600, 5120], P(('heads', 'dim'))
- k_cache: bfloat16 [128, 1024, 8, 128], P('dp', None, 'heads', 'dim')
- v_cache: bfloat16 [128, 1024, 8, 128], P('dp', None, 'heads', 'dim')
- positions: int32 [128], P('dp')
Outputs:
- output 1: bfloat16 [128, 5120], P('dp')
- output 2: bfloat16 [128, 8, 128], P('dp', 'heads', 'dim')
- output 3: bfloat16 [128, 8, 128], P('dp', 'heads', 'dim')
All inputs are finite; a program needn't handle non-finite values.
Results may differ from a plain program's by a relative error of at most 0.00674652.
Values sent between devices are 32-bit elements.
A program may use at most 1 GiB of HBM per device.

v0:
```python
import jax
import jax.numpy as jnp
from jax import lax
from jax.sharding import PartitionSpec as P

EPS = 1e-6
ROPE_BASE = 1000000.0


def rms_scale(values, gain):
    mean_sq = jnp.mean(values * values, axis=-1, keepdims=True)
    return values * lax.rsqrt(mean_sq + EPS) * gain


def solution(mesh):
    dim_count = mesh.shape['dim']
    mlp_axes = ('heads', 'dim')
    swap_perm = [(src, (src + dim_count // 2) % dim_count) for src in range(dim_count)]

    def layer_body(tokens, ln_attn, w_query, w_key, w_value, q_gain, k_gain, w_out, ln_mlp, w_gate, w_up, w_down, k_cache, v_cache, positions):
        batch_rows = tokens.shape[0]
        heads_local = w_query.shape[1]
        kv_local = w_key.shape[1]
        slice_len = w_query.shape[2]
        head_dim = slice_len * dim_count
        half_dim = head_dim // 2
        q_group = heads_local // kv_local
        cache_len = k_cache.shape[1]
        dim_index = lax.axis_index('dim')

        tok_f32 = tokens.astype(jnp.float32)
        hidden = rms_scale(tok_f32, ln_attn).astype(jnp.bfloat16)
        q_part = jnp.einsum('bd,dhs->bhs', hidden, w_query, preferred_element_type=jnp.float32)
        k_part = jnp.einsum('bd,dhs->bhs', hidden, w_key, preferred_element_type=jnp.float32)
        v_new = jnp.einsum('bd,dhs->bhs', hidden, w_value, preferred_element_type=jnp.float32).astype(jnp.bfloat16)

        qk_part = jnp.concatenate([q_part, k_part], axis=1)
        sq_total = lax.psum(jnp.sum(qk_part * qk_part, axis=-1, keepdims=True), 'dim')
        qk_gains = jnp.concatenate([jnp.broadcast_to(q_gain, (heads_local, slice_len)), jnp.broadcast_to(k_gain, (kv_local, slice_len))], axis=0)
        qk_norm = qk_part * lax.rsqrt(sq_total / head_dim + EPS) * qk_gains

        dim_pos = dim_index * slice_len + jnp.arange(slice_len)
        inv_freq = ROPE_BASE ** (-(dim_pos % half_dim).astype(jnp.float32) * 2.0 / head_dim)
        rot_angle = positions.astype(jnp.float32)[:, None, None] * inv_freq
        cos_t = jnp.cos(rot_angle)
        sin_t = jnp.where(dim_pos < half_dim, -1.0, 1.0) * jnp.sin(rot_angle)
        if dim_count == 1:
            partner = jnp.concatenate([qk_norm[..., half_dim:], qk_norm[..., :half_dim]], axis=-1)
        else:
            partner = lax.ppermute(qk_norm, 'dim', swap_perm)
        qk_rot = (qk_norm * cos_t + partner * sin_t).astype(jnp.bfloat16)
        q_rot = qk_rot[:, :heads_local].reshape(batch_rows, kv_local, q_group, slice_len)
        k_new = qk_rot[:, heads_local:]

        cache_part = jnp.einsum('bkgs,btks->bkgt', q_rot, k_cache, preferred_element_type=jnp.float32)
        new_part = jnp.einsum('bkgs,bks->bkg', q_rot, k_new, preferred_element_type=jnp.float32)
        scores = lax.psum(jnp.concatenate([cache_part, new_part[..., None]], axis=-1), 'dim') * head_dim ** -0.5
        slot_ids = jnp.arange(cache_len + 1)
        valid_mask = (slot_ids < positions[:, None]) | (slot_ids == cache_len)
        scores = jnp.where(valid_mask[:, None, None, :], scores, -jnp.inf)
        exp_scores = jnp.exp(scores - jnp.max(scores, axis=-1, keepdims=True))
        attn_prob = (exp_scores / jnp.sum(exp_scores, axis=-1, keepdims=True)).astype(jnp.bfloat16)
        attn_sum = jnp.einsum('bkgt,btks->bkgs', attn_prob[..., :cache_len], v_cache, preferred_element_type=jnp.float32)
        attn_sum = attn_sum + attn_prob[..., cache_len:].astype(jnp.float32) * v_new[:, :, None, :].astype(jnp.float32)
        attn_vals = attn_sum.astype(jnp.bfloat16).reshape(batch_rows, heads_local, slice_len)

        attn_out = lax.psum(jnp.einsum('bhs,hsd->bd', attn_vals, w_out, preferred_element_type=jnp.float32), mlp_axes)
        resid_f32 = (tok_f32 + attn_out).astype(jnp.bfloat16).astype(jnp.float32)
        hidden2 = rms_scale(resid_f32, ln_mlp).astype(jnp.bfloat16)
        gate_val = jnp.dot(hidden2, w_gate, preferred_element_type=jnp.float32)
        up_val = jnp.dot(hidden2, w_up, preferred_element_type=jnp.float32)
        mlp_act = (jax.nn.silu(gate_val) * up_val).astype(jnp.bfloat16)
        mlp_out = lax.psum(jnp.dot(mlp_act, w_down, preferred_element_type=jnp.float32), mlp_axes)
        return (resid_f32 + mlp_out).astype(jnp.bfloat16), k_new, v_new

    row_spec = P('dp', None)
    head_spec = P(None, 'heads', 'dim')
    cache_spec = P('dp', None, 'heads', 'dim')
    new_spec = P('dp', 'heads', 'dim')
    in_specs = (row_spec, P(None), head_spec, head_spec, head_spec, P('dim'), P('dim'), P('heads', 'dim', None), P(None), P(None, mlp_axes), P(None, mlp_axes), P(mlp_axes, None), cache_spec, cache_spec, P('dp'))
    out_specs = (row_spec, new_spec, new_spec)
    return jax.shard_map(layer_body, mesh=mesh, in_specs=in_specs, out_specs=out_specs, check_vma=False)
```

profile of v0, /device:TPU:0, one launch (start us, length us, event | category | flops | bytes accessed | tf_op | source)
XLA Modules:
  0.0 467.9 jit_solution(8382283590595571625)
XLA Ops:
  7.2 0.0 copy-start
  7.2 0.0 all-reduce.4.cloned.1.call-start
  7.2 1.7 fusion.4
  9.0 0.0 copy-start.3
  9.0 0.0 copy-start.9
  9.0 6.2 %fusion.38 = f32[128,1024]{0,1:S(1)} fusion(bf16[5120,1024]{0,1:T(8,128)(2,1)} %bitcast.43, bf16[128,5120]{1,0:T(8,128)(2,1)} %param.15, f32[5120]{0:T(1024)} %param.16, f32[128]{0:T(128)S(1)} %add_rsqrt_fusion.1), kind=kOutput, calls=%fused_computation.65 | convolution fusion | flops 1344798720 | bytes 12341760
  15.2 0.0 copy-start.8
  15.3 0.0 copy-start.7
  15.3 0.6 fusion.36
  15.9 0.1 multiply_reduce_fusion
  16.0 10.0 %psum.28 = f32[128,18,1]{0,1,2:T(8,128)S(1)} all-reduce(f32[128,18,1]{0,1,2:T(8,128)S(1)} %bitcast.41), channel_id=1, replica_groups=mesh['dp'=1,'dim'=2,'heads'=4] {'dim'}, use_global_device_ids=true, to_apply=%region_2.0 | all-reduce | flops 2304 | bytes 18432 | tf_op jit(solution)/shard_map/psum | solution.py:38
  26.0 0.2 multiply_multiply_fusion
  26.3 0.1 collective-permute-start
  26.4 0.2 multiply_cosine_fusion
  26.6 12.7 %collective-permute-done = f32[128,18,64]{0,2,1:T(8,128)S(1)} collective-permute-done((f32[128,18,64]{0,2,1:T(8,128)S(1)}, f32[128,18,64]{0,2,1:T(8,128)S(1)}, u32[]{:S(2)}, u32[]{:S(2)}) %collective-permute-start) | collective-permute-done | bytes 589856 | tf_op jit(solution)/shard_map/ppermute | solution.py:50
  39.3 0.1 add_convert_fusion
  39.4 0.6 fusion.41
  40.0 0.4 copy.27
  40.5 16.3 %fusion.42 = f32[128,2,8,1024]{3,2,1,0:T(8,128)} fusion(bf16[128,2,8,64]{3,2,1,0:T(8,128)(2,1)S(1)} %copy.27, bf16[128,1024,2,64]{1,3,2,0:T(8,128)(2,1)} %param.27), kind=kOutput, calls=%fused_computation.67 | convolution fusion | flops 268435456 | bytes 42205184 | tf_op jit(solution)/shard_map/bkgs,btks->bkgt/dot_general | solution.py:55
  56.8 8.8 %copy.28 = f32[128,2,8,1024]{0,2,3,1:T(8,128)} copy(f32[128,2,8,1024]{3,2,1,0:T(8,128)} %fusion.42) | data formatting | bytes 16777216 | tf_op jit(solution)/shard_map/bkgs,btks->bkgt/dot_general | solution.py:55
  65.5 0.1 multiply_reduce_fusion.1
  65.6 6.0 %pad_maximum_fusion = f32[128,2,8,1025]{0,2,3,1:T(8,128)} fusion(f32[128,2,8,1]{0,2,3,1:T(8,128)S(1)} %bitcast.42, f32[128,2,8,1024]{0,2,3,1:T(8,128)} %copy.28), kind=kLoop, calls=%fused_computation | loop fusion | flops 2099200 | bytes 16793600 | tf_op jit(solution)/shard_map/concatenate | solution.py:57
  71.6 0.0 all-reduce.4.cloned.1.call-update
  71.6 0.2 all-reduce.6.cloned.1.call-start
  71.9 1.9 fusion.34
  73.8 0.0 copy-start.5
  73.8 0.1 copy.31
  74.0 0.2 fusion.20
  74.2 190.1 %all-reduce.4.cloned.1.call-done = f32[128,2,8,1025]{0,2,3,1:T(8,128)} async-done(((f32[128,2,8,1025]{0,2,3,1:T(8,128)}), f32[128,2,8,1025]{0,2,3,1:T(8,128)}) %all-reduce.4.cloned.1.call-update) | async-done | bytes 8396816 | tf_op jit(solution)/shard_map/psum | solution.py:57
  264.3 5.8 %fusion = f32[128,2,8]{0,2,1:T(8,128)S(1)} fusion(f32[128,2,8,1025]{0,2,3,1:T(8,128)} %all-reduce.4.cloned.1.call-done, pred[128,1025]{0,1:T(8,128)(4,1)S(1)} %fusion.20), kind=kLoop, calls=%fused_computation.4 | loop fusion | flops 6295552 | bytes 8536192 | tf_op jit(solution)/shard_map/reduce_max | solution.py:61
  270.2 3.8 fusion.1
  273.9 3.1 divide_convert_fusion
  277.1 2.2 slice.18
  279.3 7.4 %copy.29 = bf16[128,2,8,1024]{3,2,1,0:T(8,128)(2,1)} copy(bf16[128,2,8,1024]{0,2,3,1:T(8,128)(2,1)} %slice.18) | data formatting | bytes 8388608 | tf_op jit(solution)/shard_map/slice | solution.py:63
  286.7 0.1 copy.30
  286.9 15.4 %fusion.18 = bf16[128,16,64]{2,1,0:T(8,128)(2,1)S(1)} fusion(bf16[128,2,8,1024]{3,2,1,0:T(8,128)(2,1)} %copy.29, bf16[128,1024,2,64]{1,3,2,0:T(8,128)(2,1)} %param.28, f32[128,2,64]{2,1,0:T(2,128)S(1)} %copy.31, f32[128,2,8]{2,1,0:T(2,128)S(1)} %copy.30), kind=kOutput, calls=%fused_computation.31 | convolution fusion | flops 268828672 | bytes 38084608 | tf_op jit(solution)/shard_map/bkgt,btks->bkgs/dot_general | solution.py:63
  302.2 7.2 %convolution_bitcast_fusion = f32[128,5120]{1,0:T(8,128)} fusion(bf16[16,64,5120]{2,1,0:T(8,128)(2,1)} %param.22, bf16[128,16,64]{2,1,0:T(8,128)(2,1)S(1)} %fusion.18), kind=kOutput, calls=%fused_computation.6 | convolution fusion | flops 1342177280 | bytes 13369344 | tf_op jit(solution)/shard_map/bhs,hsd->bd/dot_general | solution.py:67
  309.4 0.0 all-reduce.6.cloned.1.call-update
  309.4 0.0 copy-start.6
  309.4 0.3 all-reduce.8.cloned.1.call-start
  309.7 53.5 %all-reduce.6.cloned.1.call-done = f32[128,5120]{1,0:T(8,128)} async-done(((f32[128,5120]{1,0:T(8,128)}), f32[128,5120]{1,0:T(8,128)}) %all-reduce.6.cloned.1.call-update) | async-done | bytes 2621456 | tf_op jit(solution)/shard_map/psum | solution.py:67
  363.3 2.2 fusion.8
  365.5 14.0 %fusion.24 = f32[128,3200]{1,0:T(8,128)} fusion(bf16[5120,3200]{1,0:T(8,128)(2,1)} %param.24, bf16[128,5120]{1,0:T(8,128)(2,1)S(1)} %get-tuple-element.4, f32[5120]{0:T(1024)S(1)} %copy-done.6, f32[128]{0:T(128)S(1)} %add_rsqrt_fusion), kind=kOutput, calls=%fused_computation.41 | convolution fusion | flops 4196925440 | bytes 35738112 | tf_op jit(solution)/shard_map/dot_general | solution.py:70
  379.5 25.6 %fusion.3 = f32[128,5120]{1,0:T(8,128)} fusion(bf16[3200,5120]{1,0:T(8,128)(2,1)} %param.26, bf16[5120,3200]{1,0:T(8,128)(2,1)} %param.25, f32[128,3200]{1,0:T(8,128)} %fusion.24, bf16[128,5120]{1,0:T(8,128)(2,1)S(1)} %get-tuple-element.4, f32[5120]{0:T(1024)S(1)} %copy-done.6, f32[128]{0:T(128)S(1)} %add_rsqrt_fusion), kind=kOutput, calls=%fused_computation.9 | convolution fusion | flops 8393687040 | bytes 71127552 | tf_op jit(solution)/shard_map/dot_general | solution.py:73
  405.1 0.0 all-reduce.8.cloned.1.call-update
  405.1 0.0 copy-start.1
  405.1 53.2 %all-reduce.8.cloned.1.call-done = f32[128,5120]{1,0:T(8,128)} async-done(((f32[128,5120]{1,0:T(8,128)}), f32[128,5120]{1,0:T(8,128)}) %all-reduce.8.cloned.1.call-update) | async-done | bytes 2621456 | tf_op jit(solution)/shard_map/psum | solution.py:73
  458.3 3.1 fusion.11
  (26 shorter events, 0.1 us)
Async XLA Ops:
  7.2 8.1 %copy-start = (bf16[5120,2,64]{0,2,1:T(8,128)(2,1)S(1)}, bf16[5120,2,64]{0,2,1:T(8,128)(2,1)}, u32[]{:S(2)}) copy-start(bf16[5120,2,64]{0,2,1:T(8,128)(2,1)} %param.18) | copy-start | bytes 3932164
  7.2 257.1 %all-reduce.4.cloned.1.call-start = ((), (), s32[]{:S(2)}) async-start(), calls=%async_computation | async-start | bytes 16793600 | tf_op jit(solution)/shard_map/psum | solution.py:57
  9.0 6.3 %copy-start.3 = (bf16[128,5120]{1,0:T(8,128)(2,1)S(1)}, bf16[128,5120]{1,0:T(8,128)(2,1)}, u32[]{:S(2)}) copy-start(bf16[128,5120]{1,0:T(8,128)(2,1)} %param.15) | copy-start | bytes 3932164
  9.0 6.3 %copy-start.9 = (f32[5120]{0:T(1024)S(1)}, f32[5120]{0:T(1024)}, u32[]{:S(2)}) copy-start(f32[5120]{0:T(1024)} %param.16) | copy-start | bytes 61444
  15.2 10.8 %copy-start.8 = (f32[64]{0:T(128)S(1)}, f32[64]{0:T(128)}, u32[]{:S(2)}) copy-start(f32[64]{0:T(128)} %param.20) | copy-start | bytes 772
  15.2 10.8 %copy-start.10 = (f32[64]{0:T(128)S(1)}, f32[64]{0:T(128)}, u32[]{:S(2)}) copy-start(f32[64]{0:T(128)} %param.21) | copy-start | bytes 772
  15.3 11.1 %copy-start.7 = (s32[128]{0:T(128)S(1)}, s32[128]{0:T(128)}, u32[]{:S(2)}) copy-start(s32[128]{0:T(128)} %param.29) | copy-start | bytes 1540
  26.3 13.0 %collective-permute-start = (f32[128,18,64]{0,2,1:T(8,128)S(1)}, f32[128,18,64]{0,2,1:T(8,128)S(1)}, u32[]{:S(2)}, u32[]{:S(2)}) collective-permute-start(f32[128,18,64]{0,2,1:T(8,128)S(1)} %multiply_multiply_fusion), channel_id=1, source_target_pairs={{0,4},{4,0},{1,5},{5,1},{2,6},{6,2},{3,7},{7,3}} | collective-permute-start | bytes 1769480 | tf_op jit(solution)/shard_map/ppermute | solution.py:50
  71.6 291.6 %all-reduce.6.cloned.1.call-start = ((), (), s32[]{:S(2)}) async-start(), calls=%async_computation.1 | async-start | bytes 5242880 | tf_op jit(solution)/shard_map/psum | solution.py:67
  73.8 196.3 %copy-start.5 = (bf16[128,2,64]{0,2,1:T(8,128)(2,1)}, bf16[128,2,64]{0,2,1:T(8,128)(2,1)S(1)}, u32[]{:S(2)}) copy-start(bf16[128,2,64]{0,2,1:T(8,128)(2,1)S(1)} %convert_element_type.54) | copy-start | bytes 98308
  264.3 5.8 %copy-start.2 = (f32[128,2,8,1025]{0,2,3,1:T(8,128)S(1)}, f32[128,2,8,1025]{0,2,3,1:T(8,128)}, u32[]{:S(2)}) copy-start(f32[128,2,8,1025]{0,2,3,1:T(8,128)} %all-reduce.4.cloned.1.call-done) | copy-start | bytes 25190404
  309.4 53.8 %copy-start.4 = (bf16[128,5120]{1,0:T(8,128)(2,1)S(1)}, bf16[128,5120]{1,0:T(8,128)(2,1)}, u32[]{:S(2)}) copy-start(bf16[128,5120]{1,0:T(8,128)(2,1)} %param.15) | copy-start | bytes 3932164
  309.4 56.1 %copy-start.6 = (f32[5120]{0:T(1024)S(1)}, f32[5120]{0:T(1024)}, u32[]{:S(2)}) copy-start(f32[5120]{0:T(1024)} %param.23) | copy-start | bytes 61444
  309.4 148.9 %all-reduce.8.cloned.1.call-start = ((), (), s32[]{:S(2)}) async-start(), calls=%async_computation.2 | async-start | bytes 5242880 | tf_op jit(solution)/shard_map/psum | solution.py:73
  405.1 56.2 %copy-start.1 = (bf16[5120,2,64]{0,2,1:T(8,128)(2,1)S(1)}, bf16[5120,2,64]{0,2,1:T(8,128)(2,1)}, u32[]{:S(2)}) copy-start(bf16[5120,2,64]{0,2,1:T(8,128)(2,1)} %param.18) | copy-start | bytes 3932164
Sparse Core Ops, SparseCore 0:
  71.8 192.4 all-reduce.3
  309.6 53.6 all-reduce.5
  405.3 53.0 all-reduce.7
where the time goes:
time: 468 us
  waiting for transfers between devices  310 us (66%)
  matrix products  87.2 us (19%)
  other arithmetic  27.3 us (6%)
  local copies, waits for them, and re-layouts  19.2 us (4%)
  between operations  14 us (3%)
  blocking collectives  10 us (2%)
    psum x1, waiting for transfers between devices, layer_body(): lax.psum(jnp.concatenate([cache_part, new_part[..., None]], axis=-1), 'dim')  190 us
    psum x1, waiting for transfers between devices, layer_body(): lax.psum(jnp.einsum('bhs,hsd->bd', attn_vals, w_out, preferred_element_ty...  53.5 us
    psum x1, waiting for transfers between devices, layer_body(): lax.psum(jnp.dot(mlp_act, w_down, preferred_element_type=jnp.float32), ml...  53.2 us
    dot_general x1, matrix products, layer_body(): jnp.dot(mlp_act, w_down, preferred_element_type=jnp.float32)  25.6 us
    dot_general x1, matrix products, layer_body(): jnp.einsum('bkgs,btks->bkgt', q_rot, k_cache, preferred_element_type=jnp....  16.3 us
    dot_general x1, matrix products, layer_body(): jnp.einsum('bkgt,btks->bkgs', attn_prob[..., :cache_len], v_cache, prefer...  15.4 us
    dot_general x1, matrix products, layer_body(): gate_val = jnp.dot(hidden2, w_gate, preferred_element_type=jnp.float32)  14 us
    ppermute x1, waiting for transfers between devices, layer_body(): partner = lax.ppermute(qk_norm, 'dim', swap_perm)  12.7 us
  transfers between devices with their start and end apart: 4, of which 4 were waited for; matrix products, arithmetic and copies ran while one was open for 1% of the time, Pallas kernels for 0%

commit v1 on v0

v1 whole, which is shorter than its diff:
```python
import functools

import jax
import jax.numpy as jnp
from jax import lax
from jax.experimental import pallas as pl
from jax.experimental.pallas import tpu as pltpu
from jax.sharding import PartitionSpec as P

EPS = 1e-6
ROPE_BASE = 1000000.0
MESH = pl.DeviceIdType.MESH

BLK = 128
LOW = 512
CH = 4
UCH = 16
SLOTS = 4
FIRST = 8
LEAD = 4
UP_SIZES = (320, 336, 352, 512)


def rms_scale(values, gain):
    mean_sq = jnp.mean(values * values, axis=-1, keepdims=True)
    return values * lax.rsqrt(mean_sq + EPS) * gain


def attn_kernel(n_up, scale, pos_ref, off_ref, idx_ref, qd_ref, qf_ref, kf_ref, vn_ref, k_hbm, v_hbm, o_ref,
                kbuf, vbuf, own_lo, own_up, pack, rlo, rup, ksem, vsem, slo_s, slo_r, sup_s, sup_r):
    partner = {"dim": 1 - lax.axis_index("dim")}
    rows = qd_ref.shape[0]
    n_ch = rows // CH
    n_uch = n_up // UCH
    up_blocks = own_up.shape[0] // rows

    def kcopy(c):
        return pltpu.make_async_copy(k_hbm.at[pl.ds(c * CH, CH)], kbuf.at[lax.rem(c, SLOTS)], ksem.at[lax.rem(c, SLOTS)])

    def vcopy(c):
        return pltpu.make_async_copy(v_hbm.at[pl.ds(c * CH, CH)], vbuf.at[lax.rem(c, SLOTS)], vsem.at[lax.rem(c, SLOTS)])

    def lo_copy(c):
        part = pl.ds(c * CH, CH)
        return pltpu.make_async_remote_copy(src_ref=own_lo.at[part], dst_ref=rlo.at[part], send_sem=slo_s.at[c],
                                            recv_sem=slo_r.at[c], device_id=partner, device_id_type=MESH)

    def up_copy(c):
        part = pl.ds(c * UCH, UCH)
        return pltpu.make_async_remote_copy(src_ref=pack.at[part], dst_ref=rup.at[part], send_sem=sup_s.at[c],
                                            recv_sem=sup_r.at[c], device_id=partner, device_id_type=MESH)

    for c in range(SLOTS):
        kcopy(c).start()
    barrier = pltpu.get_barrier_semaphore()
    pl.semaphore_signal(barrier, inc=1, device_id=partner, device_id_type=MESH)
    pl.semaphore_wait(barrier, 1)
    for c in range(SLOTS):
        vcopy(c).start()

    @pl.loop(0, n_ch)
    def _(c):
        kcopy(c).wait()
        for r in range(CH):
            b = c * CH + r
            s = jnp.dot(qd_ref[b], kbuf[lax.rem(c, SLOTS), r], preferred_element_type=jnp.float32)
            own_lo[b] = s[:, :LOW]
            for j in range(up_blocks):
                own_up[b * up_blocks + j] = s[:, LOW + j * BLK:LOW + (j + 1) * BLK]

        @pl.when(c + SLOTS < n_ch)
        def _():
            kcopy(c + SLOTS).start()

        @pl.when((c >= 1) & (c <= FIRST))
        def _():
            lo_copy(c - 1).start()

    @pl.loop(0, n_uch + 1)
    def _(c):
        @pl.when(c < n_uch)
        def _():
            for r in range(UCH):
                j = c * UCH + r
                pack[j] = own_up[idx_ref[j]]

        @pl.when(c >= 1)
        def _():
            up_copy(c - 1).start()

    @pl.loop(FIRST, FIRST + LEAD)
    def _(c):
        lo_copy(c).start()

    @pl.loop(0, n_uch)
    def _(c):
        up_copy(c).wait_recv()

    lane = lax.broadcasted_iota(jnp.int32, (8, 2 * 64), 1)
    t_up = lax.broadcasted_iota(jnp.int32, (16, BLK), 1) + LOW

    @pl.loop(0, n_ch)
    def _(c):
        @pl.when(c + FIRST + LEAD < n_ch)
        def _():
            lo_copy(c + FIRST + LEAD).start()

        vcopy(c).wait()
        lo_copy(c).wait_recv()
        for r in range(CH):
            b = c * CH + r
            pos = pos_ref[b]
            off = off_ref[b]
            parts = [(own_lo[b] + rlo[b]) * scale]
            for j in range(up_blocks):
                total = (own_up[b * up_blocks + j] + rup[jnp.minimum(off + j, n_up - 1)]) * scale
                parts.append(jnp.where(t_up + j * BLK < pos, total, -jnp.inf))
            s = jnp.concatenate(parts, axis=1)
            kf = kf_ref[b]
            k_rows = jnp.concatenate([jnp.broadcast_to(kf[0:1], (8, 128)), jnp.broadcast_to(kf[1:2], (8, 128))], axis=0)
            s_new = jnp.sum(qf_ref[b].astype(jnp.float32) * k_rows, axis=1, keepdims=True) * scale
            m = jnp.maximum(jnp.max(s, axis=1, keepdims=True), s_new)
            e = jnp.exp(s - m)
            e_new = jnp.exp(s_new - m)
            inv = 1.0 / (jnp.sum(e, axis=1, keepdims=True) + e_new)
            p = (e * inv).astype(jnp.bfloat16)
            p_new = (e_new * inv).astype(jnp.bfloat16).astype(jnp.float32)
            o = lax.dot_general(p, vbuf[lax.rem(c, SLOTS), r], (((1,), (1,)), ((), ())), preferred_element_type=jnp.float32)
            o = o + p_new * vn_ref[pl.ds(b, 1), :]
            o_ref[b] = jnp.where(lane < 64, o[0:8], o[8:16]).astype(jnp.bfloat16)

        @pl.when(c + SLOTS < n_ch)
        def _():
            vcopy(c + SLOTS).start()

    @pl.loop(0, n_ch)
    def _(c):
        lo_copy(c).wait_send()

    @pl.loop(0, n_uch)
    def _(c):
        up_copy(c).wait_send()


def attend(n_up, cid, scale, pos, off, idx, qd, qf, kf, vn, k_t, v_t):
    rows = qd.shape[0]
    n_ch = rows // CH
    n_uch = n_up // UCH
    cache_len = k_t.shape[2]
    up_blocks = (cache_len - LOW) // BLK
    smem = pl.BlockSpec(memory_space=pltpu.SMEM)
    vmem = pl.BlockSpec(memory_space=pltpu.VMEM)
    hbm = pl.BlockSpec(memory_space=pl.ANY)
    return pl.pallas_call(
        functools.partial(attn_kernel, n_up, scale),
        out_shape=jax.ShapeDtypeStruct((rows, 8, 128), jnp.bfloat16),
        in_specs=[smem, smem, smem, vmem, vmem, vmem, vmem, hbm, hbm],
        out_specs=vmem,
        scratch_shapes=[
            pltpu.VMEM((SLOTS, CH, 128, cache_len), jnp.bfloat16),
            pltpu.VMEM((SLOTS, CH, 128, cache_len), jnp.bfloat16),
            pltpu.VMEM((rows, 16, LOW), jnp.float32),
            pltpu.VMEM((rows * up_blocks, 16, BLK), jnp.float32),
            pltpu.VMEM((n_up, 16, BLK), jnp.float32),
            pltpu.VMEM((rows, 16, LOW), jnp.float32),
            pltpu.VMEM((n_up, 16, BLK), jnp.float32),
            pltpu.SemaphoreType.DMA((SLOTS,)),
            pltpu.SemaphoreType.DMA((SLOTS,)),
            pltpu.SemaphoreType.DMA((n_ch,)),
            pltpu.SemaphoreType.DMA((n_ch,)),
            pltpu.SemaphoreType.DMA((n_uch,)),
            pltpu.SemaphoreType.DMA((n_uch,)),
        ],
        compiler_params=pltpu.CompilerParams(collective_id=cid, has_side_effects=True, vmem_limit_bytes=40 * 1024 * 1024),
        name=f"attend_{n_up}",
    )(pos, off, idx, qd, qf, kf, vn, k_t, v_t)


def solution(mesh):
    dim_count = mesh.shape['dim']
    mlp_axes = ('heads', 'dim')
    swap_perm = [(src, (src + dim_count // 2) % dim_count) for src in range(dim_count)]

    def layer_body(tokens, ln_attn, w_query, w_key, w_value, q_gain, k_gain, w_out, ln_mlp, w_gate, w_up, w_down, k_cache, v_cache, positions):
        rows = tokens.shape[0]
        heads_local = w_query.shape[1]
        kv_local = w_key.shape[1]
        slice_len = w_query.shape[2]
        head_dim = slice_len * dim_count
        half_dim = head_dim // 2
        q_group = heads_local // kv_local
        cache_len = k_cache.shape[1]
        up_blocks = (cache_len - LOW) // BLK
        dim_index = lax.axis_index('dim')

        tok_f32 = tokens.astype(jnp.float32)
        hidden = rms_scale(tok_f32, ln_attn).astype(jnp.bfloat16)
        q_part = jnp.einsum('bd,dhs->bhs', hidden, w_query, preferred_element_type=jnp.float32)
        k_part = jnp.einsum('bd,dhs->bhs', hidden, w_key, preferred_element_type=jnp.float32)
        v_new = jnp.einsum('bd,dhs->bhs', hidden, w_value, preferred_element_type=jnp.float32).astype(jnp.bfloat16)

        own = jnp.concatenate([q_part, k_part], axis=1)
        other = lax.ppermute(own, 'dim', swap_perm)
        gains = jnp.stack([q_gain, k_gain])
        gains_other = lax.ppermute(gains, 'dim', swap_perm)
        sq_total = jnp.sum(own * own, axis=-1, keepdims=True) + jnp.sum(other * other, axis=-1, keepdims=True)
        inv = lax.rsqrt(sq_total / head_dim + EPS)

        def spread(pair):
            return jnp.concatenate([jnp.broadcast_to(pair[0], (heads_local, slice_len)), jnp.broadcast_to(pair[1], (kv_local, slice_len))], axis=0)

        u_own = own * inv * spread(gains)
        u_other = other * inv * spread(gains_other)
        inv_freq = ROPE_BASE ** (-jnp.arange(half_dim, dtype=jnp.float32) * 2.0 / head_dim)
        rot_angle = positions.astype(jnp.float32)[:, None, None] * inv_freq
        cos_t = jnp.cos(rot_angle)
        sin_t = jnp.where(dim_index == 0, -1.0, 1.0) * jnp.sin(rot_angle)
        r_own = (u_own * cos_t + u_other * sin_t).astype(jnp.bfloat16)
        r_other = (u_other * cos_t - u_own * sin_t).astype(jnp.bfloat16)
        k_new = r_own[:, heads_local:]
        qf = jnp.concatenate([r_own[:, :heads_local], r_other[:, :heads_local]], axis=-1)
        kf = jnp.concatenate([k_new, r_other[:, heads_local:]], axis=-1).astype(jnp.float32)
        zeros = jnp.zeros((rows, q_group, slice_len), jnp.bfloat16)
        qd = jnp.concatenate([
            jnp.concatenate([r_own[:, :q_group], zeros], axis=-1),
            jnp.concatenate([zeros, r_own[:, q_group:heads_local]], axis=-1)], axis=1)
        vn = v_new.reshape(rows, kv_local * slice_len).astype(jnp.float32)

        n_blk = (positions - LOW + BLK - 1) // BLK
        cum = jnp.cumsum(n_blk)
        off = cum - n_blk
        slot = jnp.arange(rows * up_blocks)
        row_of = jnp.sum((cum[None, :] <= slot[:, None]).astype(jnp.int32), axis=1)
        off_of = jnp.sum(jnp.where(row_of[:, None] == jnp.arange(rows)[None, :], off[None, :], 0), axis=1)
        idx = jnp.where(row_of < rows, row_of * up_blocks + slot - off_of, 0)

        k_t = k_cache.transpose(0, 2, 3, 1).reshape(rows, kv_local * slice_len, cache_len)
        v_t = v_cache.transpose(0, 2, 3, 1).reshape(rows, kv_local * slice_len, cache_len)
        which = jnp.sum((cum[-1] > jnp.array(UP_SIZES[:-1])).astype(jnp.int32))
        branches = [functools.partial(attend, n, i, head_dim ** -0.5) for i, n in enumerate(UP_SIZES)]
        attn = lax.switch(which, branches, positions, off, idx, qd, qf, kf, vn, k_t, v_t)
        attn_vals = attn.reshape(rows, q_group, kv_local, slice_len).transpose(0, 2, 1, 3).reshape(rows, heads_local, slice_len)

        attn_out = lax.psum(jnp.einsum('bhs,hsd->bd', attn_vals, w_out, preferred_element_type=jnp.float32), mlp_axes)
        resid_f32 = (tok_f32 + attn_out).astype(jnp.bfloat16).astype(jnp.float32)
        hidden2 = rms_scale(resid_f32, ln_mlp).astype(jnp.bfloat16)
        gate_val = jnp.dot(hidden2, w_gate, preferred_element_type=jnp.float32)
        up_val = jnp.dot(hidden2, w_up, preferred_element_type=jnp.float32)
        mlp_act = (jax.nn.silu(gate_val) * up_val).astype(jnp.bfloat16)
        mlp_out = lax.psum(jnp.dot(mlp_act, w_down, preferred_element_type=jnp.float32), mlp_axes)
        return (resid_f32 + mlp_out).astype(jnp.bfloat16), k_new, v_new

    row_spec = P('dp', None)
    head_spec = P(None, 'heads', 'dim')
    cache_spec = P('dp', None, 'heads', 'dim')
    new_spec = P('dp', 'heads', 'dim')
    in_specs = (row_spec, P(None), head_spec, head_spec, head_spec, P('dim'), P('dim'), P('heads', 'dim', None), P(None), P(None, mlp_axes), P(None, mlp_axes), P(mlp_axes, None), cache_spec, cache_spec, P('dp'))
    out_specs = (row_spec, new_spec, new_spec)
    return jax.shard_map(layer_body, mesh=mesh, in_specs=in_specs, out_specs=out_specs, check_vma=False)
```

time: 468 us -> 359 us (0.77)
  waiting for transfers between devices: 310 us -> 116 us
  Pallas kernels: 0 us -> 153 us
  matrix products: 87.2 us -> 56.2 us
  local copies, waits for them, and re-layouts: 19.2 us -> 2.5 us
  other arithmetic: 27.3 us -> 12 us
  blocking collectives: 10 us -> 0 us
    psum x1 -> x0, waiting for transfers between devices: 190 us -> none  [layer_body(): lax.psum(jnp.concatenate([cache_part, new_part[..., None]], axis=-1), 'dim')]
    pallas_call x0 -> x1, Pallas kernels: none -> 153 us  [attend(): pl.pallas_call(functools.partial(attn_kernel, n_up, scale), out_shape=jax...]
    dot_general x2 -> x0, matrix products: 31.7 us -> none  [the longest x1 16.3 us: layer_body(): jnp.einsum('bkgs,btks->bkgt', q_rot, k_cache, preferred_element_type=jnp....]
    psum x1 -> x0, blocking collectives: 10 us -> none  [layer_body(): lax.psum(jnp.sum(qk_part * qk_part, axis=-1, keepdims=True), 'dim')]
    slice x3 -> x6, local copies, waits for them, and re-layouts: 9.66 us -> 0.58 us  [the longest x1 0.51 us: layer_body(): which = jnp.sum((cum[-1] > jnp.array(UP_SIZES[:-1])).astype(jnp.int32))]
    dot_general x1 -> x0, local copies, waits for them, and re-layouts: 8.76 us -> none  [layer_body(): jnp.einsum('bkgs,btks->bkgt', q_rot, k_cache, preferred_element_type=jnp....]
    concatenate x2 -> x3, other arithmetic: 6.01 us -> 0.12 us  [the longest x1 0.11 us: layer_body(): jnp.concatenate([jnp.concatenate([r_own[:, :q_group], zeros], axis=-1), j...]
    reduce_max x1 -> x0, other arithmetic: 5.83 us -> none  [layer_body(): exp_scores = jnp.exp(scores - jnp.max(scores, axis=-1, keepdims=True))]
  transfers between devices with their start and end apart: 4 -> 4, of which waited for: 4 -> 3; matrix products, arithmetic and copies ran while one was open for 1% -> 4% of each run, Pallas kernels for 0% -> 0%
where the time goes in v1:
time: 359 us
  Pallas kernels  153 us (43%)
  waiting for transfers between devices  116 us (32%)
  matrix products  56.2 us (16%)
  between operations  15 us (4%)
  other arithmetic  12 us (3%)
    pallas_call x1, Pallas kernels, attend(): pl.pallas_call(functools.partial(attn_kernel, n_up, scale), out_shape=jax...  153 us
    psum x1, waiting for transfers between devices, layer_body(): lax.psum(jnp.einsum('bhs,hsd->bd', attn_vals, w_out, preferred_element_ty...  54.5 us
    psum x1, waiting for transfers between devices, layer_body(): lax.psum(jnp.dot(mlp_act, w_down, preferred_element_type=jnp.float32), ml...  53.1 us
    dot_general x1, matrix products, layer_body(): jnp.dot(mlp_act, w_down, preferred_element_type=jnp.float32)  25.6 us
    dot_general x1, matrix products, layer_body(): gate_val = jnp.dot(hidden2, w_gate, preferred_element_type=jnp.float32)  14 us
    unnamed x3, matrix products  9.53 us
    ppermute x1, waiting for transfers between devices, layer_body(): other = lax.ppermute(own, 'dim', swap_perm)  8.74 us
  transfers between devices with their start and end apart: 4, of which 3 were waited for; matrix products, arithmetic and copies ran while one was open for 4% of the time, Pallas kernels for 0%

profile of v1, /device:TPU:0, one launch (start us, length us, event | category | flops | bytes accessed | tf_op | source)
XLA Modules:
  0.0 359.0 jit_solution(2931129717232951805)
XLA Ops:
  7.2 0.0 copy-start
  7.2 0.0 copy-start.2
  7.2 0.0 copy-start.9
  7.2 0.0 all-reduce.5.cloned.1.call-start
  7.2 0.8 pad_maximum_fusion.4
  8.1 3.4 collective-permute-start.1
  11.5 1.6 fusion.2
  13.1 1.9 fusion.28
  15.1 0.0 copy-start.6
  15.1 5.7 %fusion.30 = f32[128,1024]{0,1:S(1)} fusion(bf16[5120,1024]{0,1:T(8,128)(2,1)} %bitcast.56, bf16[128,5120]{1,0:T(8,128)(2,1)S(1)} %copy-done.2, f32[5120]{0:T(1024)S(1)} %copy-done.9, f32[128]{0:T(128)S(1)} %add_rsqrt_fusion.2), kind=kOutput, calls=%fused_computation.66 | convolution fusion | flops 1344798720 | bytes 12341760
  20.8 0.0 copy-start.7
  20.8 0.0 copy-start.10
  20.8 0.9 multiply_reduce_fusion.1
  21.7 0.0 collective-permute-start
  21.7 0.1 copy.74
  21.8 0.2 reduce-window.4
  22.0 0.1 reduce
  22.1 0.2 convert_reduce_fusion
  22.3 1.9 fusion.26
  24.2 0.6 bitcast_convert_fusion
  24.8 0.2 select_reduce_fusion
  25.1 0.2 multiply_cosine_fusion
  25.3 0.5 slice.37
  25.8 1.3 fusion.24
  27.7 8.7 %collective-permute-done = f32[128,18,64]{0,2,1:T(8,128)S(1)} collective-permute-done((f32[128,18,64]{0,2,1:T(8,128)}, f32[128,18,64]{0,2,1:T(8,128)S(1)}, u32[]{:S(2)}, u32[]{:S(2)}) %collective-permute-start) | collective-permute-done | bytes 589856 | tf_op jit(solution)/shard_map/ppermute | solution.py:203
  36.5 0.1 multiply_reduce_fusion
  36.6 0.4 subtract_convert_fusion
  37.1 0.1 fusion.18
  37.2 0.4 copy-done.4
  37.6 154.5 %conditional.1 = (bf16[128,8,128]{2,1,0:T(8,128)(2,1)S(1)}) conditional(s32[]{:T(128)} %clamp.3, (s32[128]{0:T(128)S(1)}, s32[128]{0:T(128)S(1)}, s32[512]{0:T(512)S(1)}, bf16[128,16,128]{0,2,1:T(8,128)(2,1)S(1)}, bf16[128,16,128]{0,2,1:T(8,128)(2,1)S(1)}, /*index=5*/f32[128,2,128]{0,2,1:T(8,128)S(1)}, ...), branch_computations={%region_7.8_spmd, %region_8.9_spmd, %region_9.10_spmd, %region_10.... | conditional | bytes 2490376 | solution.py:241
  37.6 0.1 copy.82.vn_ref
  37.7 0.1 copy.81.kf_ref
  37.8 0.4 copy.80.qf_ref
  38.3 0.4 copy.79.qd_ref
  38.7 153.3 %attend_336.1 = bf16[128,8,128]{2,1,0:T(8,128)(2,1)S(1)} custom-call(s32[128]{0:T(128)S(1)} %get-tuple-element.86.pos_ref, s32[128]{0:T(128)S(1)} %get-tuple-element.87.off_ref, s32[512]{0:T(512)S(1)} %get-tuple-element.88.idx_ref, bf16[128,16,128]{2,1,0:T(8,128)(2,1)S(1)} %copy.79.qd_ref, bf16[128,16,128]{2,1,0:T(8,128)(2,1)S(1)} %copy.80.qf_ref, ...), custom_call_target="tpu_custom_call" | custom-call | tf_op jit(solution)/shard_map/cond/branch_1_fun/attend_336/pallas_call | solution.py:154
  192.2 0.2 copy.91
  192.4 7.1 %convolution_bitcast_fusion = f32[128,5120]{1,0:T(8,128)} fusion(bf16[128,16,64]{0,2,1:T(8,128)(2,1)S(1)} %bitcast.48, bf16[16,64,5120]{2,1,0:T(8,128)(2,1)} %param.27), kind=kOutput, calls=%fused_computation | convolution fusion | flops 1342177280 | bytes 13369344 | tf_op jit(solution)/shard_map/bhs,hsd->bd/dot_general | solution.py:244
  199.5 0.0 all-reduce.5.cloned.1.call-update
  199.5 0.0 copy-start.5
  199.5 0.0 all-reduce.7.cloned.1.call-start
  199.6 54.5 %all-reduce.5.cloned.1.call-done = f32[128,5120]{1,0:T(8,128)} async-done(((f32[128,5120]{1,0:T(8,128)}), f32[128,5120]{1,0:T(8,128)}) %all-reduce.5.cloned.1.call-update) | async-done | bytes 2621456 | tf_op jit(solution)/shard_map/psum | solution.py:244
  254.1 2.2 fusion.6
  256.3 14.0 %fusion.21 = f32[128,3200]{1,0:T(8,128)} fusion(bf16[5120,3200]{1,0:T(8,128)(2,1)} %param.29, bf16[128,5120]{1,0:T(8,128)(2,1)S(1)} %get-tuple-element.261, f32[5120]{0:T(1024)S(1)} %copy-done.5, f32[128]{0:T(128)S(1)} %add_rsqrt_fusion.1), kind=kOutput, calls=%fused_computation.37 | convolution fusion | flops 4196925440 | bytes 35738112 | tf_op jit(solution)/shard_map/dot_general | solution.py:247
  270.3 25.6 %fusion.1 = f32[128,5120]{1,0:T(8,128)} fusion(bf16[3200,5120]{1,0:T(8,128)(2,1)} %param.31, bf16[5120,3200]{1,0:T(8,128)(2,1)} %param.30, f32[128,3200]{1,0:T(8,128)} %fusion.21, bf16[128,5120]{1,0:T(8,128)(2,1)S(1)} %get-tuple-element.261, f32[5120]{0:T(1024)S(1)} %copy-done.5, f32[128]{0:T(128)S(1)} %add_rsqrt_fusion.1), kind=kOutput, calls=%fused_computation.3 | convolution fusion | flops 8393687040 | bytes 71127552 | tf_op jit(solution)/shard_map/dot_general | solution.py:250
  296.0 0.0 all-reduce.7.cloned.1.call-update
  296.0 0.0 copy-start.1
  296.0 53.1 %all-reduce.7.cloned.1.call-done = f32[128,5120]{1,0:T(8,128)} async-done(((f32[128,5120]{1,0:T(8,128)}), f32[128,5120]{1,0:T(8,128)}) %all-reduce.7.cloned.1.call-update) | async-done | bytes 2621456 | tf_op jit(solution)/shard_map/psum | solution.py:250
  349.1 3.1 fusion.9
  (35 shorter events, 0.2 us)
Async XLA Ops:
  7.2 6.0 %copy-start = (bf16[5120,2,64]{0,2,1:T(8,128)(2,1)S(1)}, bf16[5120,2,64]{0,2,1:T(8,128)(2,1)}, u32[]{:S(2)}) copy-start(bf16[5120,2,64]{0,2,1:T(8,128)(2,1)} %param.23) | copy-start | bytes 3932164
  7.2 7.9 %copy-start.2 = (bf16[128,5120]{1,0:T(8,128)(2,1)S(1)}, bf16[128,5120]{1,0:T(8,128)(2,1)}, u32[]{:S(2)}) copy-start(bf16[128,5120]{1,0:T(8,128)(2,1)} %param.20) | copy-start | bytes 3932164
  7.2 7.9 %copy-start.9 = (f32[5120]{0:T(1024)S(1)}, f32[5120]{0:T(1024)}, u32[]{:S(2)}) copy-start(f32[5120]{0:T(1024)} %param.21) | copy-start | bytes 61444
  7.2 246.9 %all-reduce.5.cloned.1.call-start = ((), (), s32[]{:S(2)}) async-start(), calls=%async_computation | async-start | bytes 5242880 | tf_op jit(solution)/shard_map/psum | solution.py:244
  8.1 19.6 %collective-permute-start.1 = (f32[2,64]{1,0:T(2,128)S(1)}, f32[2,64]{1,0:T(2,128)S(1)}, u32[]{:S(2)}, u32[]{:S(2)}) collective-permute-start(f32[2,64]{1,0:T(2,128)S(1)} %pad_maximum_fusion.4), channel_id=1, source_target_pairs={{0,4},{4,0},{1,5},{5,1},{2,6},{6,2},{3,7},{7,3}} | collective-permute-start | bytes 1544 | tf_op jit(solution)/shard_map/ppermute | solution.py:205
  15.1 6.6 %copy-start.6 = (s32[128]{0:T(128)S(1)}, s32[128]{0:T(128)}, u32[]{:S(2)}) copy-start(s32[128]{0:T(128)} %param.34) | copy-start | bytes 1540
  20.8 5.0 %copy-start.8 = (f32[64]{0:T(128)S(1)}, f32[64]{0:T(128)}, u32[]{:S(2)}) copy-start(f32[64]{0:T(128)} %param.26) | copy-start | bytes 772
  20.8 5.0 %copy-start.7 = (f32[64]{0:T(128)S(1)}, f32[64]{0:T(128)}, u32[]{:S(2)}) copy-start(f32[64]{0:T(128)} %param.25) | copy-start | bytes 772
  20.8 5.0 %copy-start.10 = (s32[3]{0:T(128)S(1)}, s32[3]{0:T(128)}, u32[]{:S(2)}) copy-start(s32[3]{0:T(128)} %constant.69.clone) | copy-start | bytes 40
  21.7 14.8 %collective-permute-start = (f32[128,18,64]{0,2,1:T(8,128)}, f32[128,18,64]{0,2,1:T(8,128)S(1)}, u32[]{:S(2)}, u32[]{:S(2)}) collective-permute-start(f32[128,18,64]{0,2,1:T(8,128)} %get-tuple-element.267), channel_id=1, source_target_pairs={{0,4},{4,0},{1,5},{5,1},{2,6},{6,2},{3,7},{7,3}} | collective-permute-start | bytes 1769480 | tf_op jit(solution)/shard_map/ppermute | solution.py:203
  37.0 0.6 copy-start.4
  199.5 54.6 %copy-start.3 = (bf16[128,5120]{1,0:T(8,128)(2,1)S(1)}, bf16[128,5120]{1,0:T(8,128)(2,1)}, u32[]{:S(2)}) copy-start(bf16[128,5120]{1,0:T(8,128)(2,1)} %param.20) | copy-start | bytes 3932164
  199.5 56.8 %copy-start.5 = (f32[5120]{0:T(1024)S(1)}, f32[5120]{0:T(1024)}, u32[]{:S(2)}) copy-start(f32[5120]{0:T(1024)} %param.28) | copy-start | bytes 61444
  199.5 149.6 %all-reduce.7.cloned.1.call-start = ((), (), s32[]{:S(2)}) async-start(), calls=%async_computation.1 | async-start | bytes 5242880 | tf_op jit(solution)/shard_map/psum | solution.py:250
  296.0 56.2 %copy-start.1 = (bf16[5120,2,64]{0,2,1:T(8,128)(2,1)S(1)}, bf16[5120,2,64]{0,2,1:T(8,128)(2,1)}, u32[]{:S(2)}) copy-start(bf16[5120,2,64]{0,2,1:T(8,128)(2,1)} %param.23) | copy-start | bytes 3932164
Sparse Core Ops, SparseCore 0:
  199.7 54.4 all-reduce.4
  296.1 52.9 all-reduce.6

commit v2 on v1

--- a/solution.py
+++ b/solution.py
@@ -176,6 +176,268 @@
     )(pos, off, idx, qd, qf, kf, vn, k_t, v_t)
 
 
+Q = 10
+WO_SLOTS = 4
+GU_SLOTS = 4
+WD_SLOTS = 4
+
+
+def tail_kernel(x_ref, tok_ref, ln_ref, wo_hbm, wg_hbm, wu_hbm, wd_hbm, out_ref,
+                part, r1, r2, r3, full, xres, acc_g, acc_u, mact, wo, wg, wu, wd,
+                wo_s, wg_s, wu_s, wd_s, snd, rcv):
+    heads = lax.axis_index("heads")
+    core, cx, cy = lax.rem(heads, 2), heads // 2, lax.axis_index("dim")
+    sib = {"heads": 2 * cx + 1 - core}
+    xn = {"heads": 2 * (1 - cx) + core}
+    yn = {"dim": 1 - cy}
+    width = part.shape[3]
+    rows = 16 * 8
+    f32 = jnp.float32
+
+    def cols(q):
+        return pl.ds(pl.multiple_of(q * width, width), width)
+
+    def wo_copy(q):
+        s = lax.rem(q, WO_SLOTS)
+        return [pltpu.make_async_copy(wo_hbm.at[:, cols(q)], wo.at[s], wo_s.at[s])]
+
+    def gu_copy(q):
+        s = lax.rem(q, GU_SLOTS)
+        return [pltpu.make_async_copy(wg_hbm.at[cols(q)], wg.at[s], wg_s.at[s]),
+                pltpu.make_async_copy(wu_hbm.at[cols(q)], wu.at[s], wu_s.at[s])]
+
+    def wd_copy(q):
+        s = lax.rem(q, WD_SLOTS)
+        return [pltpu.make_async_copy(wd_hbm.at[:, cols(q)], wd.at[s], wd_s.at[s])]
+
+    def start(copies):
+        for cp in copies:
+            cp.start()
+
+    def wait(copies):
+        for cp in copies:
+            cp.wait()
+
+    def remote(ph, st, q, src, dst, dev):
+        return pltpu.make_async_remote_copy(src_ref=src, dst_ref=dst, send_sem=snd.at[ph, st], recv_sem=rcv.at[ph, st, q],
+                                            device_id=dev, device_id_type=MESH)
+
+    def stage(ph, k, q, sem_q):
+        if k == 0:
+            return [remote(ph, 0, sem_q, part.at[q, pl.ds(8 * (1 - core), 8)], r1.at[q], sib)]
+        if k == 1:
+            return [remote(ph, 1, sem_q, r1.at[q, pl.ds(2 * (1 - cx), 2)], r2.at[q, pl.ds(0, 2)], xn),
+                    remote(ph, 2, sem_q, r1.at[q, pl.ds(4 + 2 * (1 - cy), 2)], r2.at[q, pl.ds(2, 2)], yn)]
+        if k == 2:
+            return [remote(ph, 3, sem_q, r2.at[q, pl.ds(1 - cy, 1)], r3.at[q, pl.ds(0, 1)], yn),
+                    remote(ph, 4, sem_q, r2.at[q, pl.ds(2 + 1 - cx, 1)], r3.at[q, pl.ds(1, 1)], xn)]
+        blk_a, blk_b = core * 8, core * 8 + 4
+        if k == 3:
+            a, b = full.at[q, pl.ds(blk_a + 2 * cx + cy, 1)], full.at[q, pl.ds(blk_b + 2 * cy + cx, 1)]
+            return [remote(ph, 5, sem_q, a, a, yn), remote(ph, 6, sem_q, b, b, xn)]
+        if k == 4:
+            a, b = full.at[q, pl.ds(blk_a + 2 * cx, 2)], full.at[q, pl.ds(blk_b + 2 * cy, 2)]
+            return [remote(ph, 7, sem_q, a, a, xn), remote(ph, 8, sem_q, b, b, yn)]
+        a = full.at[q, pl.ds(blk_a, 8)]
+        return [remote(ph, 9, sem_q, a, a, sib)]
+
+    def one(ph, k, q):
+        return stage(ph, k, q, q)
+
+    def drain(ph, ks):
+        for k in ks:
+            for cp in stage(ph, k, slice(None), 0):
+                cp.wait_send()
+
+    def arrived(ph, k, q):
+        for cp in one(ph, k, q):
+            cp.wait_recv()
+
+    def when(t, lo):
+        return pl.when((t >= lo) & (t < lo + Q))
+
+    def reduce_steps(ph, t, finish):
+        @when(t, 1)
+        def _():
+            start(one(ph, 0, t - 1))
+
+        @when(t, 2)
+        def _():
+            u = t - 2
+            arrived(ph, 0, u)
+            r1[u] = r1[u] + part[u, pl.ds(8 * core, 8)]
+            start(one(ph, 1, u))
+
+        @when(t, 4)
+        def _():
+            u = t - 4
+            arrived(ph, 1, u)
+            r2[u, pl.ds(0, 2)] = r2[u, pl.ds(0, 2)] + r1[u, pl.ds(2 * cx, 2)]
+            r2[u, pl.ds(2, 2)] = r2[u, pl.ds(2, 2)] + r1[u, pl.ds(4 + 2 * cy, 2)]
+            start(one(ph, 2, u))
+
+        @when(t, 6)
+        def _():
+            u = t - 6
+            arrived(ph, 2, u)
+            finish(u, r3[u, 0] + r2[u, cy], r3[u, 1] + r2[u, 2 + cx])
+
+    def gather_steps(ph, t, finish):
+        @when(t, 0)
+        def _():
+            start(one(ph, 3, t))
+
+        @when(t, 2)
+        def _():
+            arrived(ph, 3, t - 2)
+            start(one(ph, 4, t - 2))
+
+        @when(t, 4)
+        def _():
+            arrived(ph, 4, t - 4)
+            start(one(ph, 5, t - 4))
+
+        @when(t, 5)
+        def _():
+            arrived(ph, 5, t - 5)
+            finish(t - 5)
+
+    for q in range(WO_SLOTS):
+        start(wo_copy(q))
+    barrier = pltpu.get_barrier_semaphore()
+    for dev in (sib, xn, yn):
+        pl.semaphore_signal(barrier, inc=1, device_id=dev, device_id_type=MESH)
+    pl.semaphore_wait(barrier, 3)
+
+    def finish_attn(u, a, b):
+        xres[u, 0] = (tok_ref[u, 0] + a).astype(jnp.bfloat16).astype(f32)
+        xres[u, 1] = (tok_ref[u, 1] + b).astype(jnp.bfloat16).astype(f32)
+
+    @pl.loop(0, Q + 6)
+    def _(t):
+        @when(t, 0)
+        def _():
+            wait(wo_copy(t))
+            part[t] = jnp.dot(x_ref[...], wo[lax.rem(t, WO_SLOTS)], preferred_element_type=f32).reshape(16, 8, width)
+
+            @pl.when(t + WO_SLOTS < Q)
+            def _():
+                start(wo_copy(t + WO_SLOTS))
+
+            @pl.when(t < GU_SLOTS)
+            def _():
+                start(gu_copy(t))
+
+            @pl.when((t >= GU_SLOTS) & (t < GU_SLOTS + WD_SLOTS))
+            def _():
+                start(wd_copy(t - GU_SLOTS))
+        reduce_steps(0, t, finish_attn)
+
+    drain(0, (0, 1, 2))
+    sq = jnp.zeros((2, 8, 1), f32)
+    for q in range(Q):
+        sq = sq + jnp.sum(xres[q] * xres[q], axis=-1, keepdims=True)
+    inv = lax.rsqrt(sq / (Q * width) + EPS)
+    blk_a, blk_b = core * 8 + 2 * cx + cy, core * 8 + 4 + 2 * cy + cx
+    for q in range(Q):
+        h = (xres[q] * inv * ln_ref[q]).astype(jnp.bfloat16).astype(f32)
+        full[q, blk_a] = h[0]
+        full[q, blk_b] = h[1]
+    acc_g[...] = jnp.zeros_like(acc_g)
+    acc_u[...] = jnp.zeros_like(acc_u)
+
+    def finish_gather(u):
+        wait(gu_copy(u))
+        s = lax.rem(u, GU_SLOTS)
+        h = full[u].reshape(rows, width).astype(jnp.bfloat16)
+        inner = acc_g.shape[1]
+        step = 512
+
+        @pl.loop(0, inner // step)
+        def _(n):
+            c = pl.ds(pl.multiple_of(n * step, step), step)
+            acc_g[:, c] += jnp.dot(h, wg[s, :, c], preferred_element_type=f32)
+            acc_u[:, c] += jnp.dot(h, wu[s, :, c], preferred_element_type=f32)
+        c = pl.ds(inner // step * step, inner % step)
+        acc_g[:, c] += jnp.dot(h, wg[s, :, c], preferred_element_type=f32)
+        acc_u[:, c] += jnp.dot(h, wu[s, :, c], preferred_element_type=f32)
+
+        @pl.when(u + GU_SLOTS < Q)
+        def _():
+            start(gu_copy(u + GU_SLOTS))
+
+    @pl.loop(0, Q + 5)
+    def _(t):
+        gather_steps(0, t, finish_gather)
+
+    drain(0, (3, 4, 5))
+
+    @pl.loop(0, acc_g.shape[1] // 640)
+    def _(n):
+        c = pl.ds(pl.multiple_of(n * 640, 640), 640)
+        mact[:, c] = (jax.nn.silu(acc_g[:, c]) * acc_u[:, c]).astype(jnp.bfloat16)
+
+    def finish_mlp(u, a, b):
+        full[u, blk_a] = (xres[u, 0] + a).astype(jnp.bfloat16).astype(f32)
+        full[u, blk_b] = (xres[u, 1] + b).astype(jnp.bfloat16).astype(f32)
+
+    @pl.loop(0, Q + 6)
+    def _(t):
+        @when(t, 0)
+        def _():
+            wait(wd_copy(t))
+            part[t] = jnp.dot(mact[...], wd[lax.rem(t, WD_SLOTS)], preferred_element_type=f32).reshape(16, 8, width)
+
+            @pl.when(t + WD_SLOTS < Q)
+            def _():
+                start(wd_copy(t + WD_SLOTS))
+        reduce_steps(1, t, finish_mlp)
+
+    def finish_out(u):
+        out_ref[:, cols(u)] = full[u].reshape(rows, width).astype(jnp.bfloat16)
+
+    @pl.loop(0, Q + 5)
+    def _(t):
+        gather_steps(1, t, finish_out)
+
+    drain(1, (0, 1, 2, 3, 4, 5))
+
+
+def tail(cid, attn_vals, tok_own, ln, w_out, w_gate, w_up, w_down):
+    rows, depth = attn_vals.shape
+    d_model, inner = w_gate.shape
+    width = d_model // Q
+    vmem = pl.BlockSpec(memory_space=pltpu.VMEM)
+    hbm = pl.BlockSpec(memory_space=pl.ANY)
+    f32, bf16 = jnp.float32, jnp.bfloat16
+    dma = pltpu.SemaphoreType.DMA
+    return pl.pallas_call(
+        tail_kernel,
+        out_shape=jax.ShapeDtypeStruct((rows, d_model), bf16),
+        in_specs=[vmem, vmem, vmem, hbm, hbm, hbm, hbm],
+        out_specs=vmem,
+        scratch_shapes=[
+            pltpu.VMEM((Q, 16, 8, width), f32),
+            pltpu.VMEM((Q, 8, 8, width), f32),
+            pltpu.VMEM((Q, 4, 8, width), f32),
+            pltpu.VMEM((Q, 2, 8, width), f32),
+            pltpu.VMEM((Q, 16, 8, width), f32),
+            pltpu.VMEM((Q, 2, 8, width), f32),
+            pltpu.VMEM((rows, inner), f32),
+            pltpu.VMEM((rows, inner), f32),
+            pltpu.VMEM((rows, inner), bf16),
+            pltpu.VMEM((WO_SLOTS, depth, width), bf16),
+            pltpu.VMEM((GU_SLOTS, width, inner), bf16),
+            pltpu.VMEM((GU_SLOTS, width, inner), bf16),
+            pltpu.VMEM((WD_SLOTS, inner, width), bf16),
+            dma((WO_SLOTS,)), dma((GU_SLOTS,)), dma((GU_SLOTS,)), dma((WD_SLOTS,)),
+            dma((2, 10)), dma((2, 10, Q)),
+        ],
+        compiler_params=pltpu.CompilerParams(collective_id=cid, has_side_effects=True, vmem_limit_bytes=62 * 1024 * 1024),
+        name="tail",
+    )(attn_vals, tok_own, ln, w_out, w_gate, w_up, w_down)
+
+
 def solution(mesh):
     dim_count = mesh.shape['dim']
     mlp_axes = ('heads', 'dim')
@@ -193,8 +455,7 @@
         up_blocks = (cache_len - LOW) // BLK
         dim_index = lax.axis_index('dim')
 
-        tok_f32 = tokens.astype(jnp.float32)
-        hidden = rms_scale(tok_f32, ln_attn).astype(jnp.bfloat16)
+        hidden = rms_scale(tokens.astype(jnp.float32), ln_attn).astype(jnp.bfloat16)
         q_part = jnp.einsum('bd,dhs->bhs', hidden, w_query, preferred_element_type=jnp.float32)
         k_part = jnp.einsum('bd,dhs->bhs', hidden, w_key, preferred_element_type=jnp.float32)
         v_new = jnp.einsum('bd,dhs->bhs', hidden, w_value, preferred_element_type=jnp.float32).astype(jnp.bfloat16)
@@ -241,14 +502,15 @@
         attn = lax.switch(which, branches, positions, off, idx, qd, qf, kf, vn, k_t, v_t)
         attn_vals = attn.reshape(rows, q_group, kv_local, slice_len).transpose(0, 2, 1, 3).reshape(rows, heads_local, slice_len)
 
-        attn_out = lax.psum(jnp.einsum('bhs,hsd->bd', attn_vals, w_out, preferred_element_type=jnp.float32), mlp_axes)
-        resid_f32 = (tok_f32 + attn_out).astype(jnp.bfloat16).astype(jnp.float32)
-        hidden2 = rms_scale(resid_f32, ln_mlp).astype(jnp.bfloat16)
-        gate_val = jnp.dot(hidden2, w_gate, preferred_element_type=jnp.float32)
-        up_val = jnp.dot(hidden2, w_up, preferred_element_type=jnp.float32)
-        mlp_act = (jax.nn.silu(gate_val) * up_val).astype(jnp.bfloat16)
-        mlp_out = lax.psum(jnp.dot(mlp_act, w_down, preferred_element_type=jnp.float32), mlp_axes)
-        return (resid_f32 + mlp_out).astype(jnp.bfloat16), k_new, v_new
+        attn_vals = attn_vals.reshape(rows, heads_local * slice_len)
+        heads_index = lax.axis_index('heads')
+        core, cx = heads_index % 2, heads_index // 2
+        tok_blocks = tokens.reshape(16, 8, Q, -1)
+        tok_own = jnp.stack([lax.dynamic_index_in_dim(tok_blocks, core * 8 + 2 * cx + dim_index, 0, keepdims=False),
+                             lax.dynamic_index_in_dim(tok_blocks, core * 8 + 4 + 2 * dim_index + cx, 0, keepdims=False)])
+        tok_own = tok_own.astype(jnp.float32).transpose(2, 0, 1, 3)
+        out = tail(len(UP_SIZES), attn_vals, tok_own, ln_mlp.reshape(Q, 1, -1), w_out.reshape(heads_local * slice_len, -1), w_gate, w_up, w_down)
+        return out, k_new, v_new
 
     row_spec = P('dp', None)
     head_spec = P(None, 'heads', 'dim')

time: 359 us -> 277 us (0.77)
  waiting for transfers between devices: 116 us -> 6.34 us
  Pallas kernels: 153 us -> 246 us
  matrix products: 56.2 us -> 8.79 us
  between operations: 15 us -> 1.62 us
  other arithmetic: 12 us -> 6.79 us
    psum x2 -> x0, waiting for transfers between devices: 108 us -> none  [the longest x1 54.5 us: layer_body(): lax.psum(jnp.einsum('bhs,hsd->bd', attn_vals, w_out, preferred_element_ty...]
    pallas_call x0 -> x1, Pallas kernels: none -> 90.8 us  [tail(): pl.pallas_call(tail_kernel, out_shape=jax.ShapeDtypeStruct((rows, d_model...]
    dot_general x3 -> x0, matrix products: 46.7 us -> none  [the longest x1 25.6 us: layer_body(): jnp.dot(mlp_act, w_down, preferred_element_type=jnp.float32)]
    ppermute x1, waiting for transfers between devices: 8.74 us -> 0.01 us  [layer_body(): other = lax.ppermute(own, 'dim', swap_perm)]
    ppermute x1, waiting for transfers between devices: 0.01 us -> 6.33 us  [layer_body(): gains_other = lax.ppermute(gains, 'dim', swap_perm)]
  transfers between devices with their start and end apart: 4 -> 2, of which waited for: 3 -> 1; matrix products, arithmetic and copies ran while one was open for 4% -> 2% of each run, Pallas kernels for 0% -> 0%
where the time goes in v2:
time: 277 us; the launch traced here: 279 us
  Pallas kernels  246 us (89%)
  matrix products  8.79 us (3%)
  other arithmetic  6.79 us (2%)
  waiting for transfers between devices  6.34 us (2%)
  local copies, waits for them, and re-layouts  5.87 us (2%)
  starting transfers between devices  3.41 us (1%)
    pallas_call x1, Pallas kernels, attend(): pl.pallas_call(functools.partial(attn_kernel, n_up, scale), out_shape=jax...  155 us
    pallas_call x1, Pallas kernels, tail(): pl.pallas_call(tail_kernel, out_shape=jax.ShapeDtypeStruct((rows, d_model...  90.8 us
    unnamed x3, matrix products  8.79 us
    ppermute x1, waiting for transfers between devices, layer_body(): gains_other = lax.ppermute(gains, 'dim', swap_perm)  6.33 us
  transfers between devices with their start and end apart: 2, of which 1 were waited for; matrix products, arithmetic and copies ran while one was open for 2% of the time, Pallas kernels for 0%

profile of v2, /device:TPU:0, one launch (start us, length us, event | category | flops | bytes accessed | tf_op | source)
XLA Modules:
  0.0 278.6 jit_solution(14901399789957186284)
XLA Ops:
  0.6 0.0 copy-start
  0.6 1.8 fusion
  2.4 0.0 copy-start.2
  2.4 0.0 copy-start.7
  2.4 6.2 %fusion.12 = f32[128,1024]{0,1:S(1)} fusion(bf16[5120,1024]{0,1:T(8,128)(2,1)} %bitcast.61, bf16[128,5120]{1,0:T(8,128)(2,1)} %param.20, f32[5120]{0:T(1024)} %param.21, f32[128]{0:T(128)S(1)} %add_rsqrt_fusion.1), kind=kOutput, calls=%fused_computation.47 | convolution fusion | flops 1344798720 | bytes 12341760
  8.7 0.0 copy-done
  8.7 0.0 copy-start.5
  8.7 0.0 copy-start.6
  8.7 0.0 copy-start.4
  8.7 0.0 copy-done.2
  8.7 0.0 copy-done.7
  8.7 0.6 fusion.10
  9.3 0.9 multiply_reduce_fusion.1
  10.2 3.4 %collective-permute-start = (f32[128,18,64]{0,2,1:T(8,128)}, f32[128,18,64]{0,2,1:T(8,128)S(1)}, u32[]{:S(2)}, u32[]{:S(2)}) collective-permute-start(f32[128,18,64]{0,2,1:T(8,128)} %get-tuple-element.231), channel_id=1, source_target_pairs={{0,4},{4,0},{1,5},{5,1},{2,6},{6,2},{3,7},{7,3}} | collective-permute-start | bytes 1769480 | tf_op jit(solution)/shard_map/ppermute | solution.py:464
  13.6 0.0 copy-done.5
  13.6 0.0 copy-done.6
  13.6 0.0 collective-permute-start.1
  13.7 0.0 copy-done.4
  13.7 0.1 copy.59
  13.8 0.2 reduce-window.4
  14.0 0.1 reduce
  14.1 0.2 convert_reduce_fusion
  14.3 0.2 select_reduce_fusion
  14.5 2.0 fusion.8
  16.5 0.6 bitcast_convert_fusion
  17.1 0.2 multiply_cosine_fusion
  17.4 0.5 slice.37
  17.9 0.8 convert_bitcast_fusion.tok_ref
  18.7 0.0 copy-done.8
  18.7 1.3 fusion.7
  20.6 6.3 %collective-permute-done.1 = f32[2,64]{1,0:T(2,128)S(1)} collective-permute-done((f32[2,64]{1,0:T(2,128)S(1)}, f32[2,64]{1,0:T(2,128)S(1)}, u32[]{:S(2)}, u32[]{:S(2)}) %collective-permute-start.1) | collective-permute-done | bytes 544 | tf_op jit(solution)/shard_map/ppermute | solution.py:466
  27.0 0.0 collective-permute-done
  27.0 0.1 multiply_reduce_fusion
  27.1 0.4 subtract_convert_fusion
  27.5 0.0 copy-start.3
  27.6 0.1 fusion.5
  27.7 0.4 copy-done.3
  28.1 156.0 %conditional.1 = (bf16[128,8,128]{2,1,0:T(8,128)(2,1)S(1)}) conditional(s32[]{:T(128)} %clamp.3, (s32[128]{0:T(128)S(1)}, s32[128]{0:T(128)S(1)}, s32[512]{0:T(512)S(1)}, bf16[128,16,128]{0,2,1:T(8,128)(2,1)S(1)}, bf16[128,16,128]{0,2,1:T(8,128)(2,1)S(1)}, /*index=5*/f32[128,2,128]{0,2,1:T(8,128)S(1)}, ...), branch_computations={%region_7.8_spmd, %region_8.9_spmd, %region_9.10_spmd, %region_10.... | conditional | bytes 2490376 | solution.py:502
  28.1 0.4 copy.64.qd_ref
  28.6 0.4 copy.65.qf_ref
  29.0 0.1 copy.66.kf_ref
  29.1 0.1 copy.67.vn_ref
  29.2 154.7 %attend_336.1 = bf16[128,8,128]{2,1,0:T(8,128)(2,1)S(1)} custom-call(s32[128]{0:T(128)S(1)} %get-tuple-element.86.pos_ref, s32[128]{0:T(128)S(1)} %get-tuple-element.87.off_ref, s32[512]{0:T(512)S(1)} %get-tuple-element.88.idx_ref, bf16[128,16,128]{2,1,0:T(8,128)(2,1)S(1)} %copy.64.qd_ref, bf16[128,16,128]{2,1,0:T(8,128)(2,1)S(1)} %copy.65.qf_ref, ...), custom_call_target="tpu_custom_call" | custom-call | tf_op jit(solution)/shard_map/cond/branch_1_fun/attend_336/pallas_call | solution.py:154
  184.2 0.2 copy.76
  184.4 0.9 copy.80.x_ref
  185.3 90.8 %tail.1 = bf16[128,5120]{1,0:T(8,128)(2,1)} custom-call(bf16[128,1024]{1,0:T(8,128)(2,1)} %copy.80.x_ref, f32[10,2,8,512]{3,2,1,0:T(8,128)} %convert_bitcast_fusion.tok_ref, f32[10,1,512]{2,1,0:T(1,128)} %bitcast.57, bf16[1024,5120]{1,0:T(8,128)(2,1)} %bitcast.48, bf16[5120,3200]{1,0:T(8,128)(2,1)} %wg_hbm.1, bf16[5120,3200]{1,0:T(8,128)(2,1)} %wu_hbm.1, ...), custom_call_target="tpu_custom_call" | custom-call | tf_op jit(solution)/shard_map/tail/pallas_call | solution.py:414
  276.1 2.5 copy.88
  278.6 0.0 copy-done.1
  (24 shorter events, 0.2 us)
Async XLA Ops:
  0.6 8.0 %copy-start = (bf16[5120,2,64]{0,2,1:T(8,128)(2,1)S(1)}, bf16[5120,2,64]{0,2,1:T(8,128)(2,1)}, u32[]{:S(2)}) copy-start(bf16[5120,2,64]{0,2,1:T(8,128)(2,1)} %param.23) | copy-start | bytes 3932164
  2.4 6.3 %copy-start.2 = (bf16[128,5120]{1,0:T(8,128)(2,1)S(1)}, bf16[128,5120]{1,0:T(8,128)(2,1)}, u32[]{:S(2)}) copy-start(bf16[128,5120]{1,0:T(8,128)(2,1)} %param.20) | copy-start | bytes 3932164
  2.4 6.3 %copy-start.7 = (f32[5120]{0:T(1024)S(1)}, f32[5120]{0:T(1024)}, u32[]{:S(2)}) copy-start(f32[5120]{0:T(1024)} %param.21) | copy-start | bytes 61444
  8.7 4.9 %copy-start.5 = (f32[64]{0:T(128)S(1)}, f32[64]{0:T(128)}, u32[]{:S(2)}) copy-start(f32[64]{0:T(128)} %param.25) | copy-start | bytes 772
  8.7 4.9 %copy-start.6 = (f32[64]{0:T(128)S(1)}, f32[64]{0:T(128)}, u32[]{:S(2)}) copy-start(f32[64]{0:T(128)} %param.26) | copy-start | bytes 772
  8.7 5.0 %copy-start.4 = (s32[128]{0:T(128)S(1)}, s32[128]{0:T(128)}, u32[]{:S(2)}) copy-start(s32[128]{0:T(128)} %param.34) | copy-start | bytes 1540
  10.2 8.5 %copy-start.8 = (s32[3]{0:T(128)S(1)}, s32[3]{0:T(128)}, u32[]{:S(2)}) copy-start(s32[3]{0:T(128)} %constant.100.clone) | copy-start | bytes 40
  10.2 16.8 %collective-permute-start = (f32[128,18,64]{0,2,1:T(8,128)}, f32[128,18,64]{0,2,1:T(8,128)S(1)}, u32[]{:S(2)}, u32[]{:S(2)}) collective-permute-start(f32[128,18,64]{0,2,1:T(8,128)} %get-tuple-element.231), channel_id=1, source_target_pairs={{0,4},{4,0},{1,5},{5,1},{2,6},{6,2},{3,7},{7,3}} | collective-permute-start | bytes 1769480 | tf_op jit(solution)/shard_map/ppermute | solution.py:464
  13.6 13.3 %collective-permute-start.1 = (f32[2,64]{1,0:T(2,128)S(1)}, f32[2,64]{1,0:T(2,128)S(1)}, u32[]{:S(2)}, u32[]{:S(2)}) collective-permute-start(f32[2,64]{1,0:T(2,128)S(1)} %pad_maximum_fusion.4), channel_id=1, source_target_pairs={{0,4},{4,0},{1,5},{5,1},{2,6},{6,2},{3,7},{7,3}} | collective-permute-start | bytes 1544 | tf_op jit(solution)/shard_map/ppermute | solution.py:466
  27.5 0.6 copy-start.3
  185.3 93.3 %copy-start.1 = (bf16[5120,2,64]{0,2,1:T(8,128)(2,1)S(1)}, bf16[5120,2,64]{0,2,1:T(8,128)(2,1)}, u32[]{:S(2)}) copy-start(bf16[5120,2,64]{0,2,1:T(8,128)(2,1)} %param.23) | copy-start | bytes 3932164

commit v3 on v2

--- a/solution.py
+++ b/solution.py
@@ -308,6 +308,8 @@
     for dev in (sib, xn, yn):
         pl.semaphore_signal(barrier, inc=1, device_id=dev, device_id_type=MESH)
     pl.semaphore_wait(barrier, 3)
+    acc_g[...] = jnp.zeros_like(acc_g)
+    acc_u[...] = jnp.zeros_like(acc_u)
 
     def finish_attn(u, a, b):
         xres[u, 0] = (tok_ref[u, 0] + a).astype(jnp.bfloat16).astype(f32)
@@ -343,24 +345,13 @@
         h = (xres[q] * inv * ln_ref[q]).astype(jnp.bfloat16).astype(f32)
         full[q, blk_a] = h[0]
         full[q, blk_b] = h[1]
-    acc_g[...] = jnp.zeros_like(acc_g)
-    acc_u[...] = jnp.zeros_like(acc_u)
 
     def finish_gather(u):
         wait(gu_copy(u))
         s = lax.rem(u, GU_SLOTS)
         h = full[u].reshape(rows, width).astype(jnp.bfloat16)
-        inner = acc_g.shape[1]
-        step = 512
-
-        @pl.loop(0, inner // step)
-        def _(n):
-            c = pl.ds(pl.multiple_of(n * step, step), step)
-            acc_g[:, c] += jnp.dot(h, wg[s, :, c], preferred_element_type=f32)
-            acc_u[:, c] += jnp.dot(h, wu[s, :, c], preferred_element_type=f32)
-        c = pl.ds(inner // step * step, inner % step)
-        acc_g[:, c] += jnp.dot(h, wg[s, :, c], preferred_element_type=f32)
-        acc_u[:, c] += jnp.dot(h, wu[s, :, c], preferred_element_type=f32)
+        acc_g[...] += jnp.dot(h, wg[s], preferred_element_type=f32)
+        acc_u[...] += jnp.dot(h, wu[s], preferred_element_type=f32)
 
         @pl.when(u + GU_SLOTS < Q)
         def _():
@@ -381,7 +372,10 @@
         full[u, blk_a] = (xres[u, 0] + a).astype(jnp.bfloat16).astype(f32)
         full[u, blk_b] = (xres[u, 1] + b).astype(jnp.bfloat16).astype(f32)
 
-    @pl.loop(0, Q + 6)
+    def finish_out(u):
+        out_ref[:, cols(u)] = full[u].reshape(rows, width).astype(jnp.bfloat16)
+
+    @pl.loop(0, Q + 12)
     def _(t):
         @when(t, 0)
         def _():
@@ -392,13 +386,7 @@
             def _():
                 start(wd_copy(t + WD_SLOTS))
         reduce_steps(1, t, finish_mlp)
-
-    def finish_out(u):
-        out_ref[:, cols(u)] = full[u].reshape(rows, width).astype(jnp.bfloat16)
-
-    @pl.loop(0, Q + 5)
-    def _(t):
-        gather_steps(1, t, finish_out)
+        gather_steps(1, t - 7, finish_out)
 
     drain(1, (0, 1, 2, 3, 4, 5))
 

time: 277 us -> 264 us (0.953); the launches traced: 279 us -> 262 us
  Pallas kernels: 246 us -> 229 us
    pallas_call x1, Pallas kernels: 90.8 us -> 77.2 us  [tail(): pl.pallas_call(tail_kernel, out_shape=jax.ShapeDtypeStruct((rows, d_model...]
    pallas_call x1, Pallas kernels: 155 us -> 152 us  [attend(): pl.pallas_call(functools.partial(attn_kernel, n_up, scale), out_shape=jax...]
where the time goes in v3:
time: 264 us; the launch traced here: 262 us
  Pallas kernels  229 us (87%)
  matrix products  8.79 us (3%)
  other arithmetic  6.79 us (3%)
  waiting for transfers between devices  6.34 us (2%)
  local copies, waits for them, and re-layouts  5.87 us (2%)
  starting transfers between devices  3.41 us (1%)
    pallas_call x1, Pallas kernels, attend(): pl.pallas_call(functools.partial(attn_kernel, n_up, scale), out_shape=jax...  152 us
    pallas_call x1, Pallas kernels, tail(): pl.pallas_call(tail_kernel, out_shape=jax.ShapeDtypeStruct((rows, d_model...  77.2 us
    unnamed x3, matrix products  8.79 us
    ppermute x1, waiting for transfers between devices, layer_body(): gains_other = lax.ppermute(gains, 'dim', swap_perm)  6.33 us
  transfers between devices with their start and end apart: 2, of which 1 were waited for; matrix products, arithmetic and copies ran while one was open for 2% of the time, Pallas kernels for 0%

profile of v3, /device:TPU:0, one launch (start us, length us, event | category | flops | bytes accessed | tf_op | source)
XLA Modules:
  0.0 262.2 jit_solution(4246290340497152727)
XLA Ops:
  0.6 0.0 copy-start
  0.6 1.8 fusion
  2.4 0.0 copy-start.2
  2.4 0.0 copy-start.7
  2.4 6.2 %fusion.12 = f32[128,1024]{0,1:S(1)} fusion(bf16[5120,1024]{0,1:T(8,128)(2,1)} %bitcast.61, bf16[128,5120]{1,0:T(8,128)(2,1)} %param.20, f32[5120]{0:T(1024)} %param.21, f32[128]{0:T(128)S(1)} %add_rsqrt_fusion.1), kind=kOutput, calls=%fused_computation.47 | convolution fusion | flops 1344798720 | bytes 12341760
  8.7 0.0 copy-done
  8.7 0.0 copy-start.5
  8.7 0.0 copy-start.6
  8.7 0.0 copy-start.4
  8.7 0.0 copy-done.2
  8.7 0.0 copy-done.7
  8.7 0.6 fusion.10
  9.3 0.9 multiply_reduce_fusion.1
  10.2 3.4 %collective-permute-start = (f32[128,18,64]{0,2,1:T(8,128)}, f32[128,18,64]{0,2,1:T(8,128)S(1)}, u32[]{:S(2)}, u32[]{:S(2)}) collective-permute-start(f32[128,18,64]{0,2,1:T(8,128)} %get-tuple-element.231), channel_id=1, source_target_pairs={{0,4},{4,0},{1,5},{5,1},{2,6},{6,2},{3,7},{7,3}} | collective-permute-start | bytes 1769480 | tf_op jit(solution)/shard_map/ppermute | solution.py:452
  13.6 0.0 copy-done.5
  13.6 0.0 copy-done.6
  13.6 0.0 collective-permute-start.1
  13.7 0.0 copy-done.4
  13.7 0.1 copy.59
  13.8 0.2 reduce-window.4
  14.0 0.1 reduce
  14.1 0.2 convert_reduce_fusion
  14.3 0.2 select_reduce_fusion
  14.5 2.0 fusion.8
  16.5 0.6 bitcast_convert_fusion
  17.1 0.2 multiply_cosine_fusion
  17.4 0.5 slice.37
  17.9 0.8 convert_bitcast_fusion.tok_ref
  18.7 0.0 copy-done.8
  18.7 1.3 fusion.7
  20.6 6.3 %collective-permute-done.1 = f32[2,64]{1,0:T(2,128)S(1)} collective-permute-done((f32[2,64]{1,0:T(2,128)S(1)}, f32[2,64]{1,0:T(2,128)S(1)}, u32[]{:S(2)}, u32[]{:S(2)}) %collective-permute-start.1) | collective-permute-done | bytes 544 | tf_op jit(solution)/shard_map/ppermute | solution.py:454
  27.0 0.0 collective-permute-done
  27.0 0.1 multiply_reduce_fusion
  27.1 0.4 subtract_convert_fusion
  27.5 0.0 copy-start.3
  27.6 0.1 fusion.5
  27.7 0.4 copy-done.3
  28.1 153.2 %conditional.1 = (bf16[128,8,128]{2,1,0:T(8,128)(2,1)S(1)}) conditional(s32[]{:T(128)} %clamp.3, (s32[128]{0:T(128)S(1)}, s32[128]{0:T(128)S(1)}, s32[512]{0:T(512)S(1)}, bf16[128,16,128]{0,2,1:T(8,128)(2,1)S(1)}, bf16[128,16,128]{0,2,1:T(8,128)(2,1)S(1)}, /*index=5*/f32[128,2,128]{0,2,1:T(8,128)S(1)}, ...), branch_computations={%region_7.8_spmd, %region_8.9_spmd, %region_9.10_spmd, %region_10.... | conditional | bytes 2490376 | solution.py:490
  28.1 0.4 copy.60.qd_ref
  28.6 0.4 copy.61.qf_ref
  29.0 0.1 copy.62.kf_ref
  29.1 0.1 copy.63.vn_ref
  29.2 151.9 %attend_320.1 = bf16[128,8,128]{2,1,0:T(8,128)(2,1)S(1)} custom-call(s32[128]{0:T(128)S(1)} %get-tuple-element.60.pos_ref, s32[128]{0:T(128)S(1)} %get-tuple-element.61.off_ref, s32[512]{0:T(512)S(1)} %get-tuple-element.62.idx_ref, bf16[128,16,128]{2,1,0:T(8,128)(2,1)S(1)} %copy.60.qd_ref, bf16[128,16,128]{2,1,0:T(8,128)(2,1)S(1)} %copy.61.qf_ref, ...), custom_call_target="tpu_custom_call" | custom-call | tf_op jit(solution)/shard_map/cond/branch_0_fun/attend_320/pallas_call | solution.py:154
  181.3 0.2 copy.76
  181.6 0.9 copy.80.x_ref
  182.5 77.2 %tail.1 = bf16[128,5120]{1,0:T(8,128)(2,1)} custom-call(bf16[128,1024]{1,0:T(8,128)(2,1)} %copy.80.x_ref, f32[10,2,8,512]{3,2,1,0:T(8,128)} %convert_bitcast_fusion.tok_ref, f32[10,1,512]{2,1,0:T(1,128)} %bitcast.57, bf16[1024,5120]{1,0:T(8,128)(2,1)} %bitcast.48, bf16[5120,3200]{1,0:T(8,128)(2,1)} %wg_hbm.1, bf16[5120,3200]{1,0:T(8,128)(2,1)} %wu_hbm.1, ...), custom_call_target="tpu_custom_call" | custom-call | tf_op jit(solution)/shard_map/tail/pallas_call | solution.py:402
  259.7 2.5 copy.88
  262.2 0.0 copy-done.1
  (24 shorter events, 0.2 us)
Async XLA Ops:
  0.6 8.0 %copy-start = (bf16[5120,2,64]{0,2,1:T(8,128)(2,1)S(1)}, bf16[5120,2,64]{0,2,1:T(8,128)(2,1)}, u32[]{:S(2)}) copy-start(bf16[5120,2,64]{0,2,1:T(8,128)(2,1)} %param.23) | copy-start | bytes 3932164
  2.4 6.3 %copy-start.2 = (bf16[128,5120]{1,0:T(8,128)(2,1)S(1)}, bf16[128,5120]{1,0:T(8,128)(2,1)}, u32[]{:S(2)}) copy-start(bf16[128,5120]{1,0:T(8,128)(2,1)} %param.20) | copy-start | bytes 3932164
  2.4 6.3 %copy-start.7 = (f32[5120]{0:T(1024)S(1)}, f32[5120]{0:T(1024)}, u32[]{:S(2)}) copy-start(f32[5120]{0:T(1024)} %param.21) | copy-start | bytes 61444
  8.7 4.9 %copy-start.5 = (f32[64]{0:T(128)S(1)}, f32[64]{0:T(128)}, u32[]{:S(2)}) copy-start(f32[64]{0:T(128)} %param.25) | copy-start | bytes 772
  8.7 4.9 %copy-start.6 = (f32[64]{0:T(128)S(1)}, f32[64]{0:T(128)}, u32[]{:S(2)}) copy-start(f32[64]{0:T(128)} %param.26) | copy-start | bytes 772
  8.7 5.0 %copy-start.4 = (s32[128]{0:T(128)S(1)}, s32[128]{0:T(128)}, u32[]{:S(2)}) copy-start(s32[128]{0:T(128)} %param.34) | copy-start | bytes 1540
  10.2 8.5 %copy-start.8 = (s32[3]{0:T(128)S(1)}, s32[3]{0:T(128)}, u32[]{:S(2)}) copy-start(s32[3]{0:T(128)} %constant.100.clone) | copy-start | bytes 40
  10.2 16.8 %collective-permute-start = (f32[128,18,64]{0,2,1:T(8,128)}, f32[128,18,64]{0,2,1:T(8,128)S(1)}, u32[]{:S(2)}, u32[]{:S(2)}) collective-permute-start(f32[128,18,64]{0,2,1:T(8,128)} %get-tuple-element.231), channel_id=1, source_target_pairs={{0,4},{4,0},{1,5},{5,1},{2,6},{6,2},{3,7},{7,3}} | collective-permute-start | bytes 1769480 | tf_op jit(solution)/shard_map/ppermute | solution.py:452
  13.6 13.3 %collective-permute-start.1 = (f32[2,64]{1,0:T(2,128)S(1)}, f32[2,64]{1,0:T(2,128)S(1)}, u32[]{:S(2)}, u32[]{:S(2)}) collective-permute-start(f32[2,64]{1,0:T(2,128)S(1)} %pad_maximum_fusion.4), channel_id=1, source_target_pairs={{0,4},{4,0},{1,5},{5,1},{2,6},{6,2},{3,7},{7,3}} | collective-permute-start | bytes 1544 | tf_op jit(solution)/shard_map/ppermute | solution.py:454
  27.5 0.6 copy-start.3
  182.5 79.7 %copy-start.1 = (bf16[5120,2,64]{0,2,1:T(8,128)(2,1)S(1)}, bf16[5120,2,64]{0,2,1:T(8,128)(2,1)}, u32[]{:S(2)}) copy-start(bf16[5120,2,64]{0,2,1:T(8,128)(2,1)} %param.23) | copy-start | bytes 3932164

commit v4 on v3

--- a/solution.py
+++ b/solution.py
@@ -14,25 +14,155 @@
 BLK = 128
 LOW = 512
 CH = 4
-UCH = 16
+UCH = 8
+UNIT = 32
 SLOTS = 4
 FIRST = 8
 LEAD = 4
-UP_SIZES = (320, 336, 352, 512)
-
-
-def rms_scale(values, gain):
-    mean_sq = jnp.mean(values * values, axis=-1, keepdims=True)
-    return values * lax.rsqrt(mean_sq + EPS) * gain
-
-
-def attn_kernel(n_up, scale, pos_ref, off_ref, idx_ref, qd_ref, qf_ref, kf_ref, vn_ref, k_hbm, v_hbm, o_ref,
+UP_SIZES = (240, 256, 264, 272, 280, 288, 304, 512)
+
+
+def qkv_kernel(group, tok_ref, ln_ref, cos_ref, sin_ref, gain_ref, wq_hbm, wk_hbm, wv_hbm, qd_ref, sn_ref, vn_ref, kn_ref,
+               hid, wq, wk, wv, own, other, gain_other, wsem, snd, rcv):
+    partner = {"dim": 1 - lax.axis_index("dim")}
+    rows, depth = tok_ref.shape
+    n_q = own.shape[0] - 1
+    steps = n_q // 2
+    f32, bf16 = jnp.float32, jnp.bfloat16
+    half = BLK // 2
+    per_step = wq.shape[0] // steps
+
+    def wq_copy(c):
+        part = pl.ds(pl.multiple_of(c * per_step, per_step), per_step)
+        return pltpu.make_async_copy(wq_hbm.at[part], wq.at[part], wsem.at[c])
+
+    k_load = pltpu.make_async_copy(wk_hbm, wk, wsem.at[steps])
+    v_load = pltpu.make_async_copy(wv_hbm, wv, wsem.at[steps + 1])
+
+    def remote(src, dst, i):
+        return pltpu.make_async_remote_copy(src_ref=src, dst_ref=dst, send_sem=snd.at[i], recv_sem=rcv.at[i],
+                                            device_id=partner, device_id_type=MESH)
+
+    def q_copy(c):
+        part = pl.ds(2 * c, 2)
+        return remote(own.at[part], other.at[part], c)
+
+    k_copy = remote(own.at[pl.ds(n_q, 1)], other.at[pl.ds(n_q, 1)], steps)
+    g_copy = remote(gain_ref, gain_other, steps + 1)
+
+    k_load.start()
+    for c in range(steps):
+        wq_copy(c).start()
+    v_load.start()
+    barrier = pltpu.get_barrier_semaphore()
+    pl.semaphore_signal(barrier, inc=1, device_id=partner, device_id_type=MESH)
+    pl.semaphore_wait(barrier, 1)
+    g_copy.start()
+
+    @pl.loop(0, rows // 16)
+    def _(i):
+        part = pl.ds(pl.multiple_of(i * 16, 16), 16)
+        x = tok_ref[part, :].astype(f32)
+        inv = lax.rsqrt(jnp.mean(x * x, axis=-1, keepdims=True) + EPS)
+        hid[part, :] = (x * inv * ln_ref[...]).astype(bf16)
+
+    def project(w):
+        return lax.dot_general(hid[...], w, (((1,), (1,)), ((), ())), preferred_element_type=f32)
+
+    k_load.wait()
+    own[n_q] = project(wk[...])
+
+    @pl.loop(0, steps)
+    def _(c):
+        wq_copy(c).wait()
+        u = project(wq[pl.ds(pl.multiple_of(c * per_step, per_step), per_step), :])
+
+        @pl.when(c == 0)
+        def _():
+            k_copy.start()
+
+        own[2 * c] = u[:, :BLK]
+        own[2 * c + 1] = u[:, BLK:]
+        q_copy(c).start()
+
+    v_load.wait()
+    vn_ref[...] = project(wv[...]).astype(bf16).astype(f32)
+    low = lax.broadcasted_iota(jnp.int32, (rows, BLK), 1) < half
+    cos_t, sin_t = cos_ref[...], sin_ref[...]
+
+    def halves(x):
+        return (jnp.sum(jnp.where(low, x, 0.0), axis=-1, keepdims=True), jnp.sum(jnp.where(low, 0.0, x), axis=-1, keepdims=True))
+
+    def rotate(i, g):
+        a, b = own[i], other[i]
+        s_lo, s_hi = halves(a * a + b * b)
+        inv = jnp.where(low, lax.rsqrt(s_lo / BLK + EPS), lax.rsqrt(s_hi / BLK + EPS))
+        a, b = a * inv * gain_ref[g:g + 1, :], b * inv * gain_other[g:g + 1, :]
+        return (a * cos_t + b * sin_t).astype(bf16).astype(f32), (b * cos_t - a * sin_t).astype(bf16).astype(f32)
+
+    g_copy.wait_recv()
+    k_copy.wait_recv()
+    k_own, k_oth = rotate(n_q, 1)
+    kn_ref[...] = k_own.astype(bf16)
+    kr_own, kr_oth = pltpu.roll(k_own, half, 1), pltpu.roll(k_oth, half, 1)
+    kk = [(jnp.where(low, k_own, kr_own), jnp.where(low, k_oth, kr_oth)),
+          (jnp.where(low, kr_own, k_own), jnp.where(low, kr_oth, k_oth))]
+    for i in range(n_q):
+        if i % 2 == 0:
+            q_copy(i // 2).wait_recv()
+        q_own, q_oth = rotate(i, 0)
+        kv = 2 * i // group
+        new = halves(q_own * kk[kv][0] + q_oth * kk[kv][1])
+        turned = pltpu.roll(q_own, half, 1)
+        for e in range(2):
+            sn_ref[:, 2 * i + e, :] = jnp.broadcast_to(new[e], (rows, BLK))
+            val = q_own if e == kv else turned
+            qd_ref[:, 2 * i + e, :] = jnp.where(low, val, 0.0) if kv == 0 else jnp.where(low, 0.0, val)
+    for c in range(steps):
+        q_copy(c).wait_send()
+    k_copy.wait_send()
+    g_copy.wait_send()
+
+
+def qkv(cid, group, tokens, ln, cos_t, sin_t, gain, w_q, w_k, w_v):
+    rows, depth = tokens.shape
+    n_q = w_q.shape[0] // BLK
+    steps = n_q // 2
+    vmem = pl.BlockSpec(memory_space=pltpu.VMEM)
+    hbm = pl.BlockSpec(memory_space=pl.ANY)
+    f32, bf16 = jnp.float32, jnp.bfloat16
+    heads = 2 * n_q
+    dma = pltpu.SemaphoreType.DMA
+    return pl.pallas_call(
+        functools.partial(qkv_kernel, group),
+        out_shape=(jax.ShapeDtypeStruct((rows, heads, BLK), f32), jax.ShapeDtypeStruct((rows, heads, BLK), f32),
+                   jax.ShapeDtypeStruct((rows, BLK), f32), jax.ShapeDtypeStruct((rows, BLK), bf16)),
+        in_specs=[vmem] * 5 + [hbm] * 3,
+        out_specs=(vmem,) * 4,
+        scratch_shapes=[
+            pltpu.VMEM((rows, depth), bf16),
+            pltpu.VMEM(w_q.shape, bf16),
+            pltpu.VMEM(w_k.shape, bf16),
+            pltpu.VMEM(w_v.shape, bf16),
+            pltpu.VMEM((n_q + 1, rows, BLK), f32),
+            pltpu.VMEM((n_q + 1, rows, BLK), f32),
+            pltpu.VMEM(gain.shape, f32),
+            dma((steps + 2,)), dma((steps + 2,)), dma((steps + 2,)),
+        ],
+        compiler_params=pltpu.CompilerParams(collective_id=cid, has_side_effects=True, vmem_limit_bytes=32 * 1024 * 1024),
+        name="qkv",
+    )(tokens, ln, cos_t, sin_t, gain, w_q, w_k, w_v)
+
+
+def attn_kernel(n_up, scale, pos_ref, off_ref, idx_ref, qd_ref, sn_ref, vn_ref, k_hbm, v_hbm, o_ref,
                 kbuf, vbuf, own_lo, own_up, pack, rlo, rup, ksem, vsem, slo_s, slo_r, sup_s, sup_r):
     partner = {"dim": 1 - lax.axis_index("dim")}
     rows = qd_ref.shape[0]
     n_ch = rows // CH
     n_uch = n_up // UCH
     up_blocks = own_up.shape[0] // rows
+    per_blk = BLK // UNIT
+    lane_up = lax.broadcasted_iota(jnp.int32, (16, BLK), 1)
 
     def kcopy(c):
         return pltpu.make_async_copy(k_hbm.at[pl.ds(c * CH, CH)], kbuf.at[lax.rem(c, SLOTS)], ksem.at[lax.rem(c, SLOTS)])
@@ -63,7 +193,7 @@
         kcopy(c).wait()
         for r in range(CH):
             b = c * CH + r
-            s = jnp.dot(qd_ref[b], kbuf[lax.rem(c, SLOTS), r], preferred_element_type=jnp.float32)
+            s = jnp.dot(qd_ref[b].astype(jnp.bfloat16), kbuf[lax.rem(c, SLOTS), r], preferred_element_type=jnp.float32)
             own_lo[b] = s[:, :LOW]
             for j in range(up_blocks):
                 own_up[b * up_blocks + j] = s[:, LOW + j * BLK:LOW + (j + 1) * BLK]
@@ -82,7 +212,12 @@
         def _():
             for r in range(UCH):
                 j = c * UCH + r
-                pack[j] = own_up[idx_ref[j]]
+                block = None
+                for k in range(per_blk):
+                    src = idx_ref[j * per_blk + k]
+                    piece = pltpu.roll(own_up[src // per_blk], (k + per_blk - src % per_blk) % per_blk * UNIT, 1)
+                    block = piece if k == 0 else jnp.where(lane_up >= k * UNIT, piece, block)
+                pack[j] = block
 
         @pl.when(c >= 1)
         def _():
@@ -97,7 +232,7 @@
         up_copy(c).wait_recv()
 
     lane = lax.broadcasted_iota(jnp.int32, (8, 2 * 64), 1)
-    t_up = lax.broadcasted_iota(jnp.int32, (16, BLK), 1) + LOW
+    t_up = lane_up + LOW
 
     @pl.loop(0, n_ch)
     def _(c):
@@ -112,13 +247,14 @@
             pos = pos_ref[b]
             off = off_ref[b]
             parts = [(own_lo[b] + rlo[b]) * scale]
+            skew = off % per_blk * UNIT
+            slots = [pltpu.roll(rup[jnp.minimum(off // per_blk + j, n_up - 1)], (BLK - skew) % BLK, 1) for j in range(up_blocks + 1)]
             for j in range(up_blocks):
-                total = (own_up[b * up_blocks + j] + rup[jnp.minimum(off + j, n_up - 1)]) * scale
+                got = jnp.where(lane_up < BLK - skew, slots[j], slots[j + 1])
+                total = (own_up[b * up_blocks + j] + got) * scale
                 parts.append(jnp.where(t_up + j * BLK < pos, total, -jnp.inf))
             s = jnp.concatenate(parts, axis=1)
-            kf = kf_ref[b]
-            k_rows = jnp.concatenate([jnp.broadcast_to(kf[0:1], (8, 128)), jnp.broadcast_to(kf[1:2], (8, 128))], axis=0)
-            s_new = jnp.sum(qf_ref[b].astype(jnp.float32) * k_rows, axis=1, keepdims=True) * scale
+            s_new = sn_ref[b][:, 0:1] * scale
             m = jnp.maximum(jnp.max(s, axis=1, keepdims=True), s_new)
             e = jnp.exp(s - m)
             e_new = jnp.exp(s_new - m)
@@ -142,7 +278,7 @@
         up_copy(c).wait_send()
 
 
-def attend(n_up, cid, scale, pos, off, idx, qd, qf, kf, vn, k_t, v_t):
+def attend(n_up, cid, scale, pos, off, idx, qd, sn, vn, k_t, v_t):
     rows = qd.shape[0]
     n_ch = rows // CH
     n_uch = n_up // UCH
@@ -154,7 +290,7 @@
     return pl.pallas_call(
         functools.partial(attn_kernel, n_up, scale),
         out_shape=jax.ShapeDtypeStruct((rows, 8, 128), jnp.bfloat16),
-        in_specs=[smem, smem, smem, vmem, vmem, vmem, vmem, hbm, hbm],
+        in_specs=[smem, smem, smem, vmem, vmem, vmem, hbm, hbm],
         out_specs=vmem,
         scratch_shapes=[
             pltpu.VMEM((SLOTS, CH, 128, cache_len), jnp.bfloat16),
@@ -173,7 +309,7 @@
         ],
         compiler_params=pltpu.CompilerParams(collective_id=cid, has_side_effects=True, vmem_limit_bytes=40 * 1024 * 1024),
         name=f"attend_{n_up}",
-    )(pos, off, idx, qd, qf, kf, vn, k_t, v_t)
+    )(pos, off, idx, qd, sn, vn, k_t, v_t)
 
 
 Q = 10
@@ -429,7 +565,6 @@
 def solution(mesh):
     dim_count = mesh.shape['dim']
     mlp_axes = ('heads', 'dim')
-    swap_perm = [(src, (src + dim_count // 2) % dim_count) for src in range(dim_count)]
 
     def layer_body(tokens, ln_attn, w_query, w_key, w_value, q_gain, k_gain, w_out, ln_mlp, w_gate, w_up, w_down, k_cache, v_cache, positions):
         rows = tokens.shape[0]
@@ -443,51 +578,34 @@
         up_blocks = (cache_len - LOW) // BLK
         dim_index = lax.axis_index('dim')
 
-        hidden = rms_scale(tokens.astype(jnp.float32), ln_attn).astype(jnp.bfloat16)
-        q_part = jnp.einsum('bd,dhs->bhs', hidden, w_query, preferred_element_type=jnp.float32)
-        k_part = jnp.einsum('bd,dhs->bhs', hidden, w_key, preferred_element_type=jnp.float32)
-        v_new = jnp.einsum('bd,dhs->bhs', hidden, w_value, preferred_element_type=jnp.float32).astype(jnp.bfloat16)
-
-        own = jnp.concatenate([q_part, k_part], axis=1)
-        other = lax.ppermute(own, 'dim', swap_perm)
-        gains = jnp.stack([q_gain, k_gain])
-        gains_other = lax.ppermute(gains, 'dim', swap_perm)
-        sq_total = jnp.sum(own * own, axis=-1, keepdims=True) + jnp.sum(other * other, axis=-1, keepdims=True)
-        inv = lax.rsqrt(sq_total / head_dim + EPS)
-
-        def spread(pair):
-            return jnp.concatenate([jnp.broadcast_to(pair[0], (heads_local, slice_len)), jnp.broadcast_to(pair[1], (kv_local, slice_len))], axis=0)
-
-        u_own = own * inv * spread(gains)
-        u_other = other * inv * spread(gains_other)
         inv_freq = ROPE_BASE ** (-jnp.arange(half_dim, dtype=jnp.float32) * 2.0 / head_dim)
-        rot_angle = positions.astype(jnp.float32)[:, None, None] * inv_freq
+        rot_angle = positions.astype(jnp.float32)[:, None] * jnp.tile(inv_freq, 2)
         cos_t = jnp.cos(rot_angle)
         sin_t = jnp.where(dim_index == 0, -1.0, 1.0) * jnp.sin(rot_angle)
-        r_own = (u_own * cos_t + u_other * sin_t).astype(jnp.bfloat16)
-        r_other = (u_other * cos_t - u_own * sin_t).astype(jnp.bfloat16)
-        k_new = r_own[:, heads_local:]
-        qf = jnp.concatenate([r_own[:, :heads_local], r_other[:, :heads_local]], axis=-1)
-        kf = jnp.concatenate([k_new, r_other[:, heads_local:]], axis=-1).astype(jnp.float32)
-        zeros = jnp.zeros((rows, q_group, slice_len), jnp.bfloat16)
-        qd = jnp.concatenate([
-            jnp.concatenate([r_own[:, :q_group], zeros], axis=-1),
-            jnp.concatenate([zeros, r_own[:, q_group:heads_local]], axis=-1)], axis=1)
-        vn = v_new.reshape(rows, kv_local * slice_len).astype(jnp.float32)
-
-        n_blk = (positions - LOW + BLK - 1) // BLK
-        cum = jnp.cumsum(n_blk)
-        off = cum - n_blk
-        slot = jnp.arange(rows * up_blocks)
-        row_of = jnp.sum((cum[None, :] <= slot[:, None]).astype(jnp.int32), axis=1)
+        gain = jnp.concatenate([jnp.stack([jnp.tile(q_gain, 2), jnp.tile(k_gain, 2)]), jnp.zeros((6, head_dim), jnp.float32)])
+
+        def by_column(w):
+            return w.transpose(1, 2, 0).reshape(-1, w.shape[0])
+
+        qd, sn, vn, kn = qkv(len(UP_SIZES) + 1, q_group, tokens, ln_attn[None], cos_t, sin_t, gain,
+                             by_column(w_query), by_column(w_key), by_column(w_value))
+        k_new = kn.reshape(rows, kv_local, slice_len)
+        v_new = vn.astype(jnp.bfloat16).reshape(rows, kv_local, slice_len)
+
+        row_units = up_blocks * BLK // UNIT
+        n_units = (positions - LOW + UNIT - 1) // UNIT
+        cum = jnp.cumsum(n_units)
+        off = cum - n_units
+        unit = jnp.arange(rows * row_units)
+        row_of = jnp.sum((cum[None, :] <= unit[:, None]).astype(jnp.int32), axis=1)
         off_of = jnp.sum(jnp.where(row_of[:, None] == jnp.arange(rows)[None, :], off[None, :], 0), axis=1)
-        idx = jnp.where(row_of < rows, row_of * up_blocks + slot - off_of, 0)
+        idx = jnp.where(row_of < rows, row_of * row_units + unit - off_of, 0)
 
         k_t = k_cache.transpose(0, 2, 3, 1).reshape(rows, kv_local * slice_len, cache_len)
         v_t = v_cache.transpose(0, 2, 3, 1).reshape(rows, kv_local * slice_len, cache_len)
-        which = jnp.sum((cum[-1] > jnp.array(UP_SIZES[:-1])).astype(jnp.int32))
+        which = jnp.sum((cum[-1] > jnp.array(UP_SIZES[:-1]) * (BLK // UNIT)).astype(jnp.int32))
         branches = [functools.partial(attend, n, i, head_dim ** -0.5) for i, n in enumerate(UP_SIZES)]
-        attn = lax.switch(which, branches, positions, off, idx, qd, qf, kf, vn, k_t, v_t)
+        attn = lax.switch(which, branches, positions, off, idx, qd, sn, vn, k_t, v_t)
         attn_vals = attn.reshape(rows, q_group, kv_local, slice_len).transpose(0, 2, 1, 3).reshape(rows, heads_local, slice_len)
 
         attn_vals = attn_vals.reshape(rows, heads_local * slice_len)

time: 264 us -> 266 us (level)
  local copies, waits for them, and re-layouts: 5.87 us -> 16.9 us
  Pallas kernels: 229 us -> 239 us
  matrix products: 8.79 us -> 0 us
  waiting for transfers between devices: 6.34 us -> 0 us
  starting transfers between devices: 3.41 us -> 0 us
    pallas_call x0 -> x1, Pallas kernels: none -> 21 us  [qkv(): pl.pallas_call(functools.partial(qkv_kernel, group), out_shape=(jax.Shape...]
    pallas_call x1, Pallas kernels: 152 us -> 141 us  [attend(): pl.pallas_call(functools.partial(attn_kernel, n_up, scale), out_shape=jax...]
    unnamed x20 -> x14, local copies, waits for them, and re-layouts: 2.96 us -> 12 us
    unnamed x3 -> x0, matrix products: 8.79 us -> none
    ppermute x2 -> x0, waiting for transfers between devices: 6.34 us -> none  [the longest x1 6.33 us: layer_body(): gains_other = lax.ppermute(gains, 'dim', swap_perm)]
    ppermute x2 -> x0, starting transfers between devices: 3.41 us -> none  [the longest x1 3.38 us: layer_body(): other = lax.ppermute(own, 'dim', swap_perm)]
  transfers between devices with their start and end apart: 2 -> 0, of which waited for: 1 -> 0; matrix products, arithmetic and copies ran while one was open for 2% -> 0% of each run, Pallas kernels for 0% -> 0%
where the time goes in v4:
time: 266 us; the launch traced here: 263 us
  Pallas kernels  239 us (90%)
  local copies, waits for them, and re-layouts  16.9 us (6%)
  other arithmetic  5.11 us (2%)
    pallas_call x1, Pallas kernels, attend(): pl.pallas_call(functools.partial(attn_kernel, n_up, scale), out_shape=jax...  141 us
    pallas_call x1, Pallas kernels, tail(): pl.pallas_call(tail_kernel, out_shape=jax.ShapeDtypeStruct((rows, d_model...  77 us
    pallas_call x1, Pallas kernels, qkv(): pl.pallas_call(functools.partial(qkv_kernel, group), out_shape=(jax.Shape...  21 us
    unnamed x14, local copies, waits for them, and re-layouts  12 us

profile of v4, /device:TPU:0, one launch (start us, length us, event | category | flops | bytes accessed | tf_op | source)
XLA Modules:
  0.0 263.1 jit_solution(163239831736320213)
XLA Ops:
  0.6 0.0 copy-start.5
  0.6 0.8 fusion.2
  1.4 0.1 copy.31
  1.5 0.2 reduce-window.4
  1.7 0.5 slice.5
  2.2 1.9 fusion.1
  4.8 0.1 reduce
  4.9 0.3 convert_reduce_fusion
  5.3 0.6 select_reduce_fusion
  6.0 0.1 mul.47
  6.0 0.3 fusion
  6.4 0.7 tile.8
  7.0 0.1 stack_tile.7
  7.1 0.7 tile.7
  7.8 0.1 stack_tile.6
  7.8 0.1 pad.4.clone
  7.9 0.1 maximum_maximum_fusion.gain_ref
  8.0 0.0 copy-start
  8.0 4.0 %copy-done = bf16[5120,16,64]{0,2,1:T(8,128)(2,1)S(1)} copy-done((bf16[5120,16,64]{0,2,1:T(8,128)(2,1)S(1)}, bf16[5120,16,64]{0,2,1:T(8,128)(2,1)}, u32[]{:S(2)}) %copy-start) | copy-done | bytes 10485784
  12.0 0.0 copy-start.1
  12.0 1.3 copy-done.1
  13.3 0.0 copy-start.2
  13.3 1.3 copy-done.2
  14.6 0.0 copy-start.3
  14.6 1.3 copy-done.3
  15.9 0.0 copy-start.4
  15.9 0.7 copy-done.4
  16.6 21.0 %qkv.1 = (f32[128,16,128]{2,1,0:T(8,128)S(1)}, f32[128,16,128]{2,1,0:T(8,128)S(1)}, f32[128,128]{1,0:T(8,128)S(1)}, bf16[128,128]{1,0:T(8,128)(2,1)S(1)}) custom-call(bf16[128,5120]{1,0:T(8,128)(2,1)S(1)} %copy-done.1, f32[1,5120]{1,0:T(1,128)S(1)} %bitcast.37, f32[128,128]{1,0:T(8,128)S(1)} %get-tuple-element.218.cos_ref, ...), custom_call_target="tpu_custom_call" | custom-call | tf_op jit(solution)/shard_map/qkv/pallas_call | solution.py:136
  37.6 0.0 copy-done.5
  37.6 141.7 %conditional.1 = (bf16[128,8,128]{2,1,0:T(8,128)(2,1)S(1)}) conditional(s32[]{:T(128)} %clamp.3, (s32[128]{0:T(128)S(1)}, s32[128]{0:T(128)S(1)}, s32[2048]{0:T(1024)S(1)}, f32[128,16,128]{2,1,0:T(8,128)S(1)}, f32[128,16,128]{2,1,0:T(8,128)S(1)}, /*index=5*/f32[128,128]{1,0:T(8,128)S(1)}, ...), branch_computations={%region_4.5_spmd, %region_5.6_spmd, %region_6.7_spmd, %region_7.8_... | conditional | bytes 8 | solution.py:608
  37.6 141.4 %attend_256.1 = bf16[128,8,128]{2,1,0:T(8,128)(2,1)S(1)} custom-call(s32[128]{0:T(128)S(1)} %get-tuple-element.145.pos_ref, s32[128]{0:T(128)S(1)} %get-tuple-element.146.off_ref, s32[2048]{0:T(1024)S(1)} %get-tuple-element.147.idx_ref, f32[128,16,128]{2,1,0:T(8,128)S(1)} %get-tuple-element.148.qd_ref, f32[128,16,128]{2,1,0:T(8,128)S(1)} %get-tuple-element.149.sn_ref, ...), custom_call_target="tpu_custom_call" | custom-call | tf_op jit(solution)/shard_map/cond/branch_1_fun/attend_256/pallas_call | solution.py:290
  179.3 0.2 copy.32
  179.6 0.9 copy.36.x_ref
  180.4 0.9 dynamic-slice_bitcast_fusion.1
  181.4 0.7 convert_bitcast_fusion.tok_ref
  182.1 77.0 %tail.1 = bf16[128,5120]{1,0:T(8,128)(2,1)} custom-call(bf16[128,1024]{1,0:T(8,128)(2,1)} %copy.36.x_ref, f32[10,2,8,512]{3,2,1,0:T(8,128)} %convert_bitcast_fusion.tok_ref, f32[10,1,512]{2,1,0:T(1,128)} %bitcast.59, bf16[1024,5120]{1,0:T(8,128)(2,1)} %bitcast.54, bf16[5120,3200]{1,0:T(8,128)(2,1)} %wg_hbm.1, bf16[5120,3200]{1,0:T(8,128)(2,1)} %wu_hbm.1, ...), custom_call_target="tpu_custom_call" | custom-call | tf_op jit(solution)/shard_map/tail/pallas_call | solution.py:538
  259.2 0.7 copy.37
  259.9 0.7 copy.38
  260.6 2.5 copy.50
  (7 shorter events, 0.1 us)
Async XLA Ops:
  0.6 37.0 %copy-start.5 = (s32[128]{0:T(128)S(1)}, s32[128]{0:T(128)}, u32[]{:S(2)}) copy-start(s32[128]{0:T(128)} %param.38) | copy-start | bytes 1540
  8.0 4.0 %copy-start = (bf16[5120,16,64]{0,2,1:T(8,128)(2,1)S(1)}, bf16[5120,16,64]{0,2,1:T(8,128)(2,1)}, u32[]{:S(2)}) copy-start(bf16[5120,16,64]{0,2,1:T(8,128)(2,1)} %param.26) | copy-start | bytes 31457284
  12.0 1.3 copy-start.1
  13.3 1.3 copy-start.2
  14.6 1.3 copy-start.3
  15.9 0.7 copy-start.4

commit v5 on v4

--- a/solution.py
+++ b/solution.py
@@ -2,6 +2,7 @@
 
 import jax
 import jax.numpy as jnp
+import numpy as np
 from jax import lax
 from jax.experimental import pallas as pl
 from jax.experimental.pallas import tpu as pltpu
@@ -22,8 +23,8 @@
 UP_SIZES = (240, 256, 264, 272, 280, 288, 304, 512)
 
 
-def qkv_kernel(group, tok_ref, ln_ref, cos_ref, sin_ref, gain_ref, wq_hbm, wk_hbm, wv_hbm, qd_ref, sn_ref, vn_ref, kn_ref,
-               hid, wq, wk, wv, own, other, gain_other, wsem, snd, rcv):
+def qkv_kernel(group, tok_ref, ln_ref, angle_ref, qg_ref, kg_ref, wq_hbm, wk_hbm, wv_hbm, qd_ref, sn_ref, vn_ref, kn_ref,
+               hid, wq, wk, wv, own, other, gain_ref, gain_other, wsem, snd, rcv):
     partner = {"dim": 1 - lax.axis_index("dim")}
     rows, depth = tok_ref.shape
     n_q = own.shape[0] - 1
@@ -56,8 +57,11 @@
     v_load.start()
     barrier = pltpu.get_barrier_semaphore()
     pl.semaphore_signal(barrier, inc=1, device_id=partner, device_id_type=MESH)
+    gain_ref[...] = jnp.zeros_like(gain_ref)
+    for row, ref in enumerate((qg_ref, kg_ref)):
+        gain_ref[row:row + 1, :half] = ref[...]
+        gain_ref[row:row + 1, half:] = ref[...]
     pl.semaphore_wait(barrier, 1)
-    g_copy.start()
 
     @pl.loop(0, rows // 16)
     def _(i):
@@ -69,6 +73,7 @@
     def project(w):
         return lax.dot_general(hid[...], w, (((1,), (1,)), ((), ())), preferred_element_type=f32)
 
+    g_copy.start()
     k_load.wait()
     own[n_q] = project(wk[...])
 
@@ -88,7 +93,8 @@
     v_load.wait()
     vn_ref[...] = project(wv[...]).astype(bf16).astype(f32)
     low = lax.broadcasted_iota(jnp.int32, (rows, BLK), 1) < half
-    cos_t, sin_t = cos_ref[...], sin_ref[...]
+    cos_t = jnp.cos(angle_ref[...])
+    sin_t = jnp.sin(angle_ref[...]) * jnp.where(lax.axis_index("dim") == 0, -1.0, 1.0)
 
     def halves(x):
         return (jnp.sum(jnp.where(low, x, 0.0), axis=-1, keepdims=True), jnp.sum(jnp.where(low, 0.0, x), axis=-1, keepdims=True))
@@ -115,16 +121,17 @@
         new = halves(q_own * kk[kv][0] + q_oth * kk[kv][1])
         turned = pltpu.roll(q_own, half, 1)
         for e in range(2):
-            sn_ref[:, 2 * i + e, :] = jnp.broadcast_to(new[e], (rows, BLK))
+            row = i + n_q * e
+            sn_ref[:, row, :] = jnp.broadcast_to(new[e], (rows, BLK))
             val = q_own if e == kv else turned
-            qd_ref[:, 2 * i + e, :] = jnp.where(low, val, 0.0) if kv == 0 else jnp.where(low, 0.0, val)
+            qd_ref[:, row, :] = jnp.where(low, val, 0.0) if kv == 0 else jnp.where(low, 0.0, val)
     for c in range(steps):
         q_copy(c).wait_send()
     k_copy.wait_send()
     g_copy.wait_send()
 
 
-def qkv(cid, group, tokens, ln, cos_t, sin_t, gain, w_q, w_k, w_v):
+def qkv(cid, group, tokens, ln, angle, q_gain, k_gain, w_q, w_k, w_v):
     rows, depth = tokens.shape
     n_q = w_q.shape[0] // BLK
     steps = n_q // 2
@@ -146,12 +153,13 @@
             pltpu.VMEM(w_v.shape, bf16),
             pltpu.VMEM((n_q + 1, rows, BLK), f32),
             pltpu.VMEM((n_q + 1, rows, BLK), f32),
-            pltpu.VMEM(gain.shape, f32),
+            pltpu.VMEM((8, BLK), f32),
+            pltpu.VMEM((8, BLK), f32),
             dma((steps + 2,)), dma((steps + 2,)), dma((steps + 2,)),
         ],
-        compiler_params=pltpu.CompilerParams(collective_id=cid, has_side_effects=True, vmem_limit_bytes=32 * 1024 * 1024),
+        compiler_params=pltpu.CompilerParams(collective_id=cid, has_side_effects=True, vmem_limit_bytes=62 * 1024 * 1024),
         name="qkv",
-    )(tokens, ln, cos_t, sin_t, gain, w_q, w_k, w_v)
+    )(tokens, ln, angle, q_gain, k_gain, w_q, w_k, w_v)
 
 
 def attn_kernel(n_up, scale, pos_ref, off_ref, idx_ref, qd_ref, sn_ref, vn_ref, k_hbm, v_hbm, o_ref,
@@ -214,7 +222,8 @@
                 j = c * UCH + r
                 block = None
                 for k in range(per_blk):
-                    src = idx_ref[j * per_blk + k]
+                    row = idx_ref[j * per_blk + k]
+                    src = jnp.minimum(row * (up_blocks * per_blk) + j * per_blk + k - off_ref[row], rows * up_blocks * per_blk - 1)
                     piece = pltpu.roll(own_up[src // per_blk], (k + per_blk - src % per_blk) % per_blk * UNIT, 1)
                     block = piece if k == 0 else jnp.where(lane_up >= k * UNIT, piece, block)
                 pack[j] = block
@@ -232,6 +241,7 @@
         up_copy(c).wait_recv()
 
     lane = lax.broadcasted_iota(jnp.int32, (8, 2 * 64), 1)
+    first = lax.broadcasted_iota(jnp.int32, (8, 2 * 64), 0) < 4
     t_up = lane_up + LOW
 
     @pl.loop(0, n_ch)
@@ -263,7 +273,8 @@
             p_new = (e_new * inv).astype(jnp.bfloat16).astype(jnp.float32)
             o = lax.dot_general(p, vbuf[lax.rem(c, SLOTS), r], (((1,), (1,)), ((), ())), preferred_element_type=jnp.float32)
             o = o + p_new * vn_ref[pl.ds(b, 1), :]
-            o_ref[b] = jnp.where(lane < 64, o[0:8], o[8:16]).astype(jnp.bfloat16)
+            even, odd = o[0:8], o[8:16]
+            o_ref[b] = jnp.where(lane < 64, jnp.where(first, even, pltpu.roll(even, 64, 1)), jnp.where(first, pltpu.roll(odd, 64, 1), odd))
 
         @pl.when(c + SLOTS < n_ch)
         def _():
@@ -289,7 +300,7 @@
     hbm = pl.BlockSpec(memory_space=pl.ANY)
     return pl.pallas_call(
         functools.partial(attn_kernel, n_up, scale),
-        out_shape=jax.ShapeDtypeStruct((rows, 8, 128), jnp.bfloat16),
+        out_shape=jax.ShapeDtypeStruct((rows, 8, 128), jnp.float32),
         in_specs=[smem, smem, smem, vmem, vmem, vmem, hbm, hbm],
         out_specs=vmem,
         scratch_shapes=[
@@ -318,9 +329,9 @@
 WD_SLOTS = 4
 
 
-def tail_kernel(x_ref, tok_ref, ln_ref, wo_hbm, wg_hbm, wu_hbm, wd_hbm, out_ref,
-                part, r1, r2, r3, full, xres, acc_g, acc_u, mact, wo, wg, wu, wd,
-                wo_s, wg_s, wu_s, wd_s, snd, rcv):
+def tail_kernel(attn_ref, tok_hbm, ln_ref, wo_hbm, wg_hbm, wu_hbm, wd_hbm, out_ref,
+                x_ref, tok_ref, part, r1, r2, r3, full, xres, acc_g, acc_u, mact, wo, wg, wu, wd,
+                tok_s, wo_s, wg_s, wu_s, wd_s, snd, rcv):
     heads = lax.axis_index("heads")
     core, cx, cy = lax.rem(heads, 2), heads // 2, lax.axis_index("dim")
     sib = {"heads": 2 * cx + 1 - core}
@@ -438,18 +449,24 @@
             arrived(ph, 5, t - 5)
             finish(t - 5)
 
+    blk_a, blk_b = core * 8 + 2 * cx + cy, core * 8 + 4 + 2 * cy + cx
+    tok_loads = [pltpu.make_async_copy(tok_hbm.at[blk], tok_ref.at[i], tok_s.at[i]) for i, blk in enumerate((blk_a, blk_b))]
     for q in range(WO_SLOTS):
         start(wo_copy(q))
+    start(tok_loads)
     barrier = pltpu.get_barrier_semaphore()
     for dev in (sib, xn, yn):
         pl.semaphore_signal(barrier, inc=1, device_id=dev, device_id_type=MESH)
     pl.semaphore_wait(barrier, 3)
     acc_g[...] = jnp.zeros_like(acc_g)
     acc_u[...] = jnp.zeros_like(acc_u)
+    for i in range(attn_ref.shape[1]):
+        x_ref[:, i * BLK:(i + 1) * BLK] = attn_ref[:, i, :].astype(jnp.bfloat16)
+    wait(tok_loads)
 
     def finish_attn(u, a, b):
-        xres[u, 0] = (tok_ref[u, 0] + a).astype(jnp.bfloat16).astype(f32)
-        xres[u, 1] = (tok_ref[u, 1] + b).astype(jnp.bfloat16).astype(f32)
+        xres[u, 0] = (tok_ref[0, :, cols(u)].astype(f32) + a).astype(jnp.bfloat16).astype(f32)
+        xres[u, 1] = (tok_ref[1, :, cols(u)].astype(f32) + b).astype(jnp.bfloat16).astype(f32)
 
     @pl.loop(0, Q + 6)
     def _(t):
@@ -476,7 +493,6 @@
     for q in range(Q):
         sq = sq + jnp.sum(xres[q] * xres[q], axis=-1, keepdims=True)
     inv = lax.rsqrt(sq / (Q * width) + EPS)
-    blk_a, blk_b = core * 8 + 2 * cx + cy, core * 8 + 4 + 2 * cy + cx
     for q in range(Q):
         h = (xres[q] * inv * ln_ref[q]).astype(jnp.bfloat16).astype(f32)
         full[q, blk_a] = h[0]
@@ -527,8 +543,9 @@
     drain(1, (0, 1, 2, 3, 4, 5))
 
 
-def tail(cid, attn_vals, tok_own, ln, w_out, w_gate, w_up, w_down):
-    rows, depth = attn_vals.shape
+def tail(cid, attn, tok_blocks, ln, w_out, w_gate, w_up, w_down):
+    rows = attn.shape[0]
+    depth = w_out.shape[0]
     d_model, inner = w_gate.shape
     width = d_model // Q
     vmem = pl.BlockSpec(memory_space=pltpu.VMEM)
@@ -538,9 +555,11 @@
     return pl.pallas_call(
         tail_kernel,
         out_shape=jax.ShapeDtypeStruct((rows, d_model), bf16),
-        in_specs=[vmem, vmem, vmem, hbm, hbm, hbm, hbm],
+        in_specs=[vmem, hbm, vmem, hbm, hbm, hbm, hbm],
         out_specs=vmem,
         scratch_shapes=[
+            pltpu.VMEM((rows, depth), bf16),
+            pltpu.VMEM((2, 8, d_model), bf16),
             pltpu.VMEM((Q, 16, 8, width), f32),
             pltpu.VMEM((Q, 8, 8, width), f32),
             pltpu.VMEM((Q, 4, 8, width), f32),
@@ -554,12 +573,12 @@
             pltpu.VMEM((GU_SLOTS, width, inner), bf16),
             pltpu.VMEM((GU_SLOTS, width, inner), bf16),
             pltpu.VMEM((WD_SLOTS, inner, width), bf16),
-            dma((WO_SLOTS,)), dma((GU_SLOTS,)), dma((GU_SLOTS,)), dma((WD_SLOTS,)),
+            dma((2,)), dma((WO_SLOTS,)), dma((GU_SLOTS,)), dma((GU_SLOTS,)), dma((WD_SLOTS,)),
             dma((2, 10)), dma((2, 10, Q)),
         ],
-        compiler_params=pltpu.CompilerParams(collective_id=cid, has_side_effects=True, vmem_limit_bytes=62 * 1024 * 1024),
+        compiler_params=pltpu.CompilerParams(collective_id=cid, has_side_effects=True, vmem_limit_bytes=59 * 1024 * 1024),
         name="tail",
-    )(attn_vals, tok_own, ln, w_out, w_gate, w_up, w_down)
+    )(attn, tok_blocks, ln, w_out, w_gate, w_up, w_down)
 
 
 def solution(mesh):
@@ -578,44 +597,32 @@
         up_blocks = (cache_len - LOW) // BLK
         dim_index = lax.axis_index('dim')
 
-        inv_freq = ROPE_BASE ** (-jnp.arange(half_dim, dtype=jnp.float32) * 2.0 / head_dim)
-        rot_angle = positions.astype(jnp.float32)[:, None] * jnp.tile(inv_freq, 2)
-        cos_t = jnp.cos(rot_angle)
-        sin_t = jnp.where(dim_index == 0, -1.0, 1.0) * jnp.sin(rot_angle)
-        gain = jnp.concatenate([jnp.stack([jnp.tile(q_gain, 2), jnp.tile(k_gain, 2)]), jnp.zeros((6, head_dim), jnp.float32)])
+        inv_freq = np.tile(ROPE_BASE ** (-np.arange(half_dim) * 2.0 / head_dim), 2).astype(np.float32)
+        angle = positions.astype(jnp.float32)[:, None] * inv_freq
 
         def by_column(w):
             return w.transpose(1, 2, 0).reshape(-1, w.shape[0])
 
-        qd, sn, vn, kn = qkv(len(UP_SIZES) + 1, q_group, tokens, ln_attn[None], cos_t, sin_t, gain,
+        qd, sn, vn, kn = qkv(len(UP_SIZES) + 1, q_group, tokens, ln_attn[None], angle, q_gain[None], k_gain[None],
                              by_column(w_query), by_column(w_key), by_column(w_value))
         k_new = kn.reshape(rows, kv_local, slice_len)
         v_new = vn.astype(jnp.bfloat16).reshape(rows, kv_local, slice_len)
 
         row_units = up_blocks * BLK // UNIT
         n_units = (positions - LOW + UNIT - 1) // UNIT
-        cum = jnp.cumsum(n_units)
+        seq = jnp.arange(rows)
+        cum = jnp.sum(jnp.where(seq[:, None] >= seq[None, :], n_units[None, :], 0), axis=1)
         off = cum - n_units
         unit = jnp.arange(rows * row_units)
         row_of = jnp.sum((cum[None, :] <= unit[:, None]).astype(jnp.int32), axis=1)
-        off_of = jnp.sum(jnp.where(row_of[:, None] == jnp.arange(rows)[None, :], off[None, :], 0), axis=1)
-        idx = jnp.where(row_of < rows, row_of * row_units + unit - off_of, 0)
+        row_of = jnp.minimum(row_of, rows - 1)
 
         k_t = k_cache.transpose(0, 2, 3, 1).reshape(rows, kv_local * slice_len, cache_len)
         v_t = v_cache.transpose(0, 2, 3, 1).reshape(rows, kv_local * slice_len, cache_len)
-        which = jnp.sum((cum[-1] > jnp.array(UP_SIZES[:-1]) * (BLK // UNIT)).astype(jnp.int32))
+        which = jnp.sum((jnp.sum(n_units) > np.array(UP_SIZES[:-1]) * (BLK // UNIT)).astype(jnp.int32))
         branches = [functools.partial(attend, n, i, head_dim ** -0.5) for i, n in enumerate(UP_SIZES)]
-        attn = lax.switch(which, branches, positions, off, idx, qd, sn, vn, k_t, v_t)
-        attn_vals = attn.reshape(rows, q_group, kv_local, slice_len).transpose(0, 2, 1, 3).reshape(rows, heads_local, slice_len)
-
-        attn_vals = attn_vals.reshape(rows, heads_local * slice_len)
-        heads_index = lax.axis_index('heads')
-        core, cx = heads_index % 2, heads_index // 2
-        tok_blocks = tokens.reshape(16, 8, Q, -1)
-        tok_own = jnp.stack([lax.dynamic_index_in_dim(tok_blocks, core * 8 + 2 * cx + dim_index, 0, keepdims=False),
-                             lax.dynamic_index_in_dim(tok_blocks, core * 8 + 4 + 2 * dim_index + cx, 0, keepdims=False)])
-        tok_own = tok_own.astype(jnp.float32).transpose(2, 0, 1, 3)
-        out = tail(len(UP_SIZES), attn_vals, tok_own, ln_mlp.reshape(Q, 1, -1), w_out.reshape(heads_local * slice_len, -1), w_gate, w_up, w_down)
+        attn = lax.switch(which, branches, positions, off, row_of, qd, sn, vn, k_t, v_t)
+        out = tail(len(UP_SIZES), attn, tokens.reshape(16, 8, -1), ln_mlp.reshape(Q, 1, -1), w_out.reshape(heads_local * slice_len, -1), w_gate, w_up, w_down)
         return out, k_new, v_new
 
     row_spec = P('dp', None)

time: 266 us -> 255 us (0.959); the launches traced: 263 us -> 256 us
  local copies, waits for them, and re-layouts: 16.9 us -> 3.91 us
  Pallas kernels: 239 us -> 245 us
    unnamed x14 -> x5, local copies, waits for them, and re-layouts: 12 us -> 2.47 us
    pallas_call x1, Pallas kernels: 141 us -> 145 us  [attend(): pl.pallas_call(functools.partial(attn_kernel, n_up, scale), out_shape=jax...]
where the time goes in v5:
time: 255 us; the launch traced here: 256 us
  Pallas kernels  245 us (96%)
  other arithmetic  5.17 us (2%)
  local copies, waits for them, and re-layouts  3.91 us (2%)
    pallas_call x1, Pallas kernels, attend(): pl.pallas_call(functools.partial(attn_kernel, n_up, scale), out_shape=jax...  145 us
    pallas_call x1, Pallas kernels, tail(): pl.pallas_call(tail_kernel, out_shape=jax.ShapeDtypeStruct((rows, d_model...  77.8 us
    pallas_call x1, Pallas kernels, qkv(): pl.pallas_call(functools.partial(qkv_kernel, group), out_shape=(jax.Shape...  22.7 us

profile of v5, /device:TPU:0, one launch (start us, length us, event | category | flops | bytes accessed | tf_op | source)
XLA Modules:
  0.0 255.8 jit_solution(14453850358491692922)
XLA Ops:
  0.6 0.0 copy-start
  0.6 1.4 fusion.1
  2.0 1.9 fusion
  4.6 0.1 select_reduce_fusion
  4.7 0.3 convert_reduce_fusion
  5.1 1.4 broadcast_multiply_fusion.angle_ref
  6.5 22.7 %qkv.1 = (f32[128,16,128]{2,1,0:T(8,128)S(1)}, f32[128,16,128]{2,1,0:T(8,128)}, f32[128,128]{1,0:T(8,128)S(1)}, bf16[128,128]{1,0:T(8,128)(2,1)}) custom-call(bf16[128,5120]{1,0:T(8,128)(2,1)} %tok_ref.1, f32[1,5120]{1,0:T(1,128)} %bitcast.46, f32[128,128]{1,0:T(8,128)} %broadcast_multiply_fusion.angle_ref, f32[1,64]{1,0:T(1,128)} %bitcast.48, ...), custom_call_target="tpu_custom_call" | custom-call | tf_op jit(solution)/shard_map/qkv/pallas_call | solution.py:143
  29.2 0.0 copy-done
  29.2 0.0 copy-start.1
  29.2 144.9 %conditional.1 = (f32[128,8,128]{2,1,0:T(8,128)S(1)}) conditional(s32[]{:T(128)} %clamp.3, (s32[128]{0:T(128)S(1)}, s32[128]{0:T(128)S(1)}, s32[2048]{0:T(1024)S(1)}, f32[128,16,128]{2,1,0:T(8,128)S(1)}, f32[128,16,128]{2,1,0:T(8,128)}, /*index=5*/f32[128,128]{1,0:T(8,128)S(1)}, bf16[128,128,1024]{2,1,0:T(8,128)(2,1)}, ...), branch_computations={%region_4.5_spmd, %region_5.6_spmd, %region_6.7_spmd, %region_7.8_... | conditional | bytes 8 | solution.py:624
  29.3 144.6 %attend_272.1 = f32[128,8,128]{2,1,0:T(8,128)S(1)} custom-call(s32[128]{0:T(128)S(1)} %get-tuple-element.161.pos_ref, s32[128]{0:T(128)S(1)} %get-tuple-element.162.off_ref, s32[2048]{0:T(1024)S(1)} %get-tuple-element.163.idx_ref, f32[128,16,128]{2,1,0:T(8,128)S(1)} %get-tuple-element.164.qd_ref, f32[128,16,128]{2,1,0:T(8,128)} %get-tuple-element.165.sn_ref, ...), custom_call_target="tpu_custom_call" | custom-call | tf_op jit(solution)/shard_map/cond/branch_3_fun/attend_272/pallas_call | solution.py:301
  174.1 0.0 copy-done.1
  174.1 0.7 copy.24
  174.8 0.7 copy.25
  175.6 77.8 %tail.1 = bf16[128,5120]{1,0:T(8,128)(2,1)} custom-call(f32[128,8,128]{2,1,0:T(8,128)S(1)} %get-tuple-element.224.attn_ref, bf16[16,8,5120]{2,1,0:T(8,128)(2,1)} %bitcast.41, f32[10,1,512]{2,1,0:T(1,128)} %bitcast.47, bf16[1024,5120]{1,0:T(8,128)(2,1)} %bitcast.39, bf16[5120,3200]{1,0:T(8,128)(2,1)} %wg_hbm.1, bf16[5120,3200]{1,0:T(8,128)(2,1)} %wu_hbm.1, ...), custom_call_target="tpu_custom_call" | custom-call | tf_op jit(solution)/shard_map/tail/pallas_call | solution.py:555
  253.4 2.5 copy.35
  (3 shorter events, 0.0 us)
Async XLA Ops:
  0.6 28.6 %copy-start = (s32[128]{0:T(128)S(1)}, s32[128]{0:T(128)}, u32[]{:S(2)}) copy-start(s32[128]{0:T(128)} %param.39) | copy-start | bytes 1540
  29.2 144.9 %copy-start.1 = (bf16[128,128]{1,0:T(8,128)(2,1)S(1)}, bf16[128,128]{1,0:T(8,128)(2,1)}, u32[]{:S(2)}) copy-start(bf16[128,128]{1,0:T(8,128)(2,1)} %get-tuple-element.211) | copy-start | bytes 98308

commit v6 on v5

--- a/solution.py
+++ b/solution.py
@@ -14,16 +14,16 @@
 
 BLK = 128
 LOW = 512
-CH = 4
+CH = 2
 UCH = 8
-UNIT = 32
-SLOTS = 4
-FIRST = 8
-LEAD = 4
-UP_SIZES = (240, 256, 264, 272, 280, 288, 304, 512)
-
-
-def qkv_kernel(group, tok_ref, ln_ref, angle_ref, qg_ref, kg_ref, wq_hbm, wk_hbm, wv_hbm, qd_ref, sn_ref, vn_ref, kn_ref,
+UNIT = 16
+SLOTS = 6
+FIRST = 16
+LEAD = 8
+UP_SIZES = (232, 248, 256, 264, 272, 280, 296, 512)
+
+
+def qkv_kernel(group, tok_ref, ln_ref, pos_ref, freq_ref, qg_ref, kg_ref, wq_hbm, wk_hbm, wv_hbm, qd_ref, sn_ref, vn_ref, kt_ref, vt_ref,
                hid, wq, wk, wv, own, other, gain_ref, gain_other, wsem, snd, rcv):
     partner = {"dim": 1 - lax.axis_index("dim")}
     rows, depth = tok_ref.shape
@@ -63,7 +63,7 @@
         gain_ref[row:row + 1, half:] = ref[...]
     pl.semaphore_wait(barrier, 1)
 
-    @pl.loop(0, rows // 16)
+    @pl.loop(0, rows // 16, unroll=4)
     def _(i):
         part = pl.ds(pl.multiple_of(i * 16, 16), 16)
         x = tok_ref[part, :].astype(f32)
@@ -76,25 +76,25 @@
     g_copy.start()
     k_load.wait()
     own[n_q] = project(wk[...])
+    k_copy.start()
 
     @pl.loop(0, steps)
     def _(c):
         wq_copy(c).wait()
         u = project(wq[pl.ds(pl.multiple_of(c * per_step, per_step), per_step), :])
 
-        @pl.when(c == 0)
-        def _():
-            k_copy.start()
-
         own[2 * c] = u[:, :BLK]
         own[2 * c + 1] = u[:, BLK:]
         q_copy(c).start()
 
     v_load.wait()
-    vn_ref[...] = project(wv[...]).astype(bf16).astype(f32)
+    v_row = project(wv[...]).astype(bf16).astype(f32)
+    vn_ref[...] = v_row
+    vt_ref[...] = v_row.T.astype(bf16)
     low = lax.broadcasted_iota(jnp.int32, (rows, BLK), 1) < half
-    cos_t = jnp.cos(angle_ref[...])
-    sin_t = jnp.sin(angle_ref[...]) * jnp.where(lax.axis_index("dim") == 0, -1.0, 1.0)
+    angle = jnp.broadcast_to(pos_ref[...], (rows, rows)).T * freq_ref[...]
+    cos_t = jnp.cos(angle)
+    sin_t = jnp.sin(angle) * jnp.where(lax.axis_index("dim") == 0, -1.0, 1.0)
 
     def halves(x):
         return (jnp.sum(jnp.where(low, x, 0.0), axis=-1, keepdims=True), jnp.sum(jnp.where(low, 0.0, x), axis=-1, keepdims=True))
@@ -109,7 +109,7 @@
     g_copy.wait_recv()
     k_copy.wait_recv()
     k_own, k_oth = rotate(n_q, 1)
-    kn_ref[...] = k_own.astype(bf16)
+    kt_ref[...] = k_own.T.astype(bf16)
     kr_own, kr_oth = pltpu.roll(k_own, half, 1), pltpu.roll(k_oth, half, 1)
     kk = [(jnp.where(low, k_own, kr_own), jnp.where(low, k_oth, kr_oth)),
           (jnp.where(low, kr_own, k_own), jnp.where(low, kr_oth, k_oth))]
@@ -131,7 +131,7 @@
     g_copy.wait_send()
 
 
-def qkv(cid, group, tokens, ln, angle, q_gain, k_gain, w_q, w_k, w_v):
+def qkv(cid, group, tokens, ln, pos, freq, q_gain, k_gain, w_q, w_k, w_v):
     rows, depth = tokens.shape
     n_q = w_q.shape[0] // BLK
     steps = n_q // 2
@@ -143,9 +143,9 @@
     return pl.pallas_call(
         functools.partial(qkv_kernel, group),
         out_shape=(jax.ShapeDtypeStruct((rows, heads, BLK), f32), jax.ShapeDtypeStruct((rows, heads, BLK), f32),
-                   jax.ShapeDtypeStruct((rows, BLK), f32), jax.ShapeDtypeStruct((rows, BLK), bf16)),
-        in_specs=[vmem] * 5 + [hbm] * 3,
-        out_specs=(vmem,) * 4,
+                   jax.ShapeDtypeStruct((rows, BLK), f32), jax.ShapeDtypeStruct((BLK, rows), bf16), jax.ShapeDtypeStruct((BLK, rows), bf16)),
+        in_specs=[vmem] * 6 + [hbm] * 3,
+        out_specs=(vmem,) * 5,
         scratch_shapes=[
             pltpu.VMEM((rows, depth), bf16),
             pltpu.VMEM(w_q.shape, bf16),
@@ -159,11 +159,11 @@
         ],
         compiler_params=pltpu.CompilerParams(collective_id=cid, has_side_effects=True, vmem_limit_bytes=62 * 1024 * 1024),
         name="qkv",
-    )(tokens, ln, angle, q_gain, k_gain, w_q, w_k, w_v)
-
-
-def attn_kernel(n_up, scale, pos_ref, off_ref, idx_ref, qd_ref, sn_ref, vn_ref, k_hbm, v_hbm, o_ref,
-                kbuf, vbuf, own_lo, own_up, pack, rlo, rup, ksem, vsem, slo_s, slo_r, sup_s, sup_r):
+    )(tokens, ln, pos, freq, q_gain, k_gain, w_q, w_k, w_v)
+
+
+def attn_kernel(n_up, scale, pos_ref, qd_ref, sn_ref, vn_ref, k_hbm, v_hbm, o_ref,
+                off_ref, kbuf, vbuf, own_lo, own_up, pack, rlo, rup, ksem, vsem, send, slo_r, sup_r):
     partner = {"dim": 1 - lax.axis_index("dim")}
     rows = qd_ref.shape[0]
     n_ch = rows // CH
@@ -180,12 +180,12 @@
 
     def lo_copy(c):
         part = pl.ds(c * CH, CH)
-        return pltpu.make_async_remote_copy(src_ref=own_lo.at[part], dst_ref=rlo.at[part], send_sem=slo_s.at[c],
+        return pltpu.make_async_remote_copy(src_ref=own_lo.at[part], dst_ref=rlo.at[part], send_sem=send.at[0],
                                             recv_sem=slo_r.at[c], device_id=partner, device_id_type=MESH)
 
     def up_copy(c):
         part = pl.ds(c * UCH, UCH)
-        return pltpu.make_async_remote_copy(src_ref=pack.at[part], dst_ref=rup.at[part], send_sem=sup_s.at[c],
+        return pltpu.make_async_remote_copy(src_ref=pack.at[part], dst_ref=rup.at[part], send_sem=send.at[1],
                                             recv_sem=sup_r.at[c], device_id=partner, device_id_type=MESH)
 
     for c in range(SLOTS):
@@ -195,6 +195,13 @@
     pl.semaphore_wait(barrier, 1)
     for c in range(SLOTS):
         vcopy(c).start()
+    row_units = up_blocks * per_blk
+
+    def place(b, total):
+        off_ref[b] = total
+        return total + jnp.maximum((pos_ref[b] - LOW + UNIT - 1) // UNIT, 1)
+
+    lax.fori_loop(0, rows, place, jnp.int32(0))
 
     @pl.loop(0, n_ch)
     def _(c):
@@ -214,23 +221,26 @@
         def _():
             lo_copy(c - 1).start()
 
-    @pl.loop(0, n_uch + 1)
-    def _(c):
-        @pl.when(c < n_uch)
-        def _():
-            for r in range(UCH):
-                j = c * UCH + r
-                block = None
-                for k in range(per_blk):
-                    row = idx_ref[j * per_blk + k]
-                    src = jnp.minimum(row * (up_blocks * per_blk) + j * per_blk + k - off_ref[row], rows * up_blocks * per_blk - 1)
-                    piece = pltpu.roll(own_up[src // per_blk], (k + per_blk - src % per_blk) % per_blk * UNIT, 1)
-                    block = piece if k == 0 else jnp.where(lane_up >= k * UNIT, piece, block)
-                pack[j] = block
+    def fill(c, row):
+        for r in range(UCH):
+            j = c * UCH + r
+            block = None
+            for k in range(per_blk):
+                unit = j * per_blk + k
+                following = jnp.minimum(row + 1, rows - 1)
+                row = jnp.where(unit >= off_ref[following], following, row)
+                src = jnp.minimum(unit - off_ref[row], row_units - 1)
+                piece = pltpu.roll(own_up[row * up_blocks + src // per_blk], (k + per_blk - src % per_blk) % per_blk * UNIT, 1)
+                block = piece if k == 0 else jnp.where(lane_up >= k * UNIT, piece, block)
+            pack[j] = block
 
         @pl.when(c >= 1)
         def _():
             up_copy(c - 1).start()
+        return row
+
+    lax.fori_loop(0, n_uch, fill, jnp.int32(0))
+    up_copy(n_uch - 1).start()
 
     @pl.loop(FIRST, FIRST + LEAD)
     def _(c):
@@ -280,16 +290,13 @@
         def _():
             vcopy(c + SLOTS).start()
 
-    @pl.loop(0, n_ch)
-    def _(c):
-        lo_copy(c).wait_send()
-
-    @pl.loop(0, n_uch)
-    def _(c):
-        up_copy(c).wait_send()
-
-
-def attend(n_up, cid, scale, pos, off, idx, qd, sn, vn, k_t, v_t):
+    pltpu.make_async_remote_copy(src_ref=own_lo, dst_ref=rlo, send_sem=send.at[0], recv_sem=slo_r.at[0],
+                                 device_id=partner, device_id_type=MESH).wait_send()
+    pltpu.make_async_remote_copy(src_ref=pack, dst_ref=rup, send_sem=send.at[1], recv_sem=sup_r.at[0],
+                                 device_id=partner, device_id_type=MESH).wait_send()
+
+
+def attend(n_up, cid, scale, pos, qd, sn, vn, k_t, v_t):
     rows = qd.shape[0]
     n_ch = rows // CH
     n_uch = n_up // UCH
@@ -301,9 +308,10 @@
     return pl.pallas_call(
         functools.partial(attn_kernel, n_up, scale),
         out_shape=jax.ShapeDtypeStruct((rows, 8, 128), jnp.float32),
-        in_specs=[smem, smem, smem, vmem, vmem, vmem, hbm, hbm],
+        in_specs=[smem, vmem, vmem, vmem, hbm, hbm],
         out_specs=vmem,
         scratch_shapes=[
+            pltpu.SMEM((rows,), jnp.int32),
             pltpu.VMEM((SLOTS, CH, 128, cache_len), jnp.bfloat16),
             pltpu.VMEM((SLOTS, CH, 128, cache_len), jnp.bfloat16),
             pltpu.VMEM((rows, 16, LOW), jnp.float32),
@@ -313,20 +321,19 @@
             pltpu.VMEM((n_up, 16, BLK), jnp.float32),
             pltpu.SemaphoreType.DMA((SLOTS,)),
             pltpu.SemaphoreType.DMA((SLOTS,)),
+            pltpu.SemaphoreType.DMA((2,)),
             pltpu.SemaphoreType.DMA((n_ch,)),
-            pltpu.SemaphoreType.DMA((n_ch,)),
-            pltpu.SemaphoreType.DMA((n_uch,)),
             pltpu.SemaphoreType.DMA((n_uch,)),
         ],
         compiler_params=pltpu.CompilerParams(collective_id=cid, has_side_effects=True, vmem_limit_bytes=40 * 1024 * 1024),
         name=f"attend_{n_up}",
-    )(pos, off, idx, qd, sn, vn, k_t, v_t)
+    )(pos, qd, sn, vn, k_t, v_t)
 
 
 Q = 10
 WO_SLOTS = 4
 GU_SLOTS = 4
-WD_SLOTS = 4
+WD_SLOTS = 3
 
 
 def tail_kernel(attn_ref, tok_hbm, ln_ref, wo_hbm, wg_hbm, wu_hbm, wd_hbm, out_ref,
@@ -576,7 +583,7 @@
             dma((2,)), dma((WO_SLOTS,)), dma((GU_SLOTS,)), dma((GU_SLOTS,)), dma((WD_SLOTS,)),
             dma((2, 10)), dma((2, 10, Q)),
         ],
-        compiler_params=pltpu.CompilerParams(collective_id=cid, has_side_effects=True, vmem_limit_bytes=59 * 1024 * 1024),
+        compiler_params=pltpu.CompilerParams(collective_id=cid, has_side_effects=True, vmem_limit_bytes=55 * 1024 * 1024),
         name="tail",
     )(attn, tok_blocks, ln, w_out, w_gate, w_up, w_down)
 
@@ -594,34 +601,24 @@
         half_dim = head_dim // 2
         q_group = heads_local // kv_local
         cache_len = k_cache.shape[1]
-        up_blocks = (cache_len - LOW) // BLK
         dim_index = lax.axis_index('dim')
 
         inv_freq = np.tile(ROPE_BASE ** (-np.arange(half_dim) * 2.0 / head_dim), 2).astype(np.float32)
-        angle = positions.astype(jnp.float32)[:, None] * inv_freq
 
         def by_column(w):
             return w.transpose(1, 2, 0).reshape(-1, w.shape[0])
 
-        qd, sn, vn, kn = qkv(len(UP_SIZES) + 1, q_group, tokens, ln_attn[None], angle, q_gain[None], k_gain[None],
+        qd, sn, vn, kt, vt = qkv(len(UP_SIZES) + 1, q_group, tokens, ln_attn[None], positions.astype(jnp.float32)[None], inv_freq[None], q_gain[None], k_gain[None],
                              by_column(w_query), by_column(w_key), by_column(w_value))
-        k_new = kn.reshape(rows, kv_local, slice_len)
-        v_new = vn.astype(jnp.bfloat16).reshape(rows, kv_local, slice_len)
-
-        row_units = up_blocks * BLK // UNIT
-        n_units = (positions - LOW + UNIT - 1) // UNIT
-        seq = jnp.arange(rows)
-        cum = jnp.sum(jnp.where(seq[:, None] >= seq[None, :], n_units[None, :], 0), axis=1)
-        off = cum - n_units
-        unit = jnp.arange(rows * row_units)
-        row_of = jnp.sum((cum[None, :] <= unit[:, None]).astype(jnp.int32), axis=1)
-        row_of = jnp.minimum(row_of, rows - 1)
-
+        k_new = kt.reshape(kv_local, slice_len, rows).transpose(2, 0, 1)
+        v_new = vt.reshape(kv_local, slice_len, rows).transpose(2, 0, 1)
+
+        n_units = jnp.maximum((positions - LOW + UNIT - 1) // UNIT, 1)
         k_t = k_cache.transpose(0, 2, 3, 1).reshape(rows, kv_local * slice_len, cache_len)
         v_t = v_cache.transpose(0, 2, 3, 1).reshape(rows, kv_local * slice_len, cache_len)
         which = jnp.sum((jnp.sum(n_units) > np.array(UP_SIZES[:-1]) * (BLK // UNIT)).astype(jnp.int32))
         branches = [functools.partial(attend, n, i, head_dim ** -0.5) for i, n in enumerate(UP_SIZES)]
-        attn = lax.switch(which, branches, positions, off, row_of, qd, sn, vn, k_t, v_t)
+        attn = lax.switch(which, branches, positions, qd, sn, vn, k_t, v_t)
         out = tail(len(UP_SIZES), attn, tokens.reshape(16, 8, -1), ln_mlp.reshape(Q, 1, -1), w_out.reshape(heads_local * slice_len, -1), w_gate, w_up, w_down)
         return out, k_new, v_new
 

time: 255 us -> 253 us (level)
  Pallas kernels: 245 us -> 242 us
where the time goes in v6:
time: 253 us; the launch traced here: 252 us
  Pallas kernels  242 us (96%)
  other arithmetic  3.83 us (2%)
  local copies, waits for them, and re-layouts  3.7 us (1%)
    pallas_call x1, Pallas kernels, attend(): pl.pallas_call(functools.partial(attn_kernel, n_up, scale), out_shape=jax...  142 us
    pallas_call x1, Pallas kernels, tail(): pl.pallas_call(tail_kernel, out_shape=jax.ShapeDtypeStruct((rows, d_model...  78.3 us
    pallas_call x1, Pallas kernels, qkv(): pl.pallas_call(functools.partial(qkv_kernel, group), out_shape=(jax.Shape...  21.8 us

profile of v6, /device:TPU:0, one launch (start us, length us, event | category | flops | bytes accessed | tf_op | source)
XLA Modules:
  0.0 251.6 jit_solution(16221392905649466038)
XLA Ops:
  0.6 0.0 copy-start.2
  0.6 1.9 convert_bitcast_fusion
  2.5 1.9 fusion
  5.1 21.8 %qkv.1 = (f32[128,16,128]{2,1,0:T(8,128)S(1)}, f32[128,16,128]{2,1,0:T(8,128)}, f32[128,128]{1,0:T(8,128)S(1)}, bf16[128,128]{1,0:T(8,128)(2,1)}, bf16[128,128]{1,0:T(8,128)(2,1)}) custom-call(bf16[128,5120]{1,0:T(8,128)(2,1)} %tok_ref.1, f32[1,5120]{1,0:T(1,128)} %bitcast.52, f32[1,128]{1,0:T(1,128)} %get-tuple-element.166.pos_ref, ...), custom_call_target="tpu_custom_call" | custom-call | tf_op jit(solution)/shard_map/qkv/pallas_call | solution.py:143
  26.9 0.0 copy-done.2
  26.9 142.7 %conditional.1 = (f32[128,8,128]{2,1,0:T(8,128)S(1)}) conditional(s32[]{:T(128)} %clamp.3, (s32[128]{0:T(128)S(1)}, f32[128,16,128]{2,1,0:T(8,128)S(1)}, f32[128,16,128]{2,1,0:T(8,128)}, f32[128,128]{1,0:T(8,128)S(1)}, bf16[128,128,1024]{2,1,0:T(8,128)(2,1)}, /*index=5*/bf16[128,128,1024]{2,1,0:T(8,128)(2,1)}) %tuple.61, ...), branch_computations={%region_2.3_spmd, %region_3.4_spmd, %region_4.5_spmd, %region_5.6_... | conditional | bytes 8 | solution.py:621
  27.0 142.4 %attend_264.1 = f32[128,8,128]{2,1,0:T(8,128)S(1)} custom-call(s32[128]{0:T(128)S(1)} %get-tuple-element.123.pos_ref, f32[128,16,128]{2,1,0:T(8,128)S(1)} %get-tuple-element.124.qd_ref, f32[128,16,128]{2,1,0:T(8,128)} %get-tuple-element.125.sn_ref, f32[128,128]{1,0:T(8,128)S(1)} %get-tuple-element.126.vn_ref, ...), custom_call_target="tpu_custom_call" | custom-call | tf_op jit(solution)/shard_map/cond/branch_3_fun/attend_264/pallas_call | solution.py:308
  169.6 0.0 copy-start.1
  169.6 0.0 copy-start
  169.7 78.3 %tail.1 = bf16[128,5120]{1,0:T(8,128)(2,1)} custom-call(f32[128,8,128]{2,1,0:T(8,128)S(1)} %get-tuple-element.174.attn_ref, bf16[16,8,5120]{2,1,0:T(8,128)(2,1)} %bitcast.47, f32[10,1,512]{2,1,0:T(1,128)} %bitcast.53, bf16[1024,5120]{1,0:T(8,128)(2,1)} %bitcast.45, bf16[5120,3200]{1,0:T(8,128)(2,1)} %wg_hbm.1, bf16[5120,3200]{1,0:T(8,128)(2,1)} %wu_hbm.1, ...), custom_call_target="tpu_custom_call" | custom-call | tf_op jit(solution)/shard_map/tail/pallas_call | solution.py:562
  247.9 2.5 copy.31
  250.4 0.0 copy-done.1
  250.4 0.6 copy.32
  251.0 0.0 copy-done
  251.0 0.6 copy.33
Async XLA Ops:
  0.6 26.3 %copy-start.2 = (s32[128]{0:T(128)S(1)}, s32[128]{0:T(128)}, u32[]{:S(2)}) copy-start(s32[128]{0:T(128)} %param.39) | copy-start | bytes 1540
  169.6 80.7 %copy-start.1 = (bf16[128,128]{1,0:T(8,128)(2,1)S(1)}, bf16[128,128]{1,0:T(8,128)(2,1)}, u32[]{:S(2)}) copy-start(bf16[128,128]{1,0:T(8,128)(2,1)} %get-tuple-element.164) | copy-start | bytes 98308
  169.6 81.4 %copy-start = (bf16[128,128]{1,0:T(8,128)(2,1)S(1)}, bf16[128,128]{1,0:T(8,128)(2,1)}, u32[]{:S(2)}) copy-start(bf16[128,128]{1,0:T(8,128)(2,1)} %get-tuple-element.165) | copy-start | bytes 98308

commit v7 on v6

--- a/solution.py
+++ b/solution.py
@@ -14,12 +14,12 @@
 
 BLK = 128
 LOW = 512
-CH = 2
+CH = 4
 UCH = 8
 UNIT = 16
-SLOTS = 6
-FIRST = 16
-LEAD = 8
+SLOTS = 4
+FIRST = 8
+LEAD = 4
 UP_SIZES = (232, 248, 256, 264, 272, 280, 296, 512)
 
 
@@ -92,7 +92,7 @@
     vn_ref[...] = v_row
     vt_ref[...] = v_row.T.astype(bf16)
     low = lax.broadcasted_iota(jnp.int32, (rows, BLK), 1) < half
-    angle = jnp.broadcast_to(pos_ref[...], (rows, rows)).T * freq_ref[...]
+    angle = jnp.broadcast_to(pos_ref[...].astype(f32), (rows, rows)).T * freq_ref[...]
     cos_t = jnp.cos(angle)
     sin_t = jnp.sin(angle) * jnp.where(lax.axis_index("dim") == 0, -1.0, 1.0)
 
@@ -331,6 +331,7 @@
 
 
 Q = 10
+HOP = 3
 WO_SLOTS = 4
 GU_SLOTS = 4
 WD_SLOTS = 3
@@ -411,10 +412,6 @@
         return pl.when((t >= lo) & (t < lo + Q))
 
     def reduce_steps(ph, t, finish):
-        @when(t, 1)
-        def _():
-            start(one(ph, 0, t - 1))
-
         @when(t, 2)
         def _():
             u = t - 2
@@ -422,39 +419,44 @@
             r1[u] = r1[u] + part[u, pl.ds(8 * core, 8)]
             start(one(ph, 1, u))
 
-        @when(t, 4)
-        def _():
-            u = t - 4
+        @when(t, 0)
+        def _():
+            start(one(ph, 0, t))
+
+        @when(t, 2 + HOP)
+        def _():
+            u = t - 2 - HOP
             arrived(ph, 1, u)
             r2[u, pl.ds(0, 2)] = r2[u, pl.ds(0, 2)] + r1[u, pl.ds(2 * cx, 2)]
             r2[u, pl.ds(2, 2)] = r2[u, pl.ds(2, 2)] + r1[u, pl.ds(4 + 2 * cy, 2)]
             start(one(ph, 2, u))
 
-        @when(t, 6)
-        def _():
-            u = t - 6
+        @when(t, 2 + 2 * HOP)
+        def _():
+            u = t - 2 - 2 * HOP
             arrived(ph, 2, u)
             finish(u, r3[u, 0] + r2[u, cy], r3[u, 1] + r2[u, 2 + cx])
 
+    def gather_start(ph, t):
+        @when(t, 0)
+        def _():
+            start(one(ph, 3, t))
+
     def gather_steps(ph, t, finish):
-        @when(t, 0)
-        def _():
-            start(one(ph, 3, t))
-
-        @when(t, 2)
-        def _():
-            arrived(ph, 3, t - 2)
-            start(one(ph, 4, t - 2))
-
-        @when(t, 4)
-        def _():
-            arrived(ph, 4, t - 4)
-            start(one(ph, 5, t - 4))
-
-        @when(t, 5)
-        def _():
-            arrived(ph, 5, t - 5)
-            finish(t - 5)
+        @when(t, HOP)
+        def _():
+            arrived(ph, 3, t - HOP)
+            start(one(ph, 4, t - HOP))
+
+        @when(t, 2 * HOP)
+        def _():
+            arrived(ph, 4, t - 2 * HOP)
+            start(one(ph, 5, t - 2 * HOP))
+
+        @when(t, 2 * HOP + 2)
+        def _():
+            arrived(ph, 5, t - 2 * HOP - 2)
+            finish(t - 2 * HOP - 2)
 
     blk_a, blk_b = core * 8 + 2 * cx + cy, core * 8 + 4 + 2 * cy + cx
     tok_loads = [pltpu.make_async_copy(tok_hbm.at[blk], tok_ref.at[i], tok_s.at[i]) for i, blk in enumerate((blk_a, blk_b))]
@@ -475,7 +477,7 @@
         xres[u, 0] = (tok_ref[0, :, cols(u)].astype(f32) + a).astype(jnp.bfloat16).astype(f32)
         xres[u, 1] = (tok_ref[1, :, cols(u)].astype(f32) + b).astype(jnp.bfloat16).astype(f32)
 
-    @pl.loop(0, Q + 6)
+    @pl.loop(0, Q + 2 + 2 * HOP)
     def _(t):
         @when(t, 0)
         def _():
@@ -516,8 +518,9 @@
         def _():
             start(gu_copy(u + GU_SLOTS))
 
-    @pl.loop(0, Q + 5)
+    @pl.loop(0, Q + 2 + 2 * HOP)
     def _(t):
+        gather_start(0, t)
         gather_steps(0, t, finish_gather)
 
     drain(0, (3, 4, 5))
@@ -534,8 +537,12 @@
     def finish_out(u):
         out_ref[:, cols(u)] = full[u].reshape(rows, width).astype(jnp.bfloat16)
 
-    @pl.loop(0, Q + 12)
+    lag = 3 + 2 * HOP
+
+    @pl.loop(0, Q + lag + 2 + 2 * HOP)
     def _(t):
+        gather_start(1, t - lag)
+
         @when(t, 0)
         def _():
             wait(wd_copy(t))
@@ -545,7 +552,7 @@
             def _():
                 start(wd_copy(t + WD_SLOTS))
         reduce_steps(1, t, finish_mlp)
-        gather_steps(1, t - 7, finish_out)
+        gather_steps(1, t - lag, finish_out)
 
     drain(1, (0, 1, 2, 3, 4, 5))
 
@@ -608,7 +615,7 @@
         def by_column(w):
             return w.transpose(1, 2, 0).reshape(-1, w.shape[0])
 
-        qd, sn, vn, kt, vt = qkv(len(UP_SIZES) + 1, q_group, tokens, ln_attn[None], positions.astype(jnp.float32)[None], inv_freq[None], q_gain[None], k_gain[None],
+        qd, sn, vn, kt, vt = qkv(len(UP_SIZES) + 1, q_group, tokens, ln_attn[None], positions[None], inv_freq[None], q_gain[None], k_gain[None],
                              by_column(w_query), by_column(w_key), by_column(w_value))
         k_new = kt.reshape(kv_local, slice_len, rows).transpose(2, 0, 1)
         v_new = vt.reshape(kv_local, slice_len, rows).transpose(2, 0, 1)
@@ -616,7 +623,8 @@
         n_units = jnp.maximum((positions - LOW + UNIT - 1) // UNIT, 1)
         k_t = k_cache.transpose(0, 2, 3, 1).reshape(rows, kv_local * slice_len, cache_len)
         v_t = v_cache.transpose(0, 2, 3, 1).reshape(rows, kv_local * slice_len, cache_len)
-        which = jnp.sum((jnp.sum(n_units) > np.array(UP_SIZES[:-1]) * (BLK // UNIT)).astype(jnp.int32))
+        total = jnp.sum(n_units)
+        which = sum((total > n * (BLK // UNIT)).astype(jnp.int32) for n in UP_SIZES[:-1])
         branches = [functools.partial(attend, n, i, head_dim ** -0.5) for i, n in enumerate(UP_SIZES)]
         attn = lax.switch(which, branches, positions, qd, sn, vn, k_t, v_t)
         out = tail(len(UP_SIZES), attn, tokens.reshape(16, 8, -1), ln_mlp.reshape(Q, 1, -1), w_out.reshape(heads_local * slice_len, -1), w_gate, w_up, w_down)

time: 253 us -> 251 us (level)
  between operations: 1.34 us -> 5.23 us
where the time goes in v7:
time: 251 us
  Pallas kernels  240 us (96%)
  between operations  5.23 us (2%)
  local copies, waits for them, and re-layouts  3.7 us (1%)
    pallas_call x1, Pallas kernels, attend(): pl.pallas_call(functools.partial(attn_kernel, n_up, scale), out_shape=jax...  142 us
    pallas_call x1, Pallas kernels, tail(): pl.pallas_call(tail_kernel, out_shape=jax.ShapeDtypeStruct((rows, d_model...  75.9 us
    pallas_call x1, Pallas kernels, qkv(): pl.pallas_call(functools.partial(qkv_kernel, group), out_shape=(jax.Shape...  21.8 us

profile of v7, /device:TPU:0, one launch (start us, length us, event | category | flops | bytes accessed | tf_op | source)
XLA Modules:
  0.0 250.8 jit_solution(4789021761905510167)
XLA Ops:
  0.6 0.0 copy-start
  0.6 1.4 maximum_reduce_fusion
  6.5 21.8 %qkv.1 = (f32[128,16,128]{2,1,0:T(8,128)S(1)}, f32[128,16,128]{2,1,0:T(8,128)}, f32[128,128]{1,0:T(8,128)S(1)}, bf16[128,128]{1,0:T(8,128)(2,1)}, bf16[128,128]{1,0:T(8,128)(2,1)}) custom-call(bf16[128,5120]{1,0:T(8,128)(2,1)} %tok_ref.1, f32[1,5120]{1,0:T(1,128)} %bitcast.52, s32[1,128]{1,0:T(1,128)} %bitcast.49, f32[1,128]{1,0:T(1,128)} %constant.43.clone.freq_ref, ...), custom_call_target="tpu_custom_call" | custom-call | tf_op jit(solution)/shard_map/qkv/pallas_call | solution.py:143
  28.3 0.0 copy-done
  28.3 142.7 %conditional.1 = (f32[128,8,128]{2,1,0:T(8,128)S(1)}) conditional(s32[]{:T(128)} %clamp.3, (s32[128]{0:T(128)S(1)}, f32[128,16,128]{2,1,0:T(8,128)S(1)}, f32[128,16,128]{2,1,0:T(8,128)}, f32[128,128]{1,0:T(8,128)S(1)}, bf16[128,128,1024]{2,1,0:T(8,128)(2,1)}, /*index=5*/bf16[128,128,1024]{2,1,0:T(8,128)(2,1)}) %tuple.60, ...), branch_computations={%region_1.2_spmd, %region_2.3_spmd, %region_3.4_spmd, %region_4.5_... | conditional | bytes 8 | solution.py:629
  28.4 142.5 %attend_264.1 = f32[128,8,128]{2,1,0:T(8,128)S(1)} custom-call(s32[128]{0:T(128)S(1)} %get-tuple-element.123.pos_ref, f32[128,16,128]{2,1,0:T(8,128)S(1)} %get-tuple-element.124.qd_ref, f32[128,16,128]{2,1,0:T(8,128)} %get-tuple-element.125.sn_ref, f32[128,128]{1,0:T(8,128)S(1)} %get-tuple-element.126.vn_ref, ...), custom_call_target="tpu_custom_call" | custom-call | tf_op jit(solution)/shard_map/cond/branch_3_fun/attend_264/pallas_call | solution.py:308
  171.1 0.0 copy-start.2
  171.1 0.0 copy-start.1
  171.1 75.9 %tail.1 = bf16[128,5120]{1,0:T(8,128)(2,1)} custom-call(f32[128,8,128]{2,1,0:T(8,128)S(1)} %get-tuple-element.172.attn_ref, bf16[16,8,5120]{2,1,0:T(8,128)(2,1)} %bitcast.46, f32[10,1,512]{2,1,0:T(1,128)} %bitcast.53, bf16[1024,5120]{1,0:T(8,128)(2,1)} %bitcast.44, bf16[5120,3200]{1,0:T(8,128)(2,1)} %wg_hbm.1, bf16[5120,3200]{1,0:T(8,128)(2,1)} %wu_hbm.1, ...), custom_call_target="tpu_custom_call" | custom-call | tf_op jit(solution)/shard_map/tail/pallas_call | solution.py:569
  247.1 2.5 copy.30
  249.5 0.0 copy-done.2
  249.5 0.6 copy.31
  250.1 0.0 copy-done.1
  250.1 0.6 copy.32
Async XLA Ops:
  0.6 27.7 %copy-start = (s32[128]{0:T(128)S(1)}, s32[128]{0:T(128)}, u32[]{:S(2)}) copy-start(s32[128]{0:T(128)} %param.38) | copy-start | bytes 1540
  171.1 78.4 %copy-start.2 = (bf16[128,128]{1,0:T(8,128)(2,1)S(1)}, bf16[128,128]{1,0:T(8,128)(2,1)}, u32[]{:S(2)}) copy-start(bf16[128,128]{1,0:T(8,128)(2,1)} %get-tuple-element.164) | copy-start | bytes 98308
  171.1 79.0 %copy-start.1 = (bf16[128,128]{1,0:T(8,128)(2,1)S(1)}, bf16[128,128]{1,0:T(8,128)(2,1)}, u32[]{:S(2)}) copy-start(bf16[128,128]{1,0:T(8,128)(2,1)} %get-tuple-element.165) | copy-start | bytes 98308

commit v8 on v7

--- a/solution.py
+++ b/solution.py
@@ -20,10 +20,11 @@
 SLOTS = 4
 FIRST = 8
 LEAD = 4
-UP_SIZES = (232, 248, 256, 264, 272, 280, 296, 512)
-
-
-def qkv_kernel(group, tok_ref, ln_ref, pos_ref, freq_ref, qg_ref, kg_ref, wq_hbm, wk_hbm, wv_hbm, qd_ref, sn_ref, vn_ref, kt_ref, vt_ref,
+UP_FIRST = 232
+UP_SIZES = tuple(UP_FIRST + UCH * i for i in range(9)) + (512,)
+
+
+def qkv_kernel(group, tok_ref, ln_ref, pos_ref, freq_ref, qg_ref, kg_ref, wq_hbm, wk_hbm, wv_hbm, qd_ref, vn_ref, kt_ref, vt_ref,
                hid, wq, wk, wv, own, other, gain_ref, gain_other, wsem, snd, rcv):
     partner = {"dim": 1 - lax.axis_index("dim")}
     rows, depth = tok_ref.shape
@@ -122,9 +123,8 @@
         turned = pltpu.roll(q_own, half, 1)
         for e in range(2):
             row = i + n_q * e
-            sn_ref[:, row, :] = jnp.broadcast_to(new[e], (rows, BLK))
             val = q_own if e == kv else turned
-            qd_ref[:, row, :] = jnp.where(low, val, 0.0) if kv == 0 else jnp.where(low, 0.0, val)
+            qd_ref[:, row, :] = jnp.where(low, val, new[e]) if kv == 0 else jnp.where(low, new[e], val)
     for c in range(steps):
         q_copy(c).wait_send()
     k_copy.wait_send()
@@ -142,10 +142,9 @@
     dma = pltpu.SemaphoreType.DMA
     return pl.pallas_call(
         functools.partial(qkv_kernel, group),
-        out_shape=(jax.ShapeDtypeStruct((rows, heads, BLK), f32), jax.ShapeDtypeStruct((rows, heads, BLK), f32),
-                   jax.ShapeDtypeStruct((rows, BLK), f32), jax.ShapeDtypeStruct((BLK, rows), bf16), jax.ShapeDtypeStruct((BLK, rows), bf16)),
+        out_shape=(jax.ShapeDtypeStruct((rows, heads, BLK), f32), jax.ShapeDtypeStruct((rows, BLK), f32), jax.ShapeDtypeStruct((BLK, rows), bf16), jax.ShapeDtypeStruct((BLK, rows), bf16)),
         in_specs=[vmem] * 6 + [hbm] * 3,
-        out_specs=(vmem,) * 5,
+        out_specs=(vmem,) * 4,
         scratch_shapes=[
             pltpu.VMEM((rows, depth), bf16),
             pltpu.VMEM(w_q.shape, bf16),
@@ -162,7 +161,7 @@
     )(tokens, ln, pos, freq, q_gain, k_gain, w_q, w_k, w_v)
 
 
-def attn_kernel(n_up, scale, pos_ref, qd_ref, sn_ref, vn_ref, k_hbm, v_hbm, o_ref,
+def attn_kernel(n_up, scale, pos_ref, qd_ref, vn_ref, k_hbm, v_hbm, o_ref,
                 off_ref, kbuf, vbuf, own_lo, own_up, pack, rlo, rup, ksem, vsem, send, slo_r, sup_r):
     partner = {"dim": 1 - lax.axis_index("dim")}
     rows = qd_ref.shape[0]
@@ -171,6 +170,8 @@
     up_blocks = own_up.shape[0] // rows
     per_blk = BLK // UNIT
     lane_up = lax.broadcasted_iota(jnp.int32, (16, BLK), 1)
+    kv_row = lax.broadcasted_iota(jnp.int32, (16, BLK), 0) // 4 % 2
+    q_lanes = kv_row == lane_up // 64
 
     def kcopy(c):
         return pltpu.make_async_copy(k_hbm.at[pl.ds(c * CH, CH)], kbuf.at[lax.rem(c, SLOTS)], ksem.at[lax.rem(c, SLOTS)])
@@ -197,18 +198,12 @@
         vcopy(c).start()
     row_units = up_blocks * per_blk
 
-    def place(b, total):
-        off_ref[b] = total
-        return total + jnp.maximum((pos_ref[b] - LOW + UNIT - 1) // UNIT, 1)
-
-    lax.fori_loop(0, rows, place, jnp.int32(0))
-
     @pl.loop(0, n_ch)
     def _(c):
         kcopy(c).wait()
         for r in range(CH):
             b = c * CH + r
-            s = jnp.dot(qd_ref[b].astype(jnp.bfloat16), kbuf[lax.rem(c, SLOTS), r], preferred_element_type=jnp.float32)
+            s = jnp.dot(jnp.where(q_lanes, qd_ref[b], 0.0).astype(jnp.bfloat16), kbuf[lax.rem(c, SLOTS), r], preferred_element_type=jnp.float32)
             own_lo[b] = s[:, :LOW]
             for j in range(up_blocks):
                 own_up[b * up_blocks + j] = s[:, LOW + j * BLK:LOW + (j + 1) * BLK]
@@ -220,6 +215,12 @@
         @pl.when((c >= 1) & (c <= FIRST))
         def _():
             lo_copy(c - 1).start()
+
+    def place(b, total):
+        off_ref[b] = total
+        return total + jnp.maximum((pos_ref[b] - LOW + UNIT - 1) // UNIT, 1)
+
+    lax.fori_loop(0, rows, place, jnp.int32(0))
 
     def fill(c, row):
         for r in range(UCH):
@@ -274,7 +275,8 @@
                 total = (own_up[b * up_blocks + j] + got) * scale
                 parts.append(jnp.where(t_up + j * BLK < pos, total, -jnp.inf))
             s = jnp.concatenate(parts, axis=1)
-            s_new = sn_ref[b][:, 0:1] * scale
+            q_row = qd_ref[b]
+            s_new = jnp.where(kv_row[:, 0:1] == 0, q_row[:, BLK - 1:], q_row[:, 0:1]) * scale
             m = jnp.maximum(jnp.max(s, axis=1, keepdims=True), s_new)
             e = jnp.exp(s - m)
             e_new = jnp.exp(s_new - m)
@@ -296,7 +298,7 @@
                                  device_id=partner, device_id_type=MESH).wait_send()
 
 
-def attend(n_up, cid, scale, pos, qd, sn, vn, k_t, v_t):
+def attend(n_up, cid, scale, pos, qd, vn, k_t, v_t):
     rows = qd.shape[0]
     n_ch = rows // CH
     n_uch = n_up // UCH
@@ -308,7 +310,7 @@
     return pl.pallas_call(
         functools.partial(attn_kernel, n_up, scale),
         out_shape=jax.ShapeDtypeStruct((rows, 8, 128), jnp.float32),
-        in_specs=[smem, vmem, vmem, vmem, hbm, hbm],
+        in_specs=[smem, vmem, vmem, hbm, hbm],
         out_specs=vmem,
         scratch_shapes=[
             pltpu.SMEM((rows,), jnp.int32),
@@ -327,7 +329,7 @@
         ],
         compiler_params=pltpu.CompilerParams(collective_id=cid, has_side_effects=True, vmem_limit_bytes=40 * 1024 * 1024),
         name=f"attend_{n_up}",
-    )(pos, qd, sn, vn, k_t, v_t)
+    )(pos, qd, vn, k_t, v_t)
 
 
 Q = 10
@@ -466,13 +468,12 @@
     barrier = pltpu.get_barrier_semaphore()
     for dev in (sib, xn, yn):
         pl.semaphore_signal(barrier, inc=1, device_id=dev, device_id_type=MESH)
-    pl.semaphore_wait(barrier, 3)
     acc_g[...] = jnp.zeros_like(acc_g)
     acc_u[...] = jnp.zeros_like(acc_u)
     for i in range(attn_ref.shape[1]):
         x_ref[:, i * BLK:(i + 1) * BLK] = attn_ref[:, i, :].astype(jnp.bfloat16)
     wait(tok_loads)
-
+    pl.semaphore_wait(barrier, 3)
     def finish_attn(u, a, b):
         xres[u, 0] = (tok_ref[0, :, cols(u)].astype(f32) + a).astype(jnp.bfloat16).astype(f32)
         xres[u, 1] = (tok_ref[1, :, cols(u)].astype(f32) + b).astype(jnp.bfloat16).astype(f32)
@@ -615,18 +616,20 @@
         def by_column(w):
             return w.transpose(1, 2, 0).reshape(-1, w.shape[0])
 
-        qd, sn, vn, kt, vt = qkv(len(UP_SIZES) + 1, q_group, tokens, ln_attn[None], positions[None], inv_freq[None], q_gain[None], k_gain[None],
+        qd, vn, kt, vt = qkv(len(UP_SIZES) + 1, q_group, tokens, ln_attn[None], positions[None], inv_freq[None], q_gain[None], k_gain[None],
                              by_column(w_query), by_column(w_key), by_column(w_value))
         k_new = kt.reshape(kv_local, slice_len, rows).transpose(2, 0, 1)
         v_new = vt.reshape(kv_local, slice_len, rows).transpose(2, 0, 1)
 
         n_units = jnp.maximum((positions - LOW + UNIT - 1) // UNIT, 1)
+        per_blk = BLK // UNIT
         k_t = k_cache.transpose(0, 2, 3, 1).reshape(rows, kv_local * slice_len, cache_len)
         v_t = v_cache.transpose(0, 2, 3, 1).reshape(rows, kv_local * slice_len, cache_len)
-        total = jnp.sum(n_units)
-        which = sum((total > n * (BLK // UNIT)).astype(jnp.int32) for n in UP_SIZES[:-1])
+        spare = (UP_FIRST - UCH) * per_blk // rows
+        assert spare * rows == (UP_FIRST - UCH) * per_blk
+        which = lax.shift_right_arithmetic(jnp.sum(n_units - spare), (UCH * per_blk).bit_length() - 1)
         branches = [functools.partial(attend, n, i, head_dim ** -0.5) for i, n in enumerate(UP_SIZES)]
-        attn = lax.switch(which, branches, positions, qd, sn, vn, k_t, v_t)
+        attn = lax.switch(which, branches, positions, qd, vn, k_t, v_t)
         out = tail(len(UP_SIZES), attn, tokens.reshape(16, 8, -1), ln_mlp.reshape(Q, 1, -1), w_out.reshape(heads_local * slice_len, -1), w_gate, w_up, w_down)
         return out, k_new, v_new
 

time: 251 us -> 246 us (0.980)
  between operations: 5.23 us -> 1.34 us
  Pallas kernels: 240 us -> 237 us
where the time goes in v8:
time: 246 us; the launch traced here: 244 us
  Pallas kernels  237 us (96%)
  local copies, waits for them, and re-layouts  3.7 us (2%)
    pallas_call x1, Pallas kernels, attend(): pl.pallas_call(functools.partial(attn_kernel, n_up, scale), out_shape=jax...  140 us
    pallas_call x1, Pallas kernels, tail(): pl.pallas_call(tail_kernel, out_shape=jax.ShapeDtypeStruct((rows, d_model...  75.9 us
    pallas_call x1, Pallas kernels, qkv(): pl.pallas_call(functools.partial(qkv_kernel, group), out_shape=(jax.Shape...  21.3 us

profile of v8, /device:TPU:0, one launch (start us, length us, event | category | flops | bytes accessed | tf_op | source)
XLA Modules:
  0.0 244.1 jit_solution(5939785935576994998)
XLA Ops:
  0.6 0.0 copy-start
  0.6 1.4 add_reduce_fusion
  2.7 21.3 %qkv.1 = (f32[128,16,128]{2,1,0:T(8,128)S(1)}, f32[128,128]{1,0:T(8,128)S(1)}, bf16[128,128]{1,0:T(8,128)(2,1)}, bf16[128,128]{1,0:T(8,128)(2,1)}) custom-call(bf16[128,5120]{1,0:T(8,128)(2,1)} %tok_ref.1, f32[1,5120]{1,0:T(1,128)} %bitcast.56, s32[1,128]{1,0:T(1,128)} %bitcast.53, f32[1,128]{1,0:T(1,128)} %constant.34.clone.freq_ref, f32[1,64]{1,0:T(1,128)} %bitcast.58, ...), custom_call_target="tpu_custom_call" | custom-call | tf_op jit(solution)/shard_map/qkv/pallas_call | solution.py:143
  24.0 0.0 copy-done
  24.0 140.4 %conditional.1 = (f32[128,8,128]{2,1,0:T(8,128)S(1)}) conditional(s32[]{:T(128)} %clamp.3, (s32[128]{0:T(128)S(1)}, f32[128,16,128]{2,1,0:T(8,128)S(1)}, f32[128,128]{1,0:T(8,128)S(1)}, bf16[128,128,1024]{2,1,0:T(8,128)(2,1)}, bf16[128,128,1024]{2,1,0:T(8,128)(2,1)}) %tuple.72, (s32[128]{0:T(128)S(1)}, ...), branch_computations={%region_1.2_spmd, %region_2.3_spmd, %region_3.4_spmd, %region_4.5_... | conditional | bytes 8 | solution.py:632
  24.0 140.1 %attend_256.1 = f32[128,8,128]{2,1,0:T(8,128)S(1)} custom-call(s32[128]{0:T(128)S(1)} %get-tuple-element.126.pos_ref, f32[128,16,128]{2,1,0:T(8,128)S(1)} %get-tuple-element.127.qd_ref, f32[128,128]{1,0:T(8,128)S(1)} %get-tuple-element.128.vn_ref, bf16[128,128,1024]{2,1,0:T(8,128)(2,1)} %get-tuple-element.129.k_hbm, ...), custom_call_target="tpu_custom_call" | custom-call | tf_op jit(solution)/shard_map/cond/branch_3_fun/attend_256/pallas_call | solution.py:310
  164.4 0.0 copy-start.2
  164.4 0.0 copy-start.1
  164.4 75.9 %tail.1 = bf16[128,5120]{1,0:T(8,128)(2,1)} custom-call(f32[128,8,128]{2,1,0:T(8,128)S(1)} %get-tuple-element.178.attn_ref, bf16[16,8,5120]{2,1,0:T(8,128)(2,1)} %bitcast.50, f32[10,1,512]{2,1,0:T(1,128)} %bitcast.57, bf16[1024,5120]{1,0:T(8,128)(2,1)} %bitcast.48, bf16[5120,3200]{1,0:T(8,128)(2,1)} %wg_hbm.1, bf16[5120,3200]{1,0:T(8,128)(2,1)} %wu_hbm.1, ...), custom_call_target="tpu_custom_call" | custom-call | tf_op jit(solution)/shard_map/tail/pallas_call | solution.py:570
  240.4 2.5 %copy.32 = bf16[128,5120]{1,0:T(8,128)(2,1)} copy(bf16[128,5120]{1,0:T(8,128)(2,1)} %tail.1) | data formatting | bytes 2621440
  242.8 0.0 copy-done.2
  242.9 0.6 copy.33
  243.5 0.0 copy-done.1
  243.5 0.6 copy.34
Async XLA Ops:
  0.6 23.4 %copy-start = (s32[128]{0:T(128)S(1)}, s32[128]{0:T(128)}, u32[]{:S(2)}) copy-start(s32[128]{0:T(128)} %param.40) | copy-start | bytes 1540
  164.4 78.4 %copy-start.2 = (bf16[128,128]{1,0:T(8,128)(2,1)S(1)}, bf16[128,128]{1,0:T(8,128)(2,1)}, u32[]{:S(2)}) copy-start(bf16[128,128]{1,0:T(8,128)(2,1)} %get-tuple-element.170) | copy-start | bytes 98308
  164.4 79.0 %copy-start.1 = (bf16[128,128]{1,0:T(8,128)(2,1)S(1)}, bf16[128,128]{1,0:T(8,128)(2,1)}, u32[]{:S(2)}) copy-start(bf16[128,128]{1,0:T(8,128)(2,1)} %get-tuple-element.171) | copy-start | bytes 98308

commit v9 on v8

--- a/solution.py
+++ b/solution.py
@@ -189,17 +189,20 @@
         return pltpu.make_async_remote_copy(src_ref=pack.at[part], dst_ref=rup.at[part], send_sem=send.at[1],
                                             recv_sem=sup_r.at[c], device_id=partner, device_id_type=MESH)
 
-    for c in range(SLOTS):
-        kcopy(c).start()
+    kcopy(0).start()
     barrier = pltpu.get_barrier_semaphore()
     pl.semaphore_signal(barrier, inc=1, device_id=partner, device_id_type=MESH)
     pl.semaphore_wait(barrier, 1)
-    for c in range(SLOTS):
-        vcopy(c).start()
+    for c in range(1, SLOTS):
+        kcopy(c).start()
     row_units = up_blocks * per_blk
 
     @pl.loop(0, n_ch)
     def _(c):
+        @pl.when((c >= 1) & (c <= FIRST))
+        def _():
+            lo_copy(c - 1).start()
+
         kcopy(c).wait()
         for r in range(CH):
             b = c * CH + r
@@ -212,9 +215,8 @@
         def _():
             kcopy(c + SLOTS).start()
 
-        @pl.when((c >= 1) & (c <= FIRST))
-        def _():
-            lo_copy(c - 1).start()
+    for c in range(SLOTS):
+        vcopy(c).start()
 
     def place(b, total):
         off_ref[b] = total
@@ -333,10 +335,11 @@
 
 
 Q = 10
-HOP = 3
-WO_SLOTS = 4
-GU_SLOTS = 4
-WD_SLOTS = 3
+REDUCE_LAGS = ((3, 6, 6), (2, 5, 6))
+GATHER_LAGS = ((4, 3, 2), (6, 4, 2))
+WO_SLOTS = 3
+GU_SLOTS = 5
+WD_SLOTS = 4
 
 
 def tail_kernel(attn_ref, tok_hbm, ln_ref, wo_hbm, wg_hbm, wu_hbm, wd_hbm, out_ref,
@@ -414,9 +417,11 @@
         return pl.when((t >= lo) & (t < lo + Q))
 
     def reduce_steps(ph, t, finish):
-        @when(t, 2)
-        def _():
-            u = t - 2
+        first, second, third = np.cumsum(REDUCE_LAGS[ph]).tolist()
+
+        @when(t, first)
+        def _():
+            u = t - first
             arrived(ph, 0, u)
             r1[u] = r1[u] + part[u, pl.ds(8 * core, 8)]
             start(one(ph, 1, u))
@@ -425,17 +430,17 @@
         def _():
             start(one(ph, 0, t))
 
-        @when(t, 2 + HOP)
-        def _():
-            u = t - 2 - HOP
+        @when(t, second)
+        def _():
+            u = t - second
             arrived(ph, 1, u)
             r2[u, pl.ds(0, 2)] = r2[u, pl.ds(0, 2)] + r1[u, pl.ds(2 * cx, 2)]
             r2[u, pl.ds(2, 2)] = r2[u, pl.ds(2, 2)] + r1[u, pl.ds(4 + 2 * cy, 2)]
             start(one(ph, 2, u))
 
-        @when(t, 2 + 2 * HOP)
-        def _():
-            u = t - 2 - 2 * HOP
+        @when(t, third)
+        def _():
+            u = t - third
             arrived(ph, 2, u)
             finish(u, r3[u, 0] + r2[u, cy], r3[u, 1] + r2[u, 2 + cx])
 
@@ -445,20 +450,22 @@
             start(one(ph, 3, t))
 
     def gather_steps(ph, t, finish):
-        @when(t, HOP)
-        def _():
-            arrived(ph, 3, t - HOP)
-            start(one(ph, 4, t - HOP))
-
-        @when(t, 2 * HOP)
-        def _():
-            arrived(ph, 4, t - 2 * HOP)
-            start(one(ph, 5, t - 2 * HOP))
-
-        @when(t, 2 * HOP + 2)
-        def _():
-            arrived(ph, 5, t - 2 * HOP - 2)
-            finish(t - 2 * HOP - 2)
+        first, second, third = np.cumsum(GATHER_LAGS[ph]).tolist()
+
+        @when(t, first)
+        def _():
+            arrived(ph, 3, t - first)
+            start(one(ph, 4, t - first))
+
+        @when(t, second)
+        def _():
+            arrived(ph, 4, t - second)
+            start(one(ph, 5, t - second))
+
+        @when(t, third)
+        def _():
+            arrived(ph, 5, t - third)
+            finish(t - third)
 
     blk_a, blk_b = core * 8 + 2 * cx + cy, core * 8 + 4 + 2 * cy + cx
     tok_loads = [pltpu.make_async_copy(tok_hbm.at[blk], tok_ref.at[i], tok_s.at[i]) for i, blk in enumerate((blk_a, blk_b))]
@@ -478,7 +485,7 @@
         xres[u, 0] = (tok_ref[0, :, cols(u)].astype(f32) + a).astype(jnp.bfloat16).astype(f32)
         xres[u, 1] = (tok_ref[1, :, cols(u)].astype(f32) + b).astype(jnp.bfloat16).astype(f32)
 
-    @pl.loop(0, Q + 2 + 2 * HOP)
+    @pl.loop(0, Q + sum(REDUCE_LAGS[0]))
     def _(t):
         @when(t, 0)
         def _():
@@ -489,13 +496,14 @@
             def _():
                 start(wo_copy(t + WO_SLOTS))
 
-            @pl.when(t < GU_SLOTS)
-            def _():
-                start(gu_copy(t))
-
-            @pl.when((t >= GU_SLOTS) & (t < GU_SLOTS + WD_SLOTS))
-            def _():
-                start(wd_copy(t - GU_SLOTS))
+        @pl.when((t >= WO_SLOTS) & (t < WO_SLOTS + GU_SLOTS))
+        def _():
+            start(gu_copy(t - WO_SLOTS))
+
+        @pl.when((t >= WO_SLOTS + GU_SLOTS) & (t < WO_SLOTS + GU_SLOTS + WD_SLOTS))
+        def _():
+            start(wd_copy(t - WO_SLOTS - GU_SLOTS))
+
         reduce_steps(0, t, finish_attn)
 
     drain(0, (0, 1, 2))
@@ -519,7 +527,7 @@
         def _():
             start(gu_copy(u + GU_SLOTS))
 
-    @pl.loop(0, Q + 2 + 2 * HOP)
+    @pl.loop(0, Q + sum(GATHER_LAGS[0]))
     def _(t):
         gather_start(0, t)
         gather_steps(0, t, finish_gather)
@@ -538,9 +546,9 @@
     def finish_out(u):
         out_ref[:, cols(u)] = full[u].reshape(rows, width).astype(jnp.bfloat16)
 
-    lag = 3 + 2 * HOP
-
-    @pl.loop(0, Q + lag + 2 + 2 * HOP)
+    lag = 1 + sum(REDUCE_LAGS[1])
+
+    @pl.loop(0, Q + lag + sum(GATHER_LAGS[1]))
     def _(t):
         gather_start(1, t - lag)
 
@@ -591,7 +599,7 @@
             dma((2,)), dma((WO_SLOTS,)), dma((GU_SLOTS,)), dma((GU_SLOTS,)), dma((WD_SLOTS,)),
             dma((2, 10)), dma((2, 10, Q)),
         ],
-        compiler_params=pltpu.CompilerParams(collective_id=cid, has_side_effects=True, vmem_limit_bytes=55 * 1024 * 1024),
+        compiler_params=pltpu.CompilerParams(collective_id=cid, has_side_effects=True, vmem_limit_bytes=62 * 1024 * 1024),
         name="tail",
     )(attn, tok_blocks, ln, w_out, w_gate, w_up, w_down)
 

time: 246 us -> 243 us (0.988); the launches traced: 244 us -> 247 us
  Pallas kernels: 237 us -> 240 us
    pallas_call x1, Pallas kernels: 140 us -> 147 us  [attend(): pl.pallas_call(functools.partial(attn_kernel, n_up, scale), out_shape=jax...]
    pallas_call x1, Pallas kernels: 75.9 us -> 71.7 us  [tail(): pl.pallas_call(tail_kernel, out_shape=jax.ShapeDtypeStruct((rows, d_model...]
where the time goes in v9:
time: 243 us; the launch traced here: 247 us
  Pallas kernels  240 us (99%)
  local copies, waits for them, and re-layouts  3.7 us (2%)
    pallas_call x1, Pallas kernels, attend(): pl.pallas_call(functools.partial(attn_kernel, n_up, scale), out_shape=jax...  147 us
    pallas_call x1, Pallas kernels, tail(): pl.pallas_call(tail_kernel, out_shape=jax.ShapeDtypeStruct((rows, d_model...  71.7 us
    pallas_call x1, Pallas kernels, qkv(): pl.pallas_call(functools.partial(qkv_kernel, group), out_shape=(jax.Shape...  21.3 us

profile of v9, /device:TPU:0, one launch (start us, length us, event | category | flops | bytes accessed | tf_op | source)
XLA Modules:
  0.0 246.8 jit_solution(17104934809237498817)
XLA Ops:
  0.6 0.0 copy-start
  0.6 1.4 add_reduce_fusion
  2.7 21.3 %qkv.1 = (f32[128,16,128]{2,1,0:T(8,128)S(1)}, f32[128,128]{1,0:T(8,128)S(1)}, bf16[128,128]{1,0:T(8,128)(2,1)}, bf16[128,128]{1,0:T(8,128)(2,1)}) custom-call(bf16[128,5120]{1,0:T(8,128)(2,1)} %tok_ref.1, f32[1,5120]{1,0:T(1,128)} %bitcast.56, s32[1,128]{1,0:T(1,128)} %bitcast.53, f32[1,128]{1,0:T(1,128)} %constant.34.clone.freq_ref, f32[1,64]{1,0:T(1,128)} %bitcast.58, ...), custom_call_target="tpu_custom_call" | custom-call | tf_op jit(solution)/shard_map/qkv/pallas_call | solution.py:143
  24.0 0.0 copy-done
  24.0 147.4 %conditional.1 = (f32[128,8,128]{2,1,0:T(8,128)S(1)}) conditional(s32[]{:T(128)} %clamp.3, (s32[128]{0:T(128)S(1)}, f32[128,16,128]{2,1,0:T(8,128)S(1)}, f32[128,128]{1,0:T(8,128)S(1)}, bf16[128,128,1024]{2,1,0:T(8,128)(2,1)}, bf16[128,128,1024]{2,1,0:T(8,128)(2,1)}) %tuple.72, (s32[128]{0:T(128)S(1)}, ...), branch_computations={%region_1.2_spmd, %region_2.3_spmd, %region_3.4_spmd, %region_4.5_... | conditional | bytes 8 | solution.py:640
  24.3 146.9 %attend_296.1 = f32[128,8,128]{2,1,0:T(8,128)S(1)} custom-call(s32[128]{0:T(128)S(1)} %get-tuple-element.151.pos_ref, f32[128,16,128]{2,1,0:T(8,128)S(1)} %get-tuple-element.152.qd_ref, f32[128,128]{1,0:T(8,128)S(1)} %get-tuple-element.153.vn_ref, bf16[128,128,1024]{2,1,0:T(8,128)(2,1)} %get-tuple-element.154.k_hbm, ...), custom_call_target="tpu_custom_call" | custom-call | tf_op jit(solution)/shard_map/cond/branch_8_fun/attend_296/pallas_call | solution.py:312
  171.4 0.0 copy-start.2
  171.4 0.0 copy-start.1
  171.4 71.7 %tail.1 = bf16[128,5120]{1,0:T(8,128)(2,1)} custom-call(f32[128,8,128]{2,1,0:T(8,128)S(1)} %get-tuple-element.178.attn_ref, bf16[16,8,5120]{2,1,0:T(8,128)(2,1)} %bitcast.50, f32[10,1,512]{2,1,0:T(1,128)} %bitcast.57, bf16[1024,5120]{1,0:T(8,128)(2,1)} %bitcast.48, bf16[5120,3200]{1,0:T(8,128)(2,1)} %wg_hbm.1, bf16[5120,3200]{1,0:T(8,128)(2,1)} %wu_hbm.1, ...), custom_call_target="tpu_custom_call" | custom-call | tf_op jit(solution)/shard_map/tail/pallas_call | solution.py:578
  243.1 2.5 copy.32
  245.6 0.0 copy-done.2
  245.6 0.6 copy.33
  246.2 0.0 copy-done.1
  246.2 0.6 copy.34
Async XLA Ops:
  0.6 23.4 %copy-start = (s32[128]{0:T(128)S(1)}, s32[128]{0:T(128)}, u32[]{:S(2)}) copy-start(s32[128]{0:T(128)} %param.40) | copy-start | bytes 1540
  171.4 74.2 %copy-start.2 = (bf16[128,128]{1,0:T(8,128)(2,1)S(1)}, bf16[128,128]{1,0:T(8,128)(2,1)}, u32[]{:S(2)}) copy-start(bf16[128,128]{1,0:T(8,128)(2,1)} %get-tuple-element.170) | copy-start | bytes 98308
  171.4 74.8 %copy-start.1 = (bf16[128,128]{1,0:T(8,128)(2,1)S(1)}, bf16[128,128]{1,0:T(8,128)(2,1)}, u32[]{:S(2)}) copy-start(bf16[128,128]{1,0:T(8,128)(2,1)} %get-tuple-element.171) | copy-start | bytes 98308

commit v10 on v9

--- a/solution.py
+++ b/solution.py
@@ -337,6 +337,7 @@
 Q = 10
 REDUCE_LAGS = ((3, 6, 6), (2, 5, 6))
 GATHER_LAGS = ((4, 3, 2), (6, 4, 2))
+PARTS = 4
 WO_SLOTS = 3
 GU_SLOTS = 5
 WD_SLOTS = 4
@@ -604,6 +605,36 @@
     )(attn, tok_blocks, ln, w_out, w_gate, w_up, w_down)
 
 
+def place_kernel(out_hbm, k_hbm, v_hbm, out_dst, k_dst, v_dst, out_buf, k_buf, v_buf, sem_in, sem_out):
+    rows = out_hbm.shape[0] // PARTS
+    moves = [(k_hbm, k_buf, k_dst), (v_hbm, v_buf, v_dst)]
+    for i in range(PARTS):
+        part = pl.ds(i * rows, rows)
+        moves.append((out_hbm.at[part], out_buf.at[part], out_dst.at[part]))
+    loads = [pltpu.make_async_copy(src, buf, sem_in.at[i]) for i, (src, buf, dst) in enumerate(moves)]
+    stores = [pltpu.make_async_copy(buf, dst, sem_out.at[i]) for i, (src, buf, dst) in enumerate(moves)]
+    for load in loads:
+        load.start()
+    for load, store in zip(loads, stores):
+        load.wait()
+        store.start()
+    for store in stores:
+        store.wait()
+
+
+def place_results(out, k_t, v_t):
+    hbm = pl.BlockSpec(memory_space=pl.ANY)
+    arrays = (out, k_t, v_t)
+    return pl.pallas_call(
+        place_kernel,
+        out_shape=tuple(jax.ShapeDtypeStruct(x.shape, x.dtype) for x in arrays),
+        in_specs=[hbm] * 3,
+        out_specs=(hbm,) * 3,
+        scratch_shapes=[pltpu.VMEM(x.shape, x.dtype) for x in arrays] + [pltpu.SemaphoreType.DMA((PARTS + 2,))] * 2,
+        name="place",
+    )(*arrays)
+
+
 def solution(mesh):
     dim_count = mesh.shape['dim']
     mlp_axes = ('heads', 'dim')
@@ -626,9 +657,6 @@
 
         qd, vn, kt, vt = qkv(len(UP_SIZES) + 1, q_group, tokens, ln_attn[None], positions[None], inv_freq[None], q_gain[None], k_gain[None],
                              by_column(w_query), by_column(w_key), by_column(w_value))
-        k_new = kt.reshape(kv_local, slice_len, rows).transpose(2, 0, 1)
-        v_new = vt.reshape(kv_local, slice_len, rows).transpose(2, 0, 1)
-
         n_units = jnp.maximum((positions - LOW + UNIT - 1) // UNIT, 1)
         per_blk = BLK // UNIT
         k_t = k_cache.transpose(0, 2, 3, 1).reshape(rows, kv_local * slice_len, cache_len)
@@ -639,6 +667,9 @@
         branches = [functools.partial(attend, n, i, head_dim ** -0.5) for i, n in enumerate(UP_SIZES)]
         attn = lax.switch(which, branches, positions, qd, vn, k_t, v_t)
         out = tail(len(UP_SIZES), attn, tokens.reshape(16, 8, -1), ln_mlp.reshape(Q, 1, -1), w_out.reshape(heads_local * slice_len, -1), w_gate, w_up, w_down)
+        out, kt, vt = place_results(out, kt, vt)
+        k_new = kt.reshape(kv_local, slice_len, rows).transpose(2, 0, 1)
+        v_new = vt.reshape(kv_local, slice_len, rows).transpose(2, 0, 1)
         return out, k_new, v_new
 
     row_spec = P('dp', None)

time: 243 us -> 243 us (level); the launches traced: 247 us -> 241 us
  local copies, waits for them, and re-layouts: 3.7 us -> 0.01 us
    pallas_call x1, Pallas kernels: 147 us -> 143 us  [attend(): pl.pallas_call(functools.partial(attn_kernel, n_up, scale), out_shape=jax...]
    unnamed x9 -> x2, local copies, waits for them, and re-layouts: 3.7 us -> 0.01 us
where the time goes in v10:
time: 243 us; the launch traced here: 241 us
  Pallas kernels  238 us (98%)
    pallas_call x1, Pallas kernels, attend(): pl.pallas_call(functools.partial(attn_kernel, n_up, scale), out_shape=jax...  143 us
    pallas_call x1, Pallas kernels, tail(): pl.pallas_call(tail_kernel, out_shape=jax.ShapeDtypeStruct((rows, d_model...  71.7 us
    pallas_call x1, Pallas kernels, qkv(): pl.pallas_call(functools.partial(qkv_kernel, group), out_shape=(jax.Shape...  21.3 us

profile of v10, /device:TPU:0, one launch (start us, length us, event | category | flops | bytes accessed | tf_op | source)
XLA Modules:
  0.0 241.4 jit_solution(7289194334140337513)
XLA Ops:
  0.6 0.0 copy-start
  0.6 1.4 add_reduce_fusion
  2.7 21.3 %qkv.1 = (f32[128,16,128]{2,1,0:T(8,128)S(1)}, f32[128,128]{1,0:T(8,128)S(1)}, bf16[128,128]{1,0:T(8,128)(2,1)}, bf16[128,128]{1,0:T(8,128)(2,1)}) custom-call(bf16[128,5120]{1,0:T(8,128)(2,1)} %tok_ref.1, f32[1,5120]{1,0:T(1,128)} %bitcast.54, s32[1,128]{1,0:T(1,128)} %bitcast.53, f32[1,128]{1,0:T(1,128)} %constant.34.clone.freq_ref, f32[1,64]{1,0:T(1,128)} %bitcast.56, ...), custom_call_target="tpu_custom_call" | custom-call | tf_op jit(solution)/shard_map/qkv/pallas_call | solution.py:143
  24.0 0.0 copy-done
  24.0 143.4 %conditional.1 = (f32[128,8,128]{2,1,0:T(8,128)S(1)}) conditional(s32[]{:T(128)} %clamp.3, (s32[128]{0:T(128)S(1)}, f32[128,16,128]{2,1,0:T(8,128)S(1)}, f32[128,128]{1,0:T(8,128)S(1)}, bf16[128,128,1024]{2,1,0:T(8,128)(2,1)}, bf16[128,128,1024]{2,1,0:T(8,128)(2,1)}) %tuple.70, (s32[128]{0:T(128)S(1)}, ...), branch_computations={%region_1.2_spmd, %region_2.3_spmd, %region_3.4_spmd, %region_4.5_... | conditional | bytes 8 | solution.py:668
  24.2 142.6 %attend_272.1 = f32[128,8,128]{2,1,0:T(8,128)S(1)} custom-call(s32[128]{0:T(128)S(1)} %get-tuple-element.136.pos_ref, f32[128,16,128]{2,1,0:T(8,128)S(1)} %get-tuple-element.137.qd_ref, f32[128,128]{1,0:T(8,128)S(1)} %get-tuple-element.138.vn_ref, bf16[128,128,1024]{2,1,0:T(8,128)(2,1)} %get-tuple-element.139.k_hbm, ...), custom_call_target="tpu_custom_call" | custom-call | tf_op jit(solution)/shard_map/cond/branch_5_fun/attend_272/pallas_call | solution.py:312
  167.4 71.7 %tail.1.out_hbm = bf16[128,5120]{1,0:T(8,128)(2,1)} custom-call(f32[128,8,128]{2,1,0:T(8,128)S(1)} %get-tuple-element.178.attn_ref, bf16[16,8,5120]{2,1,0:T(8,128)(2,1)} %bitcast.50, f32[10,1,512]{2,1,0:T(1,128)} %bitcast.55, bf16[1024,5120]{1,0:T(8,128)(2,1)} %bitcast.48, bf16[5120,3200]{1,0:T(8,128)(2,1)} %wg_hbm.1, bf16[5120,3200]{1,0:T(8,128)(2,1)} %wu_hbm.1, ...), custom_call_target="tpu_custom_call" | custom-call | tf_op jit(solution)/shard_map/tail/pallas_call | solution.py:579
  239.1 2.2 place.1
Async XLA Ops:
  0.6 23.4 %copy-start = (s32[128]{0:T(128)S(1)}, s32[128]{0:T(128)}, u32[]{:S(2)}) copy-start(s32[128]{0:T(128)} %param.40) | copy-start | bytes 1540
